TPU v7x, 32 devices: a whole 2x2x4 slice. The times are simulated.
32 devices in a mesh: shard: 16 (over z, y, x), mp: 2 (over core).
Axes of the slice: x: 2, y: 2, z: 4, core: 2. Of those that a mesh axis runs over, the one named last changes fastest.
Arguments:
- item_rows: float32 [4096, 256], P('shard', 'mp'), may hold values from -6 to 6
- first_moment: float32 [4096, 256], P('shard', 'mp'), may hold values from -2 to 2
- second_moment: float32 [4096, 256], P('shard', 'mp'), may hold values from 0.01 to 4
- item_cot: bfloat16 [4096, 256], P('shard', 'mp'), may hold values from -6 to 6
- tile_bits: int32 [256, 8, 128], P('shard'), may hold values from 0 to 65535, as said below
- tile_item: int32 [256], P('shard'), may hold values from 0 to 1
- tile_dest: int32 [256], P('shard'), may hold values from 0 to 15
- basket_gain: float32 [256], replicated, may hold values from 0.1 to 1.9
- item_gain: float32 [256], replicated, may hold values from 0.1 to 1.9
- gate_basket: bfloat16 [256, 2048], P(None, 'mp'), may hold values from -0.375 to 0.375
- up_basket: bfloat16 [256, 2048], P(None, 'mp'), may hold values from -0.375 to 0.375
- down_basket: bfloat16 [2048, 256], P('mp'), may hold values from -0.125 to 0.125
- gate_item: bfloat16 [256, 2048], P(None, 'mp'), may hold values from -0.375 to 0.375
- up_item: bfloat16 [256, 2048], P(None, 'mp'), may hold values from -0.375 to 0.375
- down_item: bfloat16 [2048, 256], P('mp'), may hold values from -0.125 to 0.125
Outputs:
- new_rows: float32 [4096, 256], P('shard', 'mp')
- new_first: float32 [4096, 256], P('shard', 'mp')
- new_second: float32 [4096, 256], P('shard', 'mp')
Inputs may be any that keep to these rules, and one draw needn't show every extreme that they name: `tile_bits`: each word holds 16 independent incidence bits in its low bits.
All inputs are finite; a program needn't handle non-finite values.
Results may differ from a plain program's by a relative error of at most 0.007.
Values may be sent and summed in bfloat16 or wider, within the bound.
No kernel may reach another device: no remote copies, remote signals or barrier semaphores. Data moves between devices by JAX's collectives and lax.ppermute only.
A program may use at most 128 MiB of HBM per device.

v0:
```python
import functools

import jax
import jax.numpy as jnp
import numpy as np
from jax import lax
from jax.experimental import pallas as pl
from jax.experimental.pallas import tpu as pltpu
from jax.sharding import PartitionSpec as P

BLOCK = 128
GATHER = 4
CHUNK = 256

NORM_EPSILON = 1e-05
LEARNING_RATE = 0.01
BETA_FIRST = 0.9
BETA_SECOND = 0.99
ADAM_EPSILON = 1e-08


F32 = jnp.float32
BF16 = jnp.bfloat16


def sds(shape, dtype):
    return jax.ShapeDtypeStruct(shape, dtype)


def nbytes(x):
    return int(np.prod(x.shape)) * jnp.dtype(x.dtype).itemsize


def run(body, outs, smem, args, scratch=(), flops=1 << 20, name=None):
    limit = sum(nbytes(x) for x in (*args, *jax.tree.leaves(outs), *scratch)) + (4 << 20)
    specs = [pl.BlockSpec(memory_space=pltpu.SMEM)] * len(smem)
    specs += [pl.BlockSpec(memory_space=pltpu.VMEM)] * len(args)
    return pl.pallas_call(
        body,
        out_shape=outs,
        in_specs=specs,
        out_specs=jax.tree.map(lambda _: pl.BlockSpec(memory_space=pltpu.VMEM), outs),
        scratch_shapes=list(scratch),
        cost_estimate=pl.CostEstimate(flops=flops, bytes_accessed=1 << 20, transcendentals=0),
        compiler_params=pltpu.CompilerParams(vmem_limit_bytes=min(limit, 60 * 1024 * 1024)),
        name=name,
    )(*smem, *args)


def dot(a, b):
    return jnp.dot(a, b, preferred_element_type=F32)


def dot_nt(a, b):
    return lax.dot_general(a, b, (((1,), (1,)), ((), ())), preferred_element_type=F32)


def sigmoid(v):
    return 0.5 * jnp.tanh(0.5 * v) + 0.5


def pack_body(core_ref, rows_ref, words_ref, meta_ref, pack_ref, lo_ref, hi_ref, *, half):
    items = rows_ref.shape[0]
    start = pl.multiple_of(core_ref[0] * half, half)
    pack_ref[0:items, :] = rows_ref[...].astype(BF16)
    words = words_ref[...]
    lo_ref[...] = (words & 255).astype(F32).T
    hi_ref[...] = (words >> 8).astype(F32).T
    pack_ref[items : items + half, :] = lo_ref[pl.ds(start, half), :].astype(BF16)
    pack_ref[items + half : items + 2 * half, :] = hi_ref[pl.ds(start, half), :].astype(BF16)
    pack_ref[items + 2 * half :, :] = meta_ref[...]


def join_halves(core, whole_ref, own_ref_list, other_ref, rows):
    width = other_ref.shape[1]
    mine = pl.multiple_of(core * width, width)
    theirs = pl.multiple_of((1 - core) * width, width)
    for l, own in enumerate(own_ref_list):
        whole_ref[l * rows : (l + 1) * rows, pl.ds(mine, width)] = own[0:rows, :]
        whole_ref[l * rows : (l + 1) * rows, pl.ds(theirs, width)] = other_ref[
            l * rows : (l + 1) * rows, :
        ]


def sums_body(idx_ref, *refs, members, groups, half, items, tiles):
    packs = refs[:members]
    other_ref, spread_ref = refs[members : members + 2]
    mt_ref = refs[members + 2]
    out_refs = refs[members + 3 : members + 3 + groups]
    rows_ref = refs[members + 3 + groups]
    core = idx_ref[2 * members * tiles]
    mt_ref[...] = jnp.zeros_like(mt_ref)
    byte_rows = jnp.concatenate(
        [
            jnp.concatenate(
                [p[items : items + half, :], p[items + half : items + 2 * half, :]], axis=1
            )
            for p in packs
        ],
        axis=0,
    )
    shift = lax.broadcasted_iota(jnp.int32, (members * half, 2 * BLOCK), 1) % 8
    for q in range(tiles // 2):
        spread = dot(byte_rows, spread_ref[:, q * 2 * BLOCK : (q + 1) * 2 * BLOCK])
        bits = jnp.right_shift(spread.astype(jnp.int32), shift) & 1
        mask = bits.astype(F32).astype(BF16)
        for l in range(members):
            for b in range(2):
                at = 2 * (l * tiles + 2 * q + b)
                row = pl.multiple_of(idx_ref[at], half)
                lane = pl.multiple_of(idx_ref[at + 1], BLOCK)
                where = (pl.ds(row, half), pl.ds(lane, BLOCK))
                mt_ref[where] = (
                    mt_ref[where]
                    + mask[l * half : (l + 1) * half, b * BLOCK : (b + 1) * BLOCK]
                )
    join_halves(core, rows_ref, packs, other_ref, items)
    per = members * half
    for i in range(groups):
        total = dot(mt_ref[i * per : (i + 1) * per, :], rows_ref[...])
        out_refs[i][...] = total.astype(out_refs[i].dtype)


def turn_body(mt_ref, out_ref, *, items):
    for c in range(mt_ref.shape[0] // BLOCK):
        block = mt_ref[c * BLOCK : (c + 1) * BLOCK, 0:items].astype(F32)
        out_ref[:, c * BLOCK : (c + 1) * BLOCK] = block.T.astype(BF16)


def add_all(refs):
    total = refs[0][...].astype(F32)
    for r in refs[1:]:
        total = total + r[...].astype(F32)
    return total


def rms(values):
    return lax.rsqrt(jnp.mean(values * values, axis=-1, keepdims=True) + NORM_EPSILON)


def halves(own_ref, other_ref, axis):
    for ref in (own_ref, other_ref):
        for c in range(ref.shape[axis] // CHUNK):
            yield ref, c * CHUNK


def basket_body(*refs, groups):
    parts = refs[:groups]
    gain_ref, gate_a, gate_b, up_a, up_b, down_a, down_b = refs[groups : groups + 7]
    out_ref, sum_ref, value_ref, slope_ref = refs[groups + 7 :]
    total = add_all(parts)
    sum_ref[...] = total
    normed = total * rms(total) * gain_ref[...]
    normed_bf = normed.astype(BF16)
    acc = normed
    at = 0
    for gate, up, down in ((gate_a, up_a, down_a), (gate_b, up_b, down_b)):
        for c in range(0, gate.shape[1], CHUNK):
            gate_pre = dot(normed_bf, gate[:, c : c + CHUNK])
            up_pre = dot(normed_bf, up[:, c : c + CHUNK])
            sig = sigmoid(gate_pre)
            value = gate_pre * sig
            acc = acc + dot((value * up_pre).astype(BF16), down[c : c + CHUNK, :])
            value_ref[:, at : at + CHUNK] = value.astype(BF16)
            slope_ref[:, at : at + CHUNK] = (up_pre * (sig + value * (1.0 - sig))).astype(BF16)
            at += CHUNK
    out_ref[...] = acc.astype(BF16)


def message_body(core_ref, mo_ref, *refs, groups):
    parts = refs[:groups]
    mine_ref, theirs_ref, all_ref = refs[groups:]
    per = parts[0].shape[0]
    total = dot(mo_ref[:, 0:per], parts[0][...])
    for i in range(1, groups):
        total = total + dot(mo_ref[:, i * per : (i + 1) * per], parts[i][...])
    all_ref[...] = total
    rows = mine_ref.shape[0]
    core = core_ref[0]
    mine_ref[...] = all_ref[pl.ds(pl.multiple_of(core * rows, rows), rows), :]
    theirs_ref[...] = all_ref[pl.ds(pl.multiple_of((1 - core) * rows, rows), rows), :]


def item_hidden_body(core_ref, mine_ref, other_ref, down_a, down_b, out_ref, cot_ref):
    core = core_ref[0]
    width = mine_ref.shape[1]
    cot_ref[:, pl.ds(pl.multiple_of(core * width, width), width)] = mine_ref[...]
    cot_ref[:, pl.ds(pl.multiple_of((1 - core) * width, width), width)] = other_ref[...]
    cot = cot_ref[...]
    at = 0
    for down in (down_a, down_b):
        for c in range(0, down.shape[0], CHUNK):
            out_ref[:, at : at + CHUNK] = dot_nt(cot, down[c : c + CHUNK, :])
            at += CHUNK


def item_body(mine_ref, other_ref, hidden_ref, gain_ref, gate_a, gate_b, up_a, up_b, out_ref):
    message = mine_ref[...] + other_ref[...]
    scale = rms(message)
    gain = gain_ref[...]
    query = (message * scale * gain).astype(BF16)
    acc = jnp.zeros_like(message)
    at = 0
    for gate, up in ((gate_a, up_a), (gate_b, up_b)):
        for c in range(0, gate.shape[1], CHUNK):
            gate_w = gate[:, c : c + CHUNK]
            up_w = up[:, c : c + CHUNK]
            gate_pre = dot(query, gate_w)
            up_pre = dot(query, up_w)
            sig = sigmoid(gate_pre)
            value = gate_pre * sig
            hidden = hidden_ref[:, at : at + CHUNK]
            grad_up = (hidden * value).astype(BF16)
            grad_gate = (hidden * up_pre * (sig + value * (1.0 - sig))).astype(BF16)
            acc = acc + dot_nt(grad_gate, gate_w) + dot_nt(grad_up, up_w)
            at += CHUNK
    weighted = gain * acc
    inner = jnp.mean(weighted * message, axis=1, keepdims=True)
    cubed = scale * scale * scale
    out_ref[...] = (scale * weighted - message * (cubed * inner)).astype(BF16)


def grad_sums_body(core_ref, mt_ref, *refs, members, groups):
    owns = refs[:members]
    other_ref = refs[members]
    out_refs = refs[members + 1 : members + 1 + groups]
    rows_ref = refs[members + 1 + groups]
    core = core_ref[0]
    rows = owns[0].shape[0]
    for l in range(members):
        mine = pl.multiple_of((2 * l + core) * rows, rows)
        theirs = pl.multiple_of((2 * l + 1 - core) * rows, rows)
        rows_ref[pl.ds(mine, rows), :] = owns[l][...]
        rows_ref[pl.ds(theirs, rows), :] = other_ref[l * rows : (l + 1) * rows, :]
    per = out_refs[0].shape[0]
    for i in range(groups):
        total = dot(mt_ref[i * per : (i + 1) * per, :], rows_ref[...])
        out_refs[i][...] = total.astype(out_refs[i].dtype)


def basket_back_body(*refs, groups):
    parts = refs[:groups]
    sum_ref, value_ref, slope_ref, gain_ref = refs[groups : groups + 4]
    gate_a, gate_b, up_a, up_b, down_a, down_b, out_ref = refs[groups + 4 :]
    grad_out = add_all(parts)
    grad_bf = grad_out.astype(BF16)
    acc = grad_out
    at = 0
    for gate, up, down in ((gate_a, up_a, down_a), (gate_b, up_b, down_b)):
        for c in range(0, gate.shape[1], CHUNK):
            hidden = dot_nt(grad_bf, down[c : c + CHUNK, :])
            grad_up = (hidden * value_ref[:, at : at + CHUNK].astype(F32)).astype(BF16)
            grad_gate = (hidden * slope_ref[:, at : at + CHUNK].astype(F32)).astype(BF16)
            acc = acc + dot_nt(grad_gate, gate[:, c : c + CHUNK])
            acc = acc + dot_nt(grad_up, up[:, c : c + CHUNK])
            at += CHUNK
    total = sum_ref[...]
    scale = rms(total)
    weighted = gain_ref[...] * acc
    inner = jnp.mean(weighted * total, axis=1, keepdims=True)
    cubed = scale * scale * scale
    out_ref[...] = (scale * weighted - total * (cubed * inner)).astype(BF16)


def back_body(core_ref, mo_ref, *refs, groups):
    parts = refs[:groups]
    mine_ref, theirs_ref, all_ref = refs[groups:]
    per = parts[0].shape[0]
    total = dot(mo_ref[:, 0:per], parts[0][...])
    for i in range(1, groups):
        total = total + dot(mo_ref[:, i * per : (i + 1) * per], parts[i][...])
    all_ref[...] = total
    width = mine_ref.shape[1]
    core = core_ref[0]
    mine_ref[...] = all_ref[:, pl.ds(pl.multiple_of(core * width, width), width)]
    theirs_ref[...] = all_ref[:, pl.ds(pl.multiple_of((1 - core) * width, width), width)]


def adam_body(back_ref, other_ref, cot_ref, rows_ref, first_ref, second_ref, r_ref, f_ref, s_ref):
    gradient = cot_ref[...].astype(F32) + (back_ref[...] + other_ref[...])
    first = BETA_FIRST * first_ref[...] + (1.0 - BETA_FIRST) * gradient
    second = BETA_SECOND * second_ref[...] + (1.0 - BETA_SECOND) * gradient * gradient
    f_ref[...] = first
    s_ref[...] = second
    r_ref[...] = rows_ref[...] - LEARNING_RATE * first / (jnp.sqrt(second) + ADAM_EPSILON)


def local(
    item_rows,
    first_moment,
    second_moment,
    item_cot,
    tile_bits,
    tile_item,
    tile_dest,
    basket_gain,
    item_gain,
    gate_basket,
    up_basket,
    down_basket,
    gate_item,
    up_item,
    down_item,
):
    shards = lax.axis_size("shard")
    members = GATHER if shards % GATHER == 0 else 1
    groups = shards // members
    items, width = item_rows.shape
    features = basket_gain.shape[0]
    tiles, words, _ = tile_bits.shape
    half = BLOCK // 2
    item_half = items // 2
    hidden = 2 * gate_basket.shape[1]
    per = members * half
    core = lax.axis_index("mp")
    place = lax.axis_index("shard") % groups
    core_arr = core.astype(jnp.int32).reshape(1)

    def swap(x):
        return lax.ppermute(x, "mp", [(0, 1), (1, 0)])

    def gather(x):
        return [
            lax.ppermute(
                x, "shard", [(s, (((s // groups) ^ k) * groups) + s % groups) for s in range(shards)]
            )
            for k in range(1, members)
        ]

    def exchange(xs):
        return [
            lax.ppermute(
                xs[k - 1],
                "shard",
                [(s, (s // groups) * groups + ((s % groups) ^ k)) for s in range(shards)],
            )
            for k in range(1, groups)
        ]

    meta = jnp.stack([tile_dest % 128, tile_dest // 128, tile_item]).astype(BF16)
    meta = jnp.pad(meta, ((0, 13), (0, width - tiles)))
    pack = run(
        functools.partial(pack_body, half=half),
        sds((items + 2 * half + 16, width), BF16),
        (core_arr,),
        (item_rows, tile_bits.reshape(tiles * words, BLOCK), meta),
        scratch=[pltpu.VMEM((BLOCK, tiles * words), F32)] * 2,
        name="pack",
    )
    packs = [pack] + gather(pack)
    rows_other = swap(jnp.concatenate([q[:items] for q in packs], axis=0))
    cot_other = swap(lax.dynamic_slice_in_dim(item_cot, (1 - core) * item_half, item_half, 0))
    cot_mine = lax.dynamic_slice_in_dim(item_cot, core * item_half, item_half, 0)
    gate_b, up_b, down_b = gate_basket, up_basket, down_basket
    gate_bo, up_bo, down_bo = swap(gate_basket), swap(up_basket), swap(down_basket)
    gate_io, up_io, down_io = swap(gate_item), swap(up_item), swap(down_item)

    metas = jnp.stack([q[items + 2 * half : items + 2 * half + 3, :tiles] for q in packs])
    metas = metas.astype(jnp.int32)
    dest = metas[:, 0] + 128 * metas[:, 1]
    row_at = (((dest % groups) ^ place) * members + dest // groups) * half
    lane_at = metas[:, 2] * BLOCK + items * jnp.arange(members, dtype=jnp.int32)[:, None]
    idx = jnp.concatenate([jnp.stack([row_at, lane_at], axis=-1).reshape(-1), core_arr])

    source = lax.broadcasted_iota(jnp.int32, (2 * tiles * words, tiles * BLOCK), 0)
    target = lax.broadcasted_iota(jnp.int32, (2 * tiles * words, tiles * BLOCK), 1)
    spread = (
        (source % (tiles * words) == target // 16) & (source // (tiles * words) == (target // 8) % 2)
    ).astype(BF16)

    part_shapes = [sds((per, features), F32)] + [sds((per, features), BF16)] * (groups - 1)
    mt, *parts = run(
        functools.partial(
            sums_body, members=members, groups=groups, half=half, items=items, tiles=tiles
        ),
        [sds((shards * half, members * items), BF16)] + part_shapes,
        (idx,),
        (*packs, rows_other, spread),
        scratch=[pltpu.VMEM((members * items, features), BF16)],
        flops=1 << 30,
        name="sums",
    )
    received = exchange(parts[1:])
    mo = run(
        functools.partial(turn_body, items=items),
        sds((items, shards * half), BF16),
        (),
        (mt,),
        flops=1 << 29,
        name="turn",
    )
    item_hidden = run(
        item_hidden_body,
        sds((item_half, hidden), F32),
        (core_arr,),
        (cot_mine, cot_other, down_item, down_io),
        scratch=[pltpu.VMEM((item_half, features), BF16)],
        flops=1 << 29,
        name="item_hidden",
    )
    basket_out, basket_sum, value, slope = run(
        functools.partial(basket_body, groups=groups),
        [
            sds((per, features), BF16),
            sds((per, features), F32),
            sds((per, hidden), BF16),
            sds((per, hidden), BF16),
        ],
        (),
        (
            parts[0],
            *received,
            basket_gain.reshape(1, features),
            gate_b,
            gate_bo,
            up_b,
            up_bo,
            down_b,
            down_bo,
        ),
        flops=1 << 30,
        name="basket",
    )
    outs = [basket_out] + exchange([basket_out] * (groups - 1))
    message_mine, message_theirs = run(
        functools.partial(message_body, groups=groups),
        [sds((item_half, features), F32)] * 2,
        (core_arr,),
        (mo, *outs),
        scratch=[pltpu.VMEM((items, features), F32)],
        flops=1 << 28,
        name="message",
    )
    message_other = swap(message_theirs)
    grad_message = run(
        item_body,
        sds((item_half, features), BF16),
        (),
        (
            message_mine,
            message_other,
            item_hidden,
            item_gain.reshape(1, features),
            gate_item,
            gate_io,
            up_item,
            up_io,
        ),
        flops=1 << 30,
        name="item",
    )
    grads = [grad_message] + gather(grad_message)
    grads_other = swap(jnp.concatenate(grads, axis=0))
    grad_parts = run(
        functools.partial(grad_sums_body, members=members, groups=groups),
        part_shapes,
        (core_arr,),
        (mt, *grads, grads_other),
        scratch=[pltpu.VMEM((members * items, features), BF16)],
        flops=1 << 29,
        name="grad_sums",
    )
    grad_received = exchange(grad_parts[1:])
    grad_sum = run(
        functools.partial(basket_back_body, groups=groups),
        sds((per, features), BF16),
        (),
        (
            grad_parts[0],
            *grad_received,
            basket_sum,
            value,
            slope,
            basket_gain.reshape(1, features),
            gate_b,
            gate_bo,
            up_b,
            up_bo,
            down_b,
            down_bo,
        ),
        flops=1 << 30,
        name="basket_back",
    )
    sums = [grad_sum] + exchange([grad_sum] * (groups - 1))
    back_mine, back_theirs = run(
        functools.partial(back_body, groups=groups),
        [sds((items, width), F32)] * 2,
        (core_arr,),
        (mo, *sums),
        scratch=[pltpu.VMEM((items, features), F32)],
        flops=1 << 28,
        name="back",
    )
    back_other = swap(back_theirs)
    new_rows, new_first, new_second = run(
        adam_body,
        [sds((items, width), F32)] * 3,
        (),
        (back_mine, back_other, item_cot, item_rows, first_moment, second_moment),
        name="adam",
    )
    return (new_rows, new_first, new_second)


def solution(mesh):
    return jax.shard_map(
        local,
        mesh=mesh,
        in_specs=(
            P("shard", "mp"),
            P("shard", "mp"),
            P("shard", "mp"),
            P("shard", "mp"),
            P("shard", None, None),
            P("shard"),
            P("shard"),
            P(),
            P(),
            P(None, "mp"),
            P(None, "mp"),
            P("mp", None),
            P(None, "mp"),
            P(None, "mp"),
            P("mp", None),
        ),
        out_specs=(P("shard", "mp"), P("shard", "mp"), P("shard", "mp")),
        check_vma=False,
    )
```

profile of v0, /device:TPU:0, one launch (start us, length us, event | category | flops | bytes accessed | tf_op | source)
XLA Modules:
  0.0 98.6 jit_solution(6898924100445562395)
XLA Ops:
  0.6 0.7 fusion.30
  1.4 0.9 copy-done.3
  2.2 0.8 copy-done.16
  3.2 5.1 %collective-permute-start.2 = (bf16[400,128]{1,0:T(8,128)(2,1)S(1)}, bf16[400,128]{1,0:T(8,128)(2,1)S(1)}, u32[]{:S(2)}, u32[]{:S(2)}) collective-permute-start(bf16[400,128]{1,0:T(8,128)(2,1)S(1)} %pack.1.refs_0_), channel_id=1, source_target_pairs={{0,24},{2,26},{4,28},{6,30},{8,16},{10,18},{12,20},{14,22},{16,8},... | collective-permute-start | bytes 307208 | tf_op jit(solution)/shard_map/ppermute | solution.py:324
  10.2 4.7 %collective-permute-done.refs_1_ = bf16[400,128]{1,0:T(8,128)(2,1)S(1)} collective-permute-done((bf16[400,128]{1,0:T(8,128)(2,1)S(1)}, bf16[400,128]{1,0:T(8,128)(2,1)S(1)}, u32[]{:S(2)}, u32[]{:S(2)}) %collective-permute-start) | collective-permute-done | bytes 102432 | tf_op jit(solution)/shard_map/ppermute | solution.py:324
  14.9 2.0 %collective-permute-done.1.refs_2_ = bf16[400,128]{1,0:T(8,128)(2,1)S(1)} collective-permute-done((bf16[400,128]{1,0:T(8,128)(2,1)S(1)}, bf16[400,128]{1,0:T(8,128)(2,1)S(1)}, u32[]{:S(2)}, u32[]{:S(2)}) %collective-permute-start.1) | collective-permute-done | bytes 102432 | tf_op jit(solution)/shard_map/ppermute | solution.py:324
  17.5 1.1 %collective-permute-done.3.refs_4_ = bf16[1024,128]{1,0:T(8,128)(2,1)S(1)} collective-permute-done((bf16[1024,128]{1,0:T(8,128)(2,1)S(1)}, bf16[1024,128]{1,0:T(8,128)(2,1)S(1)}, u32[]{:S(2)}, u32[]{:S(2)}) %collective-permute-start.3) | collective-permute-done | bytes 262176 | tf_op jit(solution)/shard_map/ppermute | solution.py:320
  18.6 0.7 copy-done.21
  19.3 0.9 copy-done.22
  20.3 2.2 %sums.1 = (bf16[1024,1024]{1,0:T(8,128)(2,1)S(1)}, f32[256,256]{1,0:T(8,128)S(1)}, bf16[256,256]{1,0:T(8,128)(2,1)S(1)}, bf16[256,256]{1,0:T(8,128)(2,1)S(1)}, bf16[256,256]{1,0:T(8,128)(2,1)S(1)}) custom-call(s32[129]{0:T(256)S(1)} %pad_add_fusion.1.idx_ref, bf16[400,128]{1,0:T(8,128)(2,1)S(1)} %pack.1.refs_0_, ...), custom_call_target="tpu_custom_call" | custom-call | flops 1073741824 | bytes 1048576 | tf_op jit(solution)/shard_map/sums/pallas_call | solution.py:38
  22.5 1.6 %collective-permute-start.4 = (bf16[256,256]{1,0:T(8,128)(2,1)S(1)}, bf16[256,256]{1,0:T(8,128)(2,1)S(1)}, u32[]{:S(2)}, u32[]{:S(2)}) collective-permute-start(bf16[256,256]{1,0:T(8,128)(2,1)S(1)} %get-tuple-element.22), channel_id=1, source_target_pairs={{0,2},{2,0},{4,6},{6,4},{8,10},{10,8},{12,14},{14,12},{16,18},{18,... | collective-permute-start | bytes 393224 | tf_op jit(solution)/shard_map/ppermute | solution.py:332
  24.0 1.5 %collective-permute-start.5 = (bf16[256,256]{1,0:T(8,128)(2,1)S(1)}, bf16[256,256]{1,0:T(8,128)(2,1)S(1)}, u32[]{:S(2)}, u32[]{:S(2)}) collective-permute-start(bf16[256,256]{1,0:T(8,128)(2,1)S(1)} %get-tuple-element.23), channel_id=1, source_target_pairs={{0,4},{2,6},{4,0},{6,2},{8,12},{10,14},{12,8},{14,10},{16,20},{18,... | collective-permute-start | bytes 393224 | tf_op jit(solution)/shard_map/ppermute | solution.py:332
  25.5 2.5 %collective-permute-done.4.refs_1_ = bf16[256,256]{1,0:T(8,128)(2,1)S(1)} collective-permute-done((bf16[256,256]{1,0:T(8,128)(2,1)S(1)}, bf16[256,256]{1,0:T(8,128)(2,1)S(1)}, u32[]{:S(2)}, u32[]{:S(2)}) %collective-permute-start.4) | collective-permute-done | bytes 131104 | tf_op jit(solution)/shard_map/ppermute | solution.py:332
  28.1 2.5 %collective-permute-start.6 = (bf16[256,256]{1,0:T(8,128)(2,1)S(1)}, bf16[256,256]{1,0:T(8,128)(2,1)S(1)}, u32[]{:S(2)}, u32[]{:S(2)}) collective-permute-start(bf16[256,256]{1,0:T(8,128)(2,1)S(1)} %get-tuple-element.24), channel_id=1, source_target_pairs={{0,6},{2,4},{4,2},{6,0},{8,14},{10,12},{12,10},{14,8},{16,22},{18,... | collective-permute-start | bytes 393224 | tf_op jit(solution)/shard_map/ppermute | solution.py:332
  30.5 3.4 %collective-permute-done.6.refs_3_ = bf16[256,256]{1,0:T(8,128)(2,1)S(1)} collective-permute-done((bf16[256,256]{1,0:T(8,128)(2,1)S(1)}, bf16[256,256]{1,0:T(8,128)(2,1)S(1)}, u32[]{:S(2)}, u32[]{:S(2)}) %collective-permute-start.6) | collective-permute-done | bytes 131104 | tf_op jit(solution)/shard_map/ppermute | solution.py:332
  34.5 1.0 %copy-done.5 = bf16[256,1024]{1,0:T(8,128)(2,1)S(1)} copy-done((bf16[256,1024]{1,0:T(8,128)(2,1)S(1)}, bf16[256,1024]{1,0:T(8,128)(2,1)}, u32[]{:S(2)}) %copy-start.5) | copy-done | bytes 524312
  35.5 1.0 %copy-done.7 = bf16[256,1024]{1,0:T(8,128)(2,1)S(1)} copy-done((bf16[256,1024]{1,0:T(8,128)(2,1)S(1)}, bf16[256,1024]{1,0:T(8,128)(2,1)}, u32[]{:S(2)}) %copy-start.7) | copy-done | bytes 524312
  36.5 1.0 %copy-done.9 = bf16[1024,256]{1,0:T(8,128)(2,1)S(1)} copy-done((bf16[1024,256]{1,0:T(8,128)(2,1)S(1)}, bf16[1024,256]{1,0:T(8,128)(2,1)}, u32[]{:S(2)}) %copy-start.9) | copy-done | bytes 524312
  37.6 0.7 copy-done.17
  38.3 3.5 %basket.1 = (bf16[256,256]{1,0:T(8,128)(2,1)}, f32[256,256]{1,0:T(8,128)S(1)}, bf16[256,2048]{1,0:T(8,128)(2,1)S(1)}, bf16[256,2048]{1,0:T(8,128)(2,1)S(1)}) custom-call(f32[256,256]{1,0:T(8,128)S(1)} %get-tuple-element.21.refs_0_, bf16[256,256]{1,0:T(8,128)(2,1)S(1)} %collective-permute-done.4.refs_1_, bf16[256,256]{1,0:T(8,128)(2,1)S(1)} %collective-permute-done.5.refs_2_, ...), custom_call_target="tpu_custom_call" | custom-call | flops 1073741824 | bytes 1048576 | tf_op jit(solution)/shard_map/basket/pallas_call | solution.py:38
  41.8 1.0 %copy-done = bf16[256,2048]{1,0:T(8,128)(2,1)} copy-done((bf16[256,2048]{1,0:T(8,128)(2,1)}, bf16[256,2048]{1,0:T(8,128)(2,1)S(1)}, u32[]{:S(2)}) %copy-start) | copy-done | bytes 1048600
  42.8 1.5 %collective-permute-start.10 = (bf16[256,256]{1,0:T(8,128)(2,1)}, bf16[256,256]{1,0:T(8,128)(2,1)S(1)}, u32[]{:S(2)}, u32[]{:S(2)}) collective-permute-start(bf16[256,256]{1,0:T(8,128)(2,1)} %get-tuple-element.25.refs_0_), channel_id=1, source_target_pairs={{0,2},{2,0},{4,6},{6,4},{8,10},{10,8},{12,14},{14,12},{16,18},{18,... | collective-permute-start | bytes 393224 | tf_op jit(solution)/shard_map/ppermute | solution.py:332
  44.3 1.5 %collective-permute-start.11 = (bf16[256,256]{1,0:T(8,128)(2,1)}, bf16[256,256]{1,0:T(8,128)(2,1)}, u32[]{:S(2)}, u32[]{:S(2)}) collective-permute-start(bf16[256,256]{1,0:T(8,128)(2,1)} %get-tuple-element.25.refs_0_), channel_id=1, source_target_pairs={{0,4},{2,6},{4,0},{6,2},{8,12},{10,14},{12,8},{14,10},{16,20},{18,... | collective-permute-start | bytes 393224 | tf_op jit(solution)/shard_map/ppermute | solution.py:332
  45.8 2.6 %collective-permute-done.10.refs_1_ = bf16[256,256]{1,0:T(8,128)(2,1)S(1)} collective-permute-done((bf16[256,256]{1,0:T(8,128)(2,1)}, bf16[256,256]{1,0:T(8,128)(2,1)S(1)}, u32[]{:S(2)}, u32[]{:S(2)}) %collective-permute-start.10) | collective-permute-done | bytes 131104 | tf_op jit(solution)/shard_map/ppermute | solution.py:332
  49.1 2.5 %collective-permute-start.12 = (bf16[256,256]{1,0:T(8,128)(2,1)}, bf16[256,256]{1,0:T(8,128)(2,1)}, u32[]{:S(2)}, u32[]{:S(2)}) collective-permute-start(bf16[256,256]{1,0:T(8,128)(2,1)} %get-tuple-element.25.refs_0_), channel_id=1, source_target_pairs={{0,6},{2,4},{4,2},{6,0},{8,14},{10,12},{12,10},{14,8},{16,22},{18,... | collective-permute-start | bytes 393224 | tf_op jit(solution)/shard_map/ppermute | solution.py:332
  51.8 3.5 %collective-permute-done.12.refs_3_ = bf16[256,256]{1,0:T(8,128)(2,1)} collective-permute-done((bf16[256,256]{1,0:T(8,128)(2,1)}, bf16[256,256]{1,0:T(8,128)(2,1)}, u32[]{:S(2)}, u32[]{:S(2)}) %collective-permute-start.12) | collective-permute-done | bytes 131104 | tf_op jit(solution)/shard_map/ppermute | solution.py:332
  55.3 1.4 %message.1 = (f32[128,256]{1,0:T(8,128)S(1)}, f32[128,256]{1,0:T(8,128)S(1)}) custom-call(s32[1]{0:T(128)} %bitcast.core_ref, bf16[256,1024]{1,0:T(8,128)(2,1)S(1)} %turn.1.mo_ref, bf16[256,256]{1,0:T(8,128)(2,1)} %get-tuple-element.25.refs_0_, bf16[256,256]{1,0:T(8,128)(2,1)S(1)} %copy-done.15, bf16[256,256]{1,0:T(8,128)(2,1)} %collective-permute-done.11.refs_2_, ...), custom_call_target="tpu_custom_call" | custom-call | flops 268435456 | bytes 1048576 | tf_op jit(solution)/shard_map/message/pallas_call | solution.py:38
  57.3 0.9 collective-permute-done.14.other_ref
  58.2 1.5 %item_hidden.1.hidden_ref = f32[128,2048]{1,0:T(8,128)S(1)} custom-call(s32[1]{0:T(128)} %bitcast.core_ref, bf16[128,128]{1,0:T(8,128)(2,1)S(1)} %get-tuple-element.38.mine_ref, bf16[128,128]{1,0:T(8,128)(2,1)S(1)} %collective-permute-done.14.other_ref, bf16[1024,256]{1,0:T(8,128)(2,1)S(1)} %copy-done.2, bf16[1024,256]{1,0:T(8,128)(2,1)} %collective-permute-done.15.down_b), custom_call_target="tpu_custom_call" | custom-call | flops 536870912 | bytes 1048576 | tf_op jit(solution)/shard_map/item_hidden/pallas_call | solution.py:38
  59.7 3.0 %item.1.refs_0_ = bf16[128,256]{1,0:T(8,128)(2,1)S(1)} custom-call(f32[128,256]{1,0:T(8,128)S(1)} %get-tuple-element.26.mine_ref, f32[128,256]{1,0:T(8,128)S(1)} %collective-permute-done.13.other_ref, f32[128,2048]{1,0:T(8,128)S(1)} %item_hidden.1.hidden_ref, f32[1,256]{1,0:T(1,128)S(1)} %bitcast.23, bf16[256,1024]{1,0:T(8,128)(2,1)S(1)} %copy-done.19, ...), custom_call_target="tpu_custom_call" | custom-call | flops 1073741824 | bytes 1048576 | tf_op jit(solution)/shard_map/item/pallas_call | solution.py:38
  62.8 1.4 %collective-permute-start.18 = (bf16[128,256]{1,0:T(8,128)(2,1)S(1)}, bf16[128,256]{1,0:T(8,128)(2,1)S(1)}, u32[]{:S(2)}, u32[]{:S(2)}) collective-permute-start(bf16[128,256]{1,0:T(8,128)(2,1)S(1)} %item.1.refs_0_), channel_id=1, source_target_pairs={{0,8},{2,10},{4,12},{6,14},{8,0},{10,2},{12,4},{14,6},{16,24},{18,... | collective-permute-start | bytes 196616 | tf_op jit(solution)/shard_map/ppermute | solution.py:324
  64.2 1.7 %collective-permute-start.19 = (bf16[128,256]{1,0:T(8,128)(2,1)S(1)}, bf16[128,256]{1,0:T(8,128)(2,1)S(1)}, u32[]{:S(2)}, u32[]{:S(2)}) collective-permute-start(bf16[128,256]{1,0:T(8,128)(2,1)S(1)} %item.1.refs_0_), channel_id=1, source_target_pairs={{0,16},{2,18},{4,20},{6,22},{8,24},{10,26},{12,28},{14,30},{16,0},... | collective-permute-start | bytes 196616 | tf_op jit(solution)/shard_map/ppermute | solution.py:324
  65.9 1.3 %collective-permute-start.20 = (bf16[128,256]{1,0:T(8,128)(2,1)S(1)}, bf16[128,256]{1,0:T(8,128)(2,1)S(1)}, u32[]{:S(2)}, u32[]{:S(2)}) collective-permute-start(bf16[128,256]{1,0:T(8,128)(2,1)S(1)} %item.1.refs_0_), channel_id=1, source_target_pairs={{0,24},{2,26},{4,28},{6,30},{8,16},{10,18},{12,20},{14,22},{16,8},... | collective-permute-start | bytes 196616 | tf_op jit(solution)/shard_map/ppermute | solution.py:324
  67.3 5.0 %collective-permute-done.19.refs_2_ = bf16[128,256]{1,0:T(8,128)(2,1)S(1)} collective-permute-done((bf16[128,256]{1,0:T(8,128)(2,1)S(1)}, bf16[128,256]{1,0:T(8,128)(2,1)S(1)}, u32[]{:S(2)}, u32[]{:S(2)}) %collective-permute-start.19) | collective-permute-done | bytes 65568 | tf_op jit(solution)/shard_map/ppermute | solution.py:324
  72.4 1.5 %collective-permute-done.21.refs_4_ = bf16[512,256]{1,0:T(8,128)(2,1)S(1)} collective-permute-done((bf16[512,256]{1,0:T(8,128)(2,1)S(1)}, bf16[512,256]{1,0:T(8,128)(2,1)S(1)}, u32[]{:S(2)}, u32[]{:S(2)}) %collective-permute-start.21) | collective-permute-done | bytes 262176 | tf_op jit(solution)/shard_map/ppermute | solution.py:320
  73.9 0.7 grad_sums.1
  74.6 1.6 %collective-permute-start.22 = (bf16[256,256]{1,0:T(8,128)(2,1)S(1)}, bf16[256,256]{1,0:T(8,128)(2,1)S(1)}, u32[]{:S(2)}, u32[]{:S(2)}) collective-permute-start(bf16[256,256]{1,0:T(8,128)(2,1)S(1)} %get-tuple-element.29), channel_id=1, source_target_pairs={{0,2},{2,0},{4,6},{6,4},{8,10},{10,8},{12,14},{14,12},{16,18},{18,... | collective-permute-start | bytes 393224 | tf_op jit(solution)/shard_map/ppermute | solution.py:332
  76.2 1.5 %collective-permute-start.23 = (bf16[256,256]{1,0:T(8,128)(2,1)S(1)}, bf16[256,256]{1,0:T(8,128)(2,1)S(1)}, u32[]{:S(2)}, u32[]{:S(2)}) collective-permute-start(bf16[256,256]{1,0:T(8,128)(2,1)S(1)} %get-tuple-element.30), channel_id=1, source_target_pairs={{0,4},{2,6},{4,0},{6,2},{8,12},{10,14},{12,8},{14,10},{16,20},{18,... | collective-permute-start | bytes 393224 | tf_op jit(solution)/shard_map/ppermute | solution.py:332
  78.2 2.5 %collective-permute-done.22.refs_1_ = bf16[256,256]{1,0:T(8,128)(2,1)S(1)} collective-permute-done((bf16[256,256]{1,0:T(8,128)(2,1)S(1)}, bf16[256,256]{1,0:T(8,128)(2,1)S(1)}, u32[]{:S(2)}, u32[]{:S(2)}) %collective-permute-start.22) | collective-permute-done | bytes 131104 | tf_op jit(solution)/shard_map/ppermute | solution.py:332
  80.7 3.6 %collective-permute-done.23.refs_2_ = bf16[256,256]{1,0:T(8,128)(2,1)S(1)} collective-permute-done((bf16[256,256]{1,0:T(8,128)(2,1)S(1)}, bf16[256,256]{1,0:T(8,128)(2,1)S(1)}, u32[]{:S(2)}, u32[]{:S(2)}) %collective-permute-start.23) | collective-permute-done | bytes 131104 | tf_op jit(solution)/shard_map/ppermute | solution.py:332
  84.3 3.2 %basket_back.1.refs_0_ = bf16[256,256]{1,0:T(8,128)(2,1)S(1)} custom-call(f32[256,256]{1,0:T(8,128)S(1)} %get-tuple-element.28.refs_0_, bf16[256,256]{1,0:T(8,128)(2,1)S(1)} %collective-permute-done.22.refs_1_, bf16[256,256]{1,0:T(8,128)(2,1)S(1)} %collective-permute-done.23.refs_2_, bf16[256,256]{1,0:T(8,128)(2,1)S(1)} %collective-permute-done.24.refs_3_, ...), custom_call_target="tpu_custom_call" | custom-call | flops 1073741824 | bytes 1048576 | tf_op jit(solution)/shard_map/basket_back/pallas_call | solution.py:38
  87.5 1.3 %collective-permute-start.25 = (bf16[256,256]{1,0:T(8,128)(2,1)S(1)}, bf16[256,256]{1,0:T(8,128)(2,1)S(1)}, u32[]{:S(2)}, u32[]{:S(2)}) collective-permute-start(bf16[256,256]{1,0:T(8,128)(2,1)S(1)} %basket_back.1.refs_0_), channel_id=1, source_target_pairs={{0,2},{2,0},{4,6},{6,4},{8,10},{10,8},{12,14},{14,12},{16,18},{18,... | collective-permute-start | bytes 393224 | tf_op jit(solution)/shard_map/ppermute | solution.py:332
  88.8 0.8 collective-permute-start.26
  89.6 1.4 %collective-permute-start.27 = (bf16[256,256]{1,0:T(8,128)(2,1)S(1)}, bf16[256,256]{1,0:T(8,128)(2,1)S(1)}, u32[]{:S(2)}, u32[]{:S(2)}) collective-permute-start(bf16[256,256]{1,0:T(8,128)(2,1)S(1)} %basket_back.1.refs_0_), channel_id=1, source_target_pairs={{0,6},{2,4},{4,2},{6,0},{8,14},{10,12},{12,10},{14,8},{16,22},{18,... | collective-permute-start | bytes 393224 | tf_op jit(solution)/shard_map/ppermute | solution.py:332
  91.1 2.4 %collective-permute-done.25.refs_1_ = bf16[256,256]{1,0:T(8,128)(2,1)S(1)} collective-permute-done((bf16[256,256]{1,0:T(8,128)(2,1)S(1)}, bf16[256,256]{1,0:T(8,128)(2,1)S(1)}, u32[]{:S(2)}, u32[]{:S(2)}) %collective-permute-start.25) | collective-permute-done | bytes 131104 | tf_op jit(solution)/shard_map/ppermute | solution.py:332
  93.5 2.5 %collective-permute-done.26.refs_2_ = bf16[256,256]{1,0:T(8,128)(2,1)S(1)} collective-permute-done((bf16[256,256]{1,0:T(8,128)(2,1)S(1)}, bf16[256,256]{1,0:T(8,128)(2,1)S(1)}, u32[]{:S(2)}, u32[]{:S(2)}) %collective-permute-start.26) | collective-permute-done | bytes 131104 | tf_op jit(solution)/shard_map/ppermute | solution.py:332
  96.4 1.3 %collective-permute-done.28.other_ref = f32[256,128]{1,0:T(8,128)S(1)} collective-permute-done((f32[256,128]{1,0:T(8,128)S(1)}, f32[256,128]{1,0:T(8,128)S(1)}, u32[]{:S(2)}, u32[]{:S(2)}) %collective-permute-start.28) | collective-permute-done | bytes 131104 | tf_op jit(solution)/shard_map/ppermute | solution.py:320
  97.8 0.8 adam.1
  (97 shorter events, 5.5 us)
Async XLA Ops:
  3.2 13.8 %collective-permute-start.2 = (bf16[400,128]{1,0:T(8,128)(2,1)S(1)}, bf16[400,128]{1,0:T(8,128)(2,1)S(1)}, u32[]{:S(2)}, u32[]{:S(2)}) collective-permute-start(bf16[400,128]{1,0:T(8,128)(2,1)S(1)} %pack.1.refs_0_), channel_id=1, source_target_pairs={{0,24},{2,26},{4,28},{6,30},{8,16},{10,18},{12,20},{14,22},{16,8},... | collective-permute-start | bytes 307208 | tf_op jit(solution)/shard_map/ppermute | solution.py:324
  8.3 8.6 %collective-permute-start.1 = (bf16[400,128]{1,0:T(8,128)(2,1)S(1)}, bf16[400,128]{1,0:T(8,128)(2,1)S(1)}, u32[]{:S(2)}, u32[]{:S(2)}) collective-permute-start(bf16[400,128]{1,0:T(8,128)(2,1)S(1)} %pack.1.refs_0_), channel_id=1, source_target_pairs={{0,16},{2,18},{4,20},{6,22},{8,24},{10,26},{12,28},{14,30},{16,0},... | collective-permute-start | bytes 307208 | tf_op jit(solution)/shard_map/ppermute | solution.py:324
  8.3 6.6 %collective-permute-start = (bf16[400,128]{1,0:T(8,128)(2,1)S(1)}, bf16[400,128]{1,0:T(8,128)(2,1)S(1)}, u32[]{:S(2)}, u32[]{:S(2)}) collective-permute-start(bf16[400,128]{1,0:T(8,128)(2,1)S(1)} %pack.1.refs_0_), channel_id=1, source_target_pairs={{0,8},{2,10},{4,12},{6,14},{8,0},{10,2},{12,4},{14,6},{16,24},{18,... | collective-permute-start | bytes 307208 | tf_op jit(solution)/shard_map/ppermute | solution.py:324
  9.0 25.0 %collective-permute-start.7 = (bf16[256,1024]{1,0:T(8,128)(2,1)}, bf16[256,1024]{1,0:T(8,128)(2,1)}, u32[]{:S(2)}, u32[]{:S(2)}) collective-permute-start(bf16[256,1024]{1,0:T(8,128)(2,1)} %refs_8_.1), channel_id=1, source_target_pairs={{0,1},{1,0},{2,3},{3,2},{4,5},{5,4},{6,7},{7,6},{8,9},{9,8},{10,11... | collective-permute-start | bytes 1572872 | tf_op jit(solution)/shard_map/ppermute | solution.py:320
  9.0 25.5 %collective-permute-start.8 = (bf16[256,1024]{1,0:T(8,128)(2,1)}, bf16[256,1024]{1,0:T(8,128)(2,1)}, u32[]{:S(2)}, u32[]{:S(2)}) collective-permute-start(bf16[256,1024]{1,0:T(8,128)(2,1)} %refs_10_.1), channel_id=1, source_target_pairs={{0,1},{1,0},{2,3},{3,2},{4,5},{5,4},{6,7},{7,6},{8,9},{9,8},{10,11... | collective-permute-start | bytes 1572872 | tf_op jit(solution)/shard_map/ppermute | solution.py:320
  14.9 19.5 %collective-permute-start.9 = (bf16[1024,256]{1,0:T(8,128)(2,1)}, bf16[1024,256]{1,0:T(8,128)(2,1)}, u32[]{:S(2)}, u32[]{:S(2)}) collective-permute-start(bf16[1024,256]{1,0:T(8,128)(2,1)} %refs_12_.1), channel_id=1, source_target_pairs={{0,1},{1,0},{2,3},{3,2},{4,5},{5,4},{6,7},{7,6},{8,9},{9,8},{10,11... | collective-permute-start | bytes 1572872 | tf_op jit(solution)/shard_map/ppermute | solution.py:320
  17.0 1.6 %collective-permute-start.3 = (bf16[1024,128]{1,0:T(8,128)(2,1)S(1)}, bf16[1024,128]{1,0:T(8,128)(2,1)S(1)}, u32[]{:S(2)}, u32[]{:S(2)}) collective-permute-start(bf16[1024,128]{1,0:T(8,128)(2,1)S(1)} %pad_maximum_fusion), channel_id=1, source_target_pairs={{0,1},{1,0},{2,3},{3,2},{4,5},{5,4},{6,7},{7,6},{8,9},{9,8},{10,11... | collective-permute-start | bytes 786440 | tf_op jit(solution)/shard_map/ppermute | solution.py:320
  19.3 0.9 copy-start.22
  22.5 5.6 %collective-permute-start.4 = (bf16[256,256]{1,0:T(8,128)(2,1)S(1)}, bf16[256,256]{1,0:T(8,128)(2,1)S(1)}, u32[]{:S(2)}, u32[]{:S(2)}) collective-permute-start(bf16[256,256]{1,0:T(8,128)(2,1)S(1)} %get-tuple-element.22), channel_id=1, source_target_pairs={{0,2},{2,0},{4,6},{6,4},{8,10},{10,8},{12,14},{14,12},{16,18},{18,... | collective-permute-start | bytes 393224 | tf_op jit(solution)/shard_map/ppermute | solution.py:332
  24.0 6.5 %collective-permute-start.5 = (bf16[256,256]{1,0:T(8,128)(2,1)S(1)}, bf16[256,256]{1,0:T(8,128)(2,1)S(1)}, u32[]{:S(2)}, u32[]{:S(2)}) collective-permute-start(bf16[256,256]{1,0:T(8,128)(2,1)S(1)} %get-tuple-element.23), channel_id=1, source_target_pairs={{0,4},{2,6},{4,0},{6,2},{8,12},{10,14},{12,8},{14,10},{16,20},{18,... | collective-permute-start | bytes 393224 | tf_op jit(solution)/shard_map/ppermute | solution.py:332
  28.1 5.9 %collective-permute-start.6 = (bf16[256,256]{1,0:T(8,128)(2,1)S(1)}, bf16[256,256]{1,0:T(8,128)(2,1)S(1)}, u32[]{:S(2)}, u32[]{:S(2)}) collective-permute-start(bf16[256,256]{1,0:T(8,128)(2,1)S(1)} %get-tuple-element.24), channel_id=1, source_target_pairs={{0,6},{2,4},{4,2},{6,0},{8,14},{10,12},{12,10},{14,8},{16,22},{18,... | collective-permute-start | bytes 393224 | tf_op jit(solution)/shard_map/ppermute | solution.py:332
  30.5 27.6 %collective-permute-start.15 = (bf16[1024,256]{1,0:T(8,128)(2,1)}, bf16[1024,256]{1,0:T(8,128)(2,1)}, u32[]{:S(2)}, u32[]{:S(2)}) collective-permute-start(bf16[1024,256]{1,0:T(8,128)(2,1)} %down_a.1), channel_id=1, source_target_pairs={{0,1},{1,0},{2,3},{3,2},{4,5},{5,4},{6,7},{7,6},{8,9},{9,8},{10,11... | collective-permute-start | bytes 1572872 | tf_op jit(solution)/shard_map/ppermute | solution.py:320
  33.9 25.7 %collective-permute-start.16 = (bf16[256,1024]{1,0:T(8,128)(2,1)}, bf16[256,1024]{1,0:T(8,128)(2,1)}, u32[]{:S(2)}, u32[]{:S(2)}) collective-permute-start(bf16[256,1024]{1,0:T(8,128)(2,1)} %gate_a.1), channel_id=1, source_target_pairs={{0,1},{1,0},{2,3},{3,2},{4,5},{5,4},{6,7},{7,6},{8,9},{9,8},{10,11... | collective-permute-start | bytes 1572872 | tf_op jit(solution)/shard_map/ppermute | solution.py:320
  33.9 25.7 %collective-permute-start.17 = (bf16[256,1024]{1,0:T(8,128)(2,1)}, bf16[256,1024]{1,0:T(8,128)(2,1)}, u32[]{:S(2)}, u32[]{:S(2)}) collective-permute-start(bf16[256,1024]{1,0:T(8,128)(2,1)} %up_a.1), channel_id=1, source_target_pairs={{0,1},{1,0},{2,3},{3,2},{4,5},{5,4},{6,7},{7,6},{8,9},{9,8},{10,11... | collective-permute-start | bytes 1572872 | tf_op jit(solution)/shard_map/ppermute | solution.py:320
  34.5 1.0 %copy-start.5 = (bf16[256,1024]{1,0:T(8,128)(2,1)S(1)}, bf16[256,1024]{1,0:T(8,128)(2,1)}, u32[]{:S(2)}) copy-start(bf16[256,1024]{1,0:T(8,128)(2,1)} %refs_8_.1) | copy-start | bytes 1572868
  35.5 1.0 %copy-start.7 = (bf16[256,1024]{1,0:T(8,128)(2,1)S(1)}, bf16[256,1024]{1,0:T(8,128)(2,1)}, u32[]{:S(2)}) copy-start(bf16[256,1024]{1,0:T(8,128)(2,1)} %refs_10_.1) | copy-start | bytes 1572868
  36.5 1.0 %copy-start.9 = (bf16[1024,256]{1,0:T(8,128)(2,1)S(1)}, bf16[1024,256]{1,0:T(8,128)(2,1)}, u32[]{:S(2)}) copy-start(bf16[1024,256]{1,0:T(8,128)(2,1)} %refs_12_.1) | copy-start | bytes 1572868
  41.8 1.0 %copy-start = (bf16[256,2048]{1,0:T(8,128)(2,1)}, bf16[256,2048]{1,0:T(8,128)(2,1)S(1)}, u32[]{:S(2)}) copy-start(bf16[256,2048]{1,0:T(8,128)(2,1)S(1)} %get-tuple-element.34.refs_6_) | copy-start | bytes 3145732
  42.8 13.9 %copy-start.11 = (bf16[256,128]{1,0:T(8,128)(2,1)S(1)}, bf16[256,128]{1,0:T(8,128)(2,1)}, u32[]{:S(2)}) copy-start(bf16[256,128]{1,0:T(8,128)(2,1)} %cot_ref.1) | copy-start | bytes 196612
  42.8 5.6 %collective-permute-start.10 = (bf16[256,256]{1,0:T(8,128)(2,1)}, bf16[256,256]{1,0:T(8,128)(2,1)S(1)}, u32[]{:S(2)}, u32[]{:S(2)}) collective-permute-start(bf16[256,256]{1,0:T(8,128)(2,1)} %get-tuple-element.25.refs_0_), channel_id=1, source_target_pairs={{0,2},{2,0},{4,6},{6,4},{8,10},{10,8},{12,14},{14,12},{16,18},{18,... | collective-permute-start | bytes 393224 | tf_op jit(solution)/shard_map/ppermute | solution.py:332
  44.3 7.5 %collective-permute-start.11 = (bf16[256,256]{1,0:T(8,128)(2,1)}, bf16[256,256]{1,0:T(8,128)(2,1)}, u32[]{:S(2)}, u32[]{:S(2)}) collective-permute-start(bf16[256,256]{1,0:T(8,128)(2,1)} %get-tuple-element.25.refs_0_), channel_id=1, source_target_pairs={{0,4},{2,6},{4,0},{6,2},{8,12},{10,14},{12,8},{14,10},{16,20},{18,... | collective-permute-start | bytes 393224 | tf_op jit(solution)/shard_map/ppermute | solution.py:332
  49.1 6.2 %collective-permute-start.12 = (bf16[256,256]{1,0:T(8,128)(2,1)}, bf16[256,256]{1,0:T(8,128)(2,1)}, u32[]{:S(2)}, u32[]{:S(2)}) collective-permute-start(bf16[256,256]{1,0:T(8,128)(2,1)} %get-tuple-element.25.refs_0_), channel_id=1, source_target_pairs={{0,6},{2,4},{4,2},{6,0},{8,14},{10,12},{12,10},{14,8},{16,22},{18,... | collective-permute-start | bytes 393224 | tf_op jit(solution)/shard_map/ppermute | solution.py:332
  51.5 3.7 %copy-start.15 = (bf16[256,256]{1,0:T(8,128)(2,1)S(1)}, bf16[256,256]{1,0:T(8,128)(2,1)}, u32[]{:S(2)}) copy-start(bf16[256,256]{1,0:T(8,128)(2,1)} %copy-done.14) | copy-start | bytes 393220
  51.5 6.6 %copy-start.2 = (bf16[1024,256]{1,0:T(8,128)(2,1)S(1)}, bf16[1024,256]{1,0:T(8,128)(2,1)}, u32[]{:S(2)}) copy-start(bf16[1024,256]{1,0:T(8,128)(2,1)} %down_a.1) | copy-start | bytes 1572868
  51.8 8.0 %copy-start.19 = (bf16[256,1024]{1,0:T(8,128)(2,1)S(1)}, bf16[256,1024]{1,0:T(8,128)(2,1)}, u32[]{:S(2)}) copy-start(bf16[256,1024]{1,0:T(8,128)(2,1)} %gate_a.1) | copy-start | bytes 1572868
  51.8 8.0 %copy-start.20 = (bf16[256,1024]{1,0:T(8,128)(2,1)S(1)}, bf16[256,1024]{1,0:T(8,128)(2,1)}, u32[]{:S(2)}) copy-start(bf16[256,1024]{1,0:T(8,128)(2,1)} %up_a.1) | copy-start | bytes 1572868
  51.8 8.0 %copy-start.23 = (f32[256]{0:T(256)S(1)}, f32[256]{0:T(256)}, u32[]{:S(2)}) copy-start(f32[256]{0:T(256)} %param.23) | copy-start | bytes 3076
  56.6 3.1 %collective-permute-start.13 = (f32[128,256]{1,0:T(8,128)S(1)}, f32[128,256]{1,0:T(8,128)S(1)}, u32[]{:S(2)}, u32[]{:S(2)}) collective-permute-start(f32[128,256]{1,0:T(8,128)S(1)} %get-tuple-element.27), channel_id=1, source_target_pairs={{0,1},{1,0},{2,3},{3,2},{4,5},{5,4},{6,7},{7,6},{8,9},{9,8},{10,11... | collective-permute-start | bytes 393224 | tf_op jit(solution)/shard_map/ppermute | solution.py:320
  56.7 1.4 %collective-permute-start.14 = (bf16[128,128]{1,0:T(8,128)(2,1)S(1)}, bf16[128,128]{1,0:T(8,128)(2,1)S(1)}, u32[]{:S(2)}, u32[]{:S(2)}) collective-permute-start(bf16[128,128]{1,0:T(8,128)(2,1)S(1)} %get-tuple-element.37), channel_id=1, source_target_pairs={{0,1},{1,0},{2,3},{3,2},{4,5},{5,4},{6,7},{7,6},{8,9},{9,8},{10,11... | collective-permute-start | bytes 98312 | tf_op jit(solution)/shard_map/ppermute | solution.py:320
  62.7 21.5 %copy-start.1 = (bf16[256,2048]{1,0:T(8,128)(2,1)S(1)}, bf16[256,2048]{1,0:T(8,128)(2,1)}, u32[]{:S(2)}) copy-start(bf16[256,2048]{1,0:T(8,128)(2,1)} %copy-done) | copy-start | bytes 3145732
  62.8 21.5 %copy-start.6 = (bf16[256,1024]{1,0:T(8,128)(2,1)S(1)}, bf16[256,1024]{1,0:T(8,128)(2,1)}, u32[]{:S(2)}) copy-start(bf16[256,1024]{1,0:T(8,128)(2,1)} %refs_8_.1) | copy-start | bytes 1572868
  62.8 21.5 %copy-start.8 = (bf16[256,1024]{1,0:T(8,128)(2,1)S(1)}, bf16[256,1024]{1,0:T(8,128)(2,1)}, u32[]{:S(2)}) copy-start(bf16[256,1024]{1,0:T(8,128)(2,1)} %refs_10_.1) | copy-start | bytes 1572868
  62.8 21.5 %copy-start.10 = (bf16[1024,256]{1,0:T(8,128)(2,1)S(1)}, bf16[1024,256]{1,0:T(8,128)(2,1)}, u32[]{:S(2)}) copy-start(bf16[1024,256]{1,0:T(8,128)(2,1)} %refs_12_.1) | copy-start | bytes 1572868
  62.8 21.5 %copy-start.18 = (f32[256]{0:T(256)S(1)}, f32[256]{0:T(256)}, u32[]{:S(2)}) copy-start(f32[256]{0:T(256)} %param.22) | copy-start | bytes 3076
  62.8 4.5 %collective-permute-start.18 = (bf16[128,256]{1,0:T(8,128)(2,1)S(1)}, bf16[128,256]{1,0:T(8,128)(2,1)S(1)}, u32[]{:S(2)}, u32[]{:S(2)}) collective-permute-start(bf16[128,256]{1,0:T(8,128)(2,1)S(1)} %item.1.refs_0_), channel_id=1, source_target_pairs={{0,8},{2,10},{4,12},{6,14},{8,0},{10,2},{12,4},{14,6},{16,24},{18,... | collective-permute-start | bytes 196616 | tf_op jit(solution)/shard_map/ppermute | solution.py:324
  64.2 8.1 %collective-permute-start.19 = (bf16[128,256]{1,0:T(8,128)(2,1)S(1)}, bf16[128,256]{1,0:T(8,128)(2,1)S(1)}, u32[]{:S(2)}, u32[]{:S(2)}) collective-permute-start(bf16[128,256]{1,0:T(8,128)(2,1)S(1)} %item.1.refs_0_), channel_id=1, source_target_pairs={{0,16},{2,18},{4,20},{6,22},{8,24},{10,26},{12,28},{14,30},{16,0},... | collective-permute-start | bytes 196616 | tf_op jit(solution)/shard_map/ppermute | solution.py:324
  65.9 6.4 %collective-permute-start.20 = (bf16[128,256]{1,0:T(8,128)(2,1)S(1)}, bf16[128,256]{1,0:T(8,128)(2,1)S(1)}, u32[]{:S(2)}, u32[]{:S(2)}) collective-permute-start(bf16[128,256]{1,0:T(8,128)(2,1)S(1)} %item.1.refs_0_), channel_id=1, source_target_pairs={{0,24},{2,26},{4,28},{6,30},{8,16},{10,18},{12,20},{14,22},{16,8},... | collective-permute-start | bytes 196616 | tf_op jit(solution)/shard_map/ppermute | solution.py:324
  72.3 1.6 %collective-permute-start.21 = (bf16[512,256]{1,0:T(8,128)(2,1)S(1)}, bf16[512,256]{1,0:T(8,128)(2,1)S(1)}, u32[]{:S(2)}, u32[]{:S(2)}) collective-permute-start(bf16[512,256]{1,0:T(8,128)(2,1)S(1)} %pad_maximum_fusion.1), channel_id=1, source_target_pairs={{0,1},{1,0},{2,3},{3,2},{4,5},{5,4},{6,7},{7,6},{8,9},{9,8},{10,11... | collective-permute-start | bytes 786440 | tf_op jit(solution)/shard_map/ppermute | solution.py:320
  74.6 6.0 %collective-permute-start.22 = (bf16[256,256]{1,0:T(8,128)(2,1)S(1)}, bf16[256,256]{1,0:T(8,128)(2,1)S(1)}, u32[]{:S(2)}, u32[]{:S(2)}) collective-permute-start(bf16[256,256]{1,0:T(8,128)(2,1)S(1)} %get-tuple-element.29), channel_id=1, source_target_pairs={{0,2},{2,0},{4,6},{6,4},{8,10},{10,8},{12,14},{14,12},{16,18},{18,... | collective-permute-start | bytes 393224 | tf_op jit(solution)/shard_map/ppermute | solution.py:332
  76.2 8.1 %collective-permute-start.23 = (bf16[256,256]{1,0:T(8,128)(2,1)S(1)}, bf16[256,256]{1,0:T(8,128)(2,1)S(1)}, u32[]{:S(2)}, u32[]{:S(2)}) collective-permute-start(bf16[256,256]{1,0:T(8,128)(2,1)S(1)} %get-tuple-element.30), channel_id=1, source_target_pairs={{0,4},{2,6},{4,0},{6,2},{8,12},{10,14},{12,8},{14,10},{16,20},{18,... | collective-permute-start | bytes 393224 | tf_op jit(solution)/shard_map/ppermute | solution.py:332
  77.7 6.6 %collective-permute-start.24 = (bf16[256,256]{1,0:T(8,128)(2,1)S(1)}, bf16[256,256]{1,0:T(8,128)(2,1)S(1)}, u32[]{:S(2)}, u32[]{:S(2)}) collective-permute-start(bf16[256,256]{1,0:T(8,128)(2,1)S(1)} %get-tuple-element.31), channel_id=1, source_target_pairs={{0,6},{2,4},{4,2},{6,0},{8,14},{10,12},{12,10},{14,8},{16,22},{18,... | collective-permute-start | bytes 393224 | tf_op jit(solution)/shard_map/ppermute | solution.py:332
  84.3 13.4 %copy-start.4 = (f32[256,128]{1,0:T(8,128)S(1)}, f32[256,128]{1,0:T(8,128)}, u32[]{:S(2)}) copy-start(f32[256,128]{1,0:T(8,128)} %rows_ref.3) | copy-start | bytes 393220
  84.3 13.4 %copy-start.12 = (f32[256,128]{1,0:T(8,128)S(1)}, f32[256,128]{1,0:T(8,128)}, u32[]{:S(2)}) copy-start(f32[256,128]{1,0:T(8,128)} %first_ref.1) | copy-start | bytes 393220
  84.3 13.4 %copy-start.13 = (f32[256,128]{1,0:T(8,128)S(1)}, f32[256,128]{1,0:T(8,128)}, u32[]{:S(2)}) copy-start(f32[256,128]{1,0:T(8,128)} %second_ref.1) | copy-start | bytes 393220
  87.5 6.0 %collective-permute-start.25 = (bf16[256,256]{1,0:T(8,128)(2,1)S(1)}, bf16[256,256]{1,0:T(8,128)(2,1)S(1)}, u32[]{:S(2)}, u32[]{:S(2)}) collective-permute-start(bf16[256,256]{1,0:T(8,128)(2,1)S(1)} %basket_back.1.refs_0_), channel_id=1, source_target_pairs={{0,2},{2,0},{4,6},{6,4},{8,10},{10,8},{12,14},{14,12},{16,18},{18,... | collective-permute-start | bytes 393224 | tf_op jit(solution)/shard_map/ppermute | solution.py:332
  88.8 7.2 %collective-permute-start.26 = (bf16[256,256]{1,0:T(8,128)(2,1)S(1)}, bf16[256,256]{1,0:T(8,128)(2,1)S(1)}, u32[]{:S(2)}, u32[]{:S(2)}) collective-permute-start(bf16[256,256]{1,0:T(8,128)(2,1)S(1)} %basket_back.1.refs_0_), channel_id=1, source_target_pairs={{0,4},{2,6},{4,0},{6,2},{8,12},{10,14},{12,8},{14,10},{16,20},{18,... | collective-permute-start | bytes 393224 | tf_op jit(solution)/shard_map/ppermute | solution.py:332
  89.6 6.4 %collective-permute-start.27 = (bf16[256,256]{1,0:T(8,128)(2,1)S(1)}, bf16[256,256]{1,0:T(8,128)(2,1)S(1)}, u32[]{:S(2)}, u32[]{:S(2)}) collective-permute-start(bf16[256,256]{1,0:T(8,128)(2,1)S(1)} %basket_back.1.refs_0_), channel_id=1, source_target_pairs={{0,6},{2,4},{4,2},{6,0},{8,14},{10,12},{12,10},{14,8},{16,22},{18,... | collective-permute-start | bytes 393224 | tf_op jit(solution)/shard_map/ppermute | solution.py:332
  96.3 1.4 %collective-permute-start.28 = (f32[256,128]{1,0:T(8,128)S(1)}, f32[256,128]{1,0:T(8,128)S(1)}, u32[]{:S(2)}, u32[]{:S(2)}) collective-permute-start(f32[256,128]{1,0:T(8,128)S(1)} %get-tuple-element.36), channel_id=1, source_target_pairs={{0,1},{1,0},{2,3},{3,2},{4,5},{5,4},{6,7},{7,6},{8,9},{9,8},{10,11... | collective-permute-start | bytes 393224 | tf_op jit(solution)/shard_map/ppermute | solution.py:320
  (5 other events, 3.8 us)
where the time goes:
time: 99.1 us; the launch traced here: 98.6 us
  waiting for transfers between devices  39.6 us (40%)
  starting transfers between devices  30.2 us (30%)
  Pallas kernels  16.9 us (17%)
  local copies, waits for them, and re-layouts  9.23 us (9%)
  other arithmetic  1.54 us (2%)
  between operations  1.11 us (1%)
    ppermute x12, waiting for transfers between devices, exchange(): lax.ppermute(xs[k - 1], 'shard', [(s, s // groups * groups + (s % groups...  23 us
    ppermute x12, starting transfers between devices, exchange(): lax.ppermute(xs[k - 1], 'shard', [(s, s // groups * groups + (s % groups...  18.1 us
    pallas_call x11, Pallas kernels, run(): pl.pallas_call(body, out_shape=outs, in_specs=specs, out_specs=jax.tree.m...  16.9 us
    ppermute x6, waiting for transfers between devices, gather(): lax.ppermute(x, 'shard', [(s, (s // groups ^ k) * groups + s % groups) fo...  11.7 us
    ppermute x6, starting transfers between devices, gather(): lax.ppermute(x, 'shard', [(s, (s // groups ^ k) * groups + s % groups) fo...  10.2 us
    unnamed x48, local copies, waits for them, and re-layouts  8.95 us
    ppermute x11, waiting for transfers between devices, swap(): return lax.ppermute(x, 'mp', [(0, 1), (1, 0)])  4.85 us
  transfers between devices with their start and end apart: 29, of which 15 were waited for; matrix products, arithmetic and copies ran while one was open for 1% of the time, Pallas kernels for 9%

commit v1 on v0

--- a/solution.py
+++ b/solution.py
@@ -59,16 +59,39 @@
     return 0.5 * jnp.tanh(0.5 * v) + 0.5
 
 
-def pack_body(core_ref, rows_ref, words_ref, meta_ref, pack_ref, lo_ref, hi_ref, *, half):
+def pack_body(
+    dest_ref, item_ref, rows_ref, words_ref, cot_ref, pack_ref, send_ref, lo_ref, hi_ref, *, half, members, groups
+):
     items = rows_ref.shape[0]
-    start = pl.multiple_of(core_ref[0] * half, half)
+    tiles = dest_ref.shape[0]
+    core = lax.axis_index("mp")
+    place = lax.axis_index("shard") % groups
+    start = pl.multiple_of(core * half, half)
     pack_ref[0:items, :] = rows_ref[...].astype(BF16)
     words = words_ref[...]
     lo_ref[...] = (words & 255).astype(F32).T
     hi_ref[...] = (words >> 8).astype(F32).T
     pack_ref[items : items + half, :] = lo_ref[pl.ds(start, half), :].astype(BF16)
     pack_ref[items + half : items + 2 * half, :] = hi_ref[pl.ds(start, half), :].astype(BF16)
-    pack_ref[items + 2 * half :, :] = meta_ref[...]
+    lanes = lax.broadcasted_iota(jnp.int32, (16, pack_ref.shape[1]), 1)
+    meta = jnp.zeros_like(lanes)
+    for t in range(tiles):
+        dest = dest_ref[t]
+        slot = ((dest % groups) ^ place) * members + dest // groups
+        meta = jnp.where(lanes == t, slot, meta)
+        meta = jnp.where(lanes == tiles + t, item_ref[t], meta)
+    pack_ref[items + 2 * half :, :] = meta.astype(F32).astype(BF16)
+    rows = send_ref.shape[0]
+    send_ref[...] = cot_ref[pl.ds(pl.multiple_of((1 - core) * rows, rows), rows), :]
+
+
+def spread_body(pack_ref, out_ref):
+    source = lax.broadcasted_iota(jnp.int32, (out_ref.shape[0], 2 * BLOCK), 0)
+    words = out_ref.shape[0] // 2
+    for c in range(0, out_ref.shape[1], 2 * BLOCK):
+        target = lax.broadcasted_iota(jnp.int32, (out_ref.shape[0], 2 * BLOCK), 1) + c
+        hit = source == (target // 16) + words * ((target // 8) % 2)
+        out_ref[:, c : c + 2 * BLOCK] = jnp.where(hit, 1.0, 0.0).astype(BF16)
 
 
 def join_halves(core, whole_ref, own_ref_list, other_ref, rows):
@@ -88,7 +111,7 @@
     mt_ref = refs[members + 2]
     out_refs = refs[members + 3 : members + 3 + groups]
     rows_ref = refs[members + 3 + groups]
-    core = idx_ref[2 * members * tiles]
+    core = lax.axis_index("mp")
     mt_ref[...] = jnp.zeros_like(mt_ref)
     byte_rows = jnp.concatenate(
         [
@@ -106,9 +129,9 @@
         mask = bits.astype(F32).astype(BF16)
         for l in range(members):
             for b in range(2):
-                at = 2 * (l * tiles + 2 * q + b)
-                row = pl.multiple_of(idx_ref[at], half)
-                lane = pl.multiple_of(idx_ref[at + 1], BLOCK)
+                t = 2 * q + b
+                row = pl.multiple_of(idx_ref[l, t] * half, half)
+                lane = pl.multiple_of(idx_ref[l, tiles + t] * BLOCK + l * items, BLOCK)
                 where = (pl.ds(row, half), pl.ds(lane, BLOCK))
                 mt_ref[where] = (
                     mt_ref[where]
@@ -121,7 +144,20 @@
         out_refs[i][...] = total.astype(out_refs[i].dtype)
 
 
-def turn_body(mt_ref, out_ref, *, items):
+def turn_body(mt_ref, mine_ref, other_ref, down_a, down_b, out_ref, hid_ref, cot_ref, *, items):
+    core = lax.axis_index("mp")
+    width = mine_ref.shape[1]
+    rows = other_ref.shape[0]
+    cot_ref[:, pl.ds(pl.multiple_of(core * width, width), width)] = mine_ref[
+        pl.ds(pl.multiple_of(core * rows, rows), rows), :
+    ]
+    cot_ref[:, pl.ds(pl.multiple_of((1 - core) * width, width), width)] = other_ref[...]
+    cot = cot_ref[...]
+    at = 0
+    for down in (down_a, down_b):
+        for c in range(0, down.shape[0], CHUNK):
+            hid_ref[:, at : at + CHUNK] = dot_nt(cot, down[c : c + CHUNK, :])
+            at += CHUNK
     for c in range(mt_ref.shape[0] // BLOCK):
         block = mt_ref[c * BLOCK : (c + 1) * BLOCK, 0:items].astype(F32)
         out_ref[:, c * BLOCK : (c + 1) * BLOCK] = block.T.astype(BF16)
@@ -136,12 +172,6 @@
 
 def rms(values):
     return lax.rsqrt(jnp.mean(values * values, axis=-1, keepdims=True) + NORM_EPSILON)
-
-
-def halves(own_ref, other_ref, axis):
-    for ref in (own_ref, other_ref):
-        for c in range(ref.shape[axis] // CHUNK):
-            yield ref, c * CHUNK
 
 
 def basket_body(*refs, groups):
@@ -167,7 +197,7 @@
     out_ref[...] = acc.astype(BF16)
 
 
-def message_body(core_ref, mo_ref, *refs, groups):
+def message_body(mo_ref, *refs, groups):
     parts = refs[:groups]
     mine_ref, theirs_ref, all_ref = refs[groups:]
     per = parts[0].shape[0]
@@ -176,22 +206,9 @@
         total = total + dot(mo_ref[:, i * per : (i + 1) * per], parts[i][...])
     all_ref[...] = total
     rows = mine_ref.shape[0]
-    core = core_ref[0]
+    core = lax.axis_index("mp")
     mine_ref[...] = all_ref[pl.ds(pl.multiple_of(core * rows, rows), rows), :]
     theirs_ref[...] = all_ref[pl.ds(pl.multiple_of((1 - core) * rows, rows), rows), :]
-
-
-def item_hidden_body(core_ref, mine_ref, other_ref, down_a, down_b, out_ref, cot_ref):
-    core = core_ref[0]
-    width = mine_ref.shape[1]
-    cot_ref[:, pl.ds(pl.multiple_of(core * width, width), width)] = mine_ref[...]
-    cot_ref[:, pl.ds(pl.multiple_of((1 - core) * width, width), width)] = other_ref[...]
-    cot = cot_ref[...]
-    at = 0
-    for down in (down_a, down_b):
-        for c in range(0, down.shape[0], CHUNK):
-            out_ref[:, at : at + CHUNK] = dot_nt(cot, down[c : c + CHUNK, :])
-            at += CHUNK
 
 
 def item_body(mine_ref, other_ref, hidden_ref, gain_ref, gate_a, gate_b, up_a, up_b, out_ref):
@@ -220,12 +237,12 @@
     out_ref[...] = (scale * weighted - message * (cubed * inner)).astype(BF16)
 
 
-def grad_sums_body(core_ref, mt_ref, *refs, members, groups):
+def grad_sums_body(mt_ref, *refs, members, groups):
     owns = refs[:members]
     other_ref = refs[members]
     out_refs = refs[members + 1 : members + 1 + groups]
     rows_ref = refs[members + 1 + groups]
-    core = core_ref[0]
+    core = lax.axis_index("mp")
     rows = owns[0].shape[0]
     for l in range(members):
         mine = pl.multiple_of((2 * l + core) * rows, rows)
@@ -262,7 +279,7 @@
     out_ref[...] = (scale * weighted - total * (cubed * inner)).astype(BF16)
 
 
-def back_body(core_ref, mo_ref, *refs, groups):
+def back_body(mo_ref, *refs, groups):
     parts = refs[:groups]
     mine_ref, theirs_ref, all_ref = refs[groups:]
     per = parts[0].shape[0]
@@ -271,7 +288,7 @@
         total = total + dot(mo_ref[:, i * per : (i + 1) * per], parts[i][...])
     all_ref[...] = total
     width = mine_ref.shape[1]
-    core = core_ref[0]
+    core = lax.axis_index("mp")
     mine_ref[...] = all_ref[:, pl.ds(pl.multiple_of(core * width, width), width)]
     theirs_ref[...] = all_ref[:, pl.ds(pl.multiple_of((1 - core) * width, width), width)]
 
@@ -312,10 +329,6 @@
     item_half = items // 2
     hidden = 2 * gate_basket.shape[1]
     per = members * half
-    core = lax.axis_index("mp")
-    place = lax.axis_index("shard") % groups
-    core_arr = core.astype(jnp.int32).reshape(1)
-
     def swap(x):
         return lax.ppermute(x, "mp", [(0, 1), (1, 0)])
 
@@ -337,36 +350,30 @@
             for k in range(1, groups)
         ]
 
-    meta = jnp.stack([tile_dest % 128, tile_dest // 128, tile_item]).astype(BF16)
-    meta = jnp.pad(meta, ((0, 13), (0, width - tiles)))
-    pack = run(
-        functools.partial(pack_body, half=half),
-        sds((items + 2 * half + 16, width), BF16),
-        (core_arr,),
-        (item_rows, tile_bits.reshape(tiles * words, BLOCK), meta),
+    pack, cot_send = run(
+        functools.partial(pack_body, half=half, members=members, groups=groups),
+        [sds((items + 2 * half + 16, width), BF16), sds((item_half, width), BF16)],
+        (tile_dest, tile_item),
+        (item_rows, tile_bits.reshape(tiles * words, BLOCK), item_cot),
         scratch=[pltpu.VMEM((BLOCK, tiles * words), F32)] * 2,
         name="pack",
     )
     packs = [pack] + gather(pack)
-    rows_other = swap(jnp.concatenate([q[:items] for q in packs], axis=0))
-    cot_other = swap(lax.dynamic_slice_in_dim(item_cot, (1 - core) * item_half, item_half, 0))
-    cot_mine = lax.dynamic_slice_in_dim(item_cot, core * item_half, item_half, 0)
+    spread = run(
+        spread_body,
+        sds((2 * tiles * words, tiles * BLOCK), BF16),
+        (),
+        (pack,),
+        flops=1 << 29,
+        name="spread",
+    )
+    cot_other = swap(cot_send)
     gate_b, up_b, down_b = gate_basket, up_basket, down_basket
     gate_bo, up_bo, down_bo = swap(gate_basket), swap(up_basket), swap(down_basket)
     gate_io, up_io, down_io = swap(gate_item), swap(up_item), swap(down_item)
-
-    metas = jnp.stack([q[items + 2 * half : items + 2 * half + 3, :tiles] for q in packs])
-    metas = metas.astype(jnp.int32)
-    dest = metas[:, 0] + 128 * metas[:, 1]
-    row_at = (((dest % groups) ^ place) * members + dest // groups) * half
-    lane_at = metas[:, 2] * BLOCK + items * jnp.arange(members, dtype=jnp.int32)[:, None]
-    idx = jnp.concatenate([jnp.stack([row_at, lane_at], axis=-1).reshape(-1), core_arr])
-
-    source = lax.broadcasted_iota(jnp.int32, (2 * tiles * words, tiles * BLOCK), 0)
-    target = lax.broadcasted_iota(jnp.int32, (2 * tiles * words, tiles * BLOCK), 1)
-    spread = (
-        (source % (tiles * words) == target // 16) & (source // (tiles * words) == (target // 8) % 2)
-    ).astype(BF16)
+    rows_other = swap(jnp.concatenate([q[:items] for q in packs], axis=0))
+    metas = [q[items + 2 * half : items + 2 * half + 1] for q in packs]
+    idx = jnp.concatenate(metas, axis=0).astype(jnp.int32)
 
     part_shapes = [sds((per, features), F32)] + [sds((per, features), BF16)] * (groups - 1)
     mt, *parts = run(
@@ -381,22 +388,14 @@
         name="sums",
     )
     received = exchange(parts[1:])
-    mo = run(
+    mo, item_hidden = run(
         functools.partial(turn_body, items=items),
-        sds((items, shards * half), BF16),
-        (),
-        (mt,),
+        [sds((items, shards * half), BF16), sds((item_half, hidden), F32)],
+        (),
+        (mt, item_cot, cot_other, down_item, down_io),
+        scratch=[pltpu.VMEM((item_half, features), BF16)],
         flops=1 << 29,
         name="turn",
-    )
-    item_hidden = run(
-        item_hidden_body,
-        sds((item_half, hidden), F32),
-        (core_arr,),
-        (cot_mine, cot_other, down_item, down_io),
-        scratch=[pltpu.VMEM((item_half, features), BF16)],
-        flops=1 << 29,
-        name="item_hidden",
     )
     basket_out, basket_sum, value, slope = run(
         functools.partial(basket_body, groups=groups),
@@ -425,7 +424,7 @@
     message_mine, message_theirs = run(
         functools.partial(message_body, groups=groups),
         [sds((item_half, features), F32)] * 2,
-        (core_arr,),
+        (),
         (mo, *outs),
         scratch=[pltpu.VMEM((items, features), F32)],
         flops=1 << 28,
@@ -454,7 +453,7 @@
     grad_parts = run(
         functools.partial(grad_sums_body, members=members, groups=groups),
         part_shapes,
-        (core_arr,),
+        (),
         (mt, *grads, grads_other),
         scratch=[pltpu.VMEM((members * items, features), BF16)],
         flops=1 << 29,
@@ -486,7 +485,7 @@
     back_mine, back_theirs = run(
         functools.partial(back_body, groups=groups),
         [sds((items, width), F32)] * 2,
-        (core_arr,),
+        (),
         (mo, *sums),
         scratch=[pltpu.VMEM((items, features), F32)],
         flops=1 << 28,

time: 99.1 us -> 89.8 us (0.906)
  Pallas kernels: 16.9 us -> 10.9 us
  waiting for transfers between devices: 39.6 us -> 45.4 us
  local copies, waits for them, and re-layouts: 9.23 us -> 3.98 us
  starting transfers between devices: 30.2 us -> 28.3 us
  other arithmetic: 1.54 us -> 0.05 us
    pallas_call x11, Pallas kernels: 16.9 us -> 10.9 us  [run(): pl.pallas_call(body, out_shape=outs, in_specs=specs, out_specs=jax.tree.m...]
    unnamed x48 -> x34, local copies, waits for them, and re-layouts: 8.95 us -> 3.95 us
    ppermute x12, waiting for transfers between devices: 23 us -> 26.9 us  [exchange(): lax.ppermute(xs[k - 1], 'shard', [(s, s // groups * groups + (s % groups...]
    ppermute x12, starting transfers between devices: 18.1 us -> 16.2 us  [exchange(): lax.ppermute(xs[k - 1], 'shard', [(s, s // groups * groups + (s % groups...]
    ppermute x6, waiting for transfers between devices: 11.7 us -> 13.6 us  [gather(): lax.ppermute(x, 'shard', [(s, (s // groups ^ k) * groups + s % groups) fo...]
  transfers between devices with their start and end apart: 29 -> 29, of which waited for: 15 -> 17; matrix products, arithmetic and copies ran while one was open for 1% -> 0% of each run, Pallas kernels for 9% -> 5%
where the time goes in v1:
time: 89.8 us; the launch traced here: 89.6 us
  waiting for transfers between devices  45.4 us (51%)
  starting transfers between devices  28.3 us (32%)
  Pallas kernels  10.9 us (12%)
  local copies, waits for them, and re-layouts  3.98 us (4%)
  between operations  0.92 us (1%)
    ppermute x12, waiting for transfers between devices, exchange(): lax.ppermute(xs[k - 1], 'shard', [(s, s // groups * groups + (s % groups...  26.9 us
    ppermute x12, starting transfers between devices, exchange(): lax.ppermute(xs[k - 1], 'shard', [(s, s // groups * groups + (s % groups...  16.2 us
    ppermute x6, waiting for transfers between devices, gather(): lax.ppermute(x, 'shard', [(s, (s // groups ^ k) * groups + s % groups) fo...  13.6 us
    pallas_call x11, Pallas kernels, run(): pl.pallas_call(body, out_shape=outs, in_specs=specs, out_specs=jax.tree.m...  10.9 us
    ppermute x6, starting transfers between devices, gather(): lax.ppermute(x, 'shard', [(s, (s // groups ^ k) * groups + s % groups) fo...  10.2 us
    ppermute x11, waiting for transfers between devices, swap(): return lax.ppermute(x, 'mp', [(0, 1), (1, 0)])  4.87 us
    unnamed x34, local copies, waits for them, and re-layouts  3.95 us
    ppermute x11, starting transfers between devices, swap(): return lax.ppermute(x, 'mp', [(0, 1), (1, 0)])  1.94 us
  transfers between devices with their start and end apart: 29, of which 17 were waited for; matrix products, arithmetic and copies ran while one was open for 0% of the time, Pallas kernels for 5%

profile of v1, /device:TPU:0, one launch (start us, length us, event | category | flops | bytes accessed | tf_op | source)
XLA Modules:
  0.0 89.6 jit_solution(14398995359401155332)
XLA Ops:
  0.6 0.8 copy-done
  1.5 0.9 %copy-done.3 = f32[256,128]{1,0:T(8,128)S(1)} copy-done((f32[256,128]{1,0:T(8,128)S(1)}, f32[256,128]{1,0:T(8,128)}, u32[]{:S(2)}) %copy-start.3) | copy-done | bytes 131096
  2.4 0.8 copy-done.10
  3.2 0.7 copy-done.12
  3.9 0.7 copy-done.13
  4.5 0.7 pack.1
  5.2 3.1 %collective-permute-start = (bf16[400,128]{1,0:T(8,128)(2,1)S(1)}, bf16[400,128]{1,0:T(8,128)(2,1)S(1)}, u32[]{:S(2)}, u32[]{:S(2)}) collective-permute-start(bf16[400,128]{1,0:T(8,128)(2,1)S(1)} %get-tuple-element.24.pack_ref.refs_0_), channel_id=1, source_target_pairs={{0,8},{2,10},{4,12},{6,14},{8,0},{10,2},{12,4},{14,6},{16,24},{18,... | collective-permute-start | bytes 307208 | tf_op jit(solution)/shard_map/ppermute | solution.py:337
  8.3 2.6 %collective-permute-start.1 = (bf16[400,128]{1,0:T(8,128)(2,1)S(1)}, bf16[400,128]{1,0:T(8,128)(2,1)S(1)}, u32[]{:S(2)}, u32[]{:S(2)}) collective-permute-start(bf16[400,128]{1,0:T(8,128)(2,1)S(1)} %get-tuple-element.24.pack_ref.refs_0_), channel_id=1, source_target_pairs={{0,16},{2,18},{4,20},{6,22},{8,24},{10,26},{12,28},{14,30},{16,0},... | collective-permute-start | bytes 307208 | tf_op jit(solution)/shard_map/ppermute | solution.py:337
  11.2 7.8 %collective-permute-done.1.refs_2_ = bf16[400,128]{1,0:T(8,128)(2,1)S(1)} collective-permute-done((bf16[400,128]{1,0:T(8,128)(2,1)S(1)}, bf16[400,128]{1,0:T(8,128)(2,1)S(1)}, u32[]{:S(2)}, u32[]{:S(2)}) %collective-permute-start.1) | collective-permute-done | bytes 102432 | tf_op jit(solution)/shard_map/ppermute | solution.py:337
  19.2 0.5 collective-permute-start.10
  20.0 0.7 collective-permute-done.3.refs_4_
  20.7 2.2 %sums.1 = (bf16[1024,1024]{1,0:T(8,128)(2,1)S(1)}, f32[256,256]{1,0:T(8,128)S(1)}, bf16[256,256]{1,0:T(8,128)(2,1)S(1)}, bf16[256,256]{1,0:T(8,128)(2,1)S(1)}, bf16[256,256]{1,0:T(8,128)(2,1)S(1)}) custom-call(s32[4,128]{1,0:T(4,128)S(1)} %maximum_convert_fusion.idx_ref, bf16[400,128]{1,0:T(8,128)(2,1)S(1)} %get-tuple-element.24.pack_ref.refs_0_, ...), custom_call_target="tpu_custom_call" | custom-call | flops 1073741824 | bytes 1048576 | tf_op jit(solution)/shard_map/sums/pallas_call | solution.py:38
  23.0 1.6 %collective-permute-start.6 = (bf16[256,256]{1,0:T(8,128)(2,1)S(1)}, bf16[256,256]{1,0:T(8,128)(2,1)S(1)}, u32[]{:S(2)}, u32[]{:S(2)}) collective-permute-start(bf16[256,256]{1,0:T(8,128)(2,1)S(1)} %get-tuple-element.29), channel_id=1, source_target_pairs={{0,2},{2,0},{4,6},{6,4},{8,10},{10,8},{12,14},{14,12},{16,18},{18,... | collective-permute-start | bytes 393224 | tf_op jit(solution)/shard_map/ppermute | solution.py:345
  24.5 0.5 collective-permute-start.9
  25.1 3.5 %collective-permute-done.6.refs_1_ = bf16[256,256]{1,0:T(8,128)(2,1)S(1)} collective-permute-done((bf16[256,256]{1,0:T(8,128)(2,1)S(1)}, bf16[256,256]{1,0:T(8,128)(2,1)S(1)}, u32[]{:S(2)}, u32[]{:S(2)}) %collective-permute-start.6) | collective-permute-done | bytes 131104 | tf_op jit(solution)/shard_map/ppermute | solution.py:345
  28.6 1.5 %collective-permute-start.7 = (bf16[256,256]{1,0:T(8,128)(2,1)S(1)}, bf16[256,256]{1,0:T(8,128)(2,1)S(1)}, u32[]{:S(2)}, u32[]{:S(2)}) collective-permute-start(bf16[256,256]{1,0:T(8,128)(2,1)S(1)} %get-tuple-element.30), channel_id=1, source_target_pairs={{0,4},{2,6},{4,0},{6,2},{8,12},{10,14},{12,8},{14,10},{16,20},{18,... | collective-permute-start | bytes 393224 | tf_op jit(solution)/shard_map/ppermute | solution.py:345
  30.1 3.5 %collective-permute-done.7.refs_2_ = bf16[256,256]{1,0:T(8,128)(2,1)S(1)} collective-permute-done((bf16[256,256]{1,0:T(8,128)(2,1)S(1)}, bf16[256,256]{1,0:T(8,128)(2,1)S(1)}, u32[]{:S(2)}, u32[]{:S(2)}) %collective-permute-start.7) | collective-permute-done | bytes 131104 | tf_op jit(solution)/shard_map/ppermute | solution.py:345
  33.5 2.4 %collective-permute-start.8 = (bf16[256,256]{1,0:T(8,128)(2,1)S(1)}, bf16[256,256]{1,0:T(8,128)(2,1)S(1)}, u32[]{:S(2)}, u32[]{:S(2)}) collective-permute-start(bf16[256,256]{1,0:T(8,128)(2,1)S(1)} %get-tuple-element.31), channel_id=1, source_target_pairs={{0,6},{2,4},{4,2},{6,0},{8,14},{10,12},{12,10},{14,8},{16,22},{18,... | collective-permute-start | bytes 393224 | tf_op jit(solution)/shard_map/ppermute | solution.py:345
  36.0 3.4 %collective-permute-done.8.refs_3_ = bf16[256,256]{1,0:T(8,128)(2,1)S(1)} collective-permute-done((bf16[256,256]{1,0:T(8,128)(2,1)S(1)}, bf16[256,256]{1,0:T(8,128)(2,1)S(1)}, u32[]{:S(2)}, u32[]{:S(2)}) %collective-permute-start.8) | collective-permute-done | bytes 131104 | tf_op jit(solution)/shard_map/ppermute | solution.py:345
  39.4 0.5 collective-permute-start.17
  40.0 1.5 %basket.1 = (bf16[256,256]{1,0:T(8,128)(2,1)S(1)}, f32[256,256]{1,0:T(8,128)S(1)}, bf16[256,2048]{1,0:T(8,128)(2,1)S(1)}, bf16[256,2048]{1,0:T(8,128)(2,1)S(1)}) custom-call(f32[256,256]{1,0:T(8,128)S(1)} %get-tuple-element.28.refs_0_, bf16[256,256]{1,0:T(8,128)(2,1)S(1)} %collective-permute-done.6.refs_1_, ...), custom_call_target="tpu_custom_call" | custom-call | flops 1073741824 | bytes 1048576 | tf_op jit(solution)/shard_map/basket/pallas_call | solution.py:38
  41.6 1.6 %collective-permute-start.12 = (bf16[256,256]{1,0:T(8,128)(2,1)S(1)}, bf16[256,256]{1,0:T(8,128)(2,1)S(1)}, u32[]{:S(2)}, u32[]{:S(2)}) collective-permute-start(bf16[256,256]{1,0:T(8,128)(2,1)S(1)} %get-tuple-element.32.refs_0_), channel_id=1, source_target_pairs={{0,2},{2,0},{4,6},{6,4},{8,10},{10,8},{12,14},{14,12},{16,18},{18,... | collective-permute-start | bytes 393224 | tf_op jit(solution)/shard_map/ppermute | solution.py:345
  43.1 1.5 %collective-permute-start.13 = (bf16[256,256]{1,0:T(8,128)(2,1)S(1)}, bf16[256,256]{1,0:T(8,128)(2,1)S(1)}, u32[]{:S(2)}, u32[]{:S(2)}) collective-permute-start(bf16[256,256]{1,0:T(8,128)(2,1)S(1)} %get-tuple-element.32.refs_0_), channel_id=1, source_target_pairs={{0,4},{2,6},{4,0},{6,2},{8,12},{10,14},{12,8},{14,10},{16,20},{18,... | collective-permute-start | bytes 393224 | tf_op jit(solution)/shard_map/ppermute | solution.py:345
  44.6 0.5 collective-permute-start.14
  45.6 2.3 %collective-permute-done.12.refs_1_ = bf16[256,256]{1,0:T(8,128)(2,1)S(1)} collective-permute-done((bf16[256,256]{1,0:T(8,128)(2,1)S(1)}, bf16[256,256]{1,0:T(8,128)(2,1)S(1)}, u32[]{:S(2)}, u32[]{:S(2)}) %collective-permute-start.12) | collective-permute-done | bytes 131104 | tf_op jit(solution)/shard_map/ppermute | solution.py:345
  47.9 3.6 %collective-permute-done.13.refs_2_ = bf16[256,256]{1,0:T(8,128)(2,1)S(1)} collective-permute-done((bf16[256,256]{1,0:T(8,128)(2,1)S(1)}, bf16[256,256]{1,0:T(8,128)(2,1)S(1)}, u32[]{:S(2)}, u32[]{:S(2)}) %collective-permute-start.13) | collective-permute-done | bytes 131104 | tf_op jit(solution)/shard_map/ppermute | solution.py:345
  51.9 1.3 %collective-permute-done.15.other_ref = f32[128,256]{1,0:T(8,128)S(1)} collective-permute-done((f32[128,256]{1,0:T(8,128)S(1)}, f32[128,256]{1,0:T(8,128)S(1)}, u32[]{:S(2)}, u32[]{:S(2)}) %collective-permute-start.15) | collective-permute-done | bytes 131104 | tf_op jit(solution)/shard_map/ppermute | solution.py:333
  53.3 1.8 %item.1.refs_0_ = bf16[128,256]{1,0:T(8,128)(2,1)S(1)} custom-call(f32[128,256]{1,0:T(8,128)S(1)} %get-tuple-element.33.mine_ref, f32[128,256]{1,0:T(8,128)S(1)} %collective-permute-done.15.other_ref, f32[128,2048]{1,0:T(8,128)S(1)} %get-tuple-element.35.hidden_ref, f32[1,256]{1,0:T(1,128)S(1)} %bitcast.6, bf16[256,1024]{1,0:T(8,128)(2,1)S(1)} %copy-done.14, ...), custom_call_target="tpu_custom_call" | custom-call | flops 1073741824 | bytes 1048576 | tf_op jit(solution)/shard_map/item/pallas_call | solution.py:38
  55.1 1.7 %collective-permute-start.18 = (bf16[128,256]{1,0:T(8,128)(2,1)S(1)}, bf16[128,256]{1,0:T(8,128)(2,1)S(1)}, u32[]{:S(2)}, u32[]{:S(2)}) collective-permute-start(bf16[128,256]{1,0:T(8,128)(2,1)S(1)} %item.1.refs_0_), channel_id=1, source_target_pairs={{0,8},{2,10},{4,12},{6,14},{8,0},{10,2},{12,4},{14,6},{16,24},{18,... | collective-permute-start | bytes 196616 | tf_op jit(solution)/shard_map/ppermute | solution.py:337
  56.8 1.4 %collective-permute-start.19 = (bf16[128,256]{1,0:T(8,128)(2,1)S(1)}, bf16[128,256]{1,0:T(8,128)(2,1)S(1)}, u32[]{:S(2)}, u32[]{:S(2)}) collective-permute-start(bf16[128,256]{1,0:T(8,128)(2,1)S(1)} %item.1.refs_0_), channel_id=1, source_target_pairs={{0,16},{2,18},{4,20},{6,22},{8,24},{10,26},{12,28},{14,30},{16,0},... | collective-permute-start | bytes 196616 | tf_op jit(solution)/shard_map/ppermute | solution.py:337
  58.2 1.3 %collective-permute-start.20 = (bf16[128,256]{1,0:T(8,128)(2,1)S(1)}, bf16[128,256]{1,0:T(8,128)(2,1)S(1)}, u32[]{:S(2)}, u32[]{:S(2)}) collective-permute-start(bf16[128,256]{1,0:T(8,128)(2,1)S(1)} %item.1.refs_0_), channel_id=1, source_target_pairs={{0,24},{2,26},{4,28},{6,30},{8,16},{10,18},{12,20},{14,22},{16,8},... | collective-permute-start | bytes 196616 | tf_op jit(solution)/shard_map/ppermute | solution.py:337
  59.5 5.5 %collective-permute-done.19.refs_2_ = bf16[128,256]{1,0:T(8,128)(2,1)S(1)} collective-permute-done((bf16[128,256]{1,0:T(8,128)(2,1)S(1)}, bf16[128,256]{1,0:T(8,128)(2,1)S(1)}, u32[]{:S(2)}, u32[]{:S(2)}) %collective-permute-start.19) | collective-permute-done | bytes 65568 | tf_op jit(solution)/shard_map/ppermute | solution.py:337
  65.1 1.5 %collective-permute-done.21.refs_4_ = bf16[512,256]{1,0:T(8,128)(2,1)S(1)} collective-permute-done((bf16[512,256]{1,0:T(8,128)(2,1)S(1)}, bf16[512,256]{1,0:T(8,128)(2,1)S(1)}, u32[]{:S(2)}, u32[]{:S(2)}) %collective-permute-start.21) | collective-permute-done | bytes 262176 | tf_op jit(solution)/shard_map/ppermute | solution.py:333
  66.6 0.7 grad_sums.1
  67.4 1.3 %collective-permute-start.22 = (bf16[256,256]{1,0:T(8,128)(2,1)S(1)}, bf16[256,256]{1,0:T(8,128)(2,1)S(1)}, u32[]{:S(2)}, u32[]{:S(2)}) collective-permute-start(bf16[256,256]{1,0:T(8,128)(2,1)S(1)} %get-tuple-element.37), channel_id=1, source_target_pairs={{0,2},{2,0},{4,6},{6,4},{8,10},{10,8},{12,14},{14,12},{16,18},{18,... | collective-permute-start | bytes 393224 | tf_op jit(solution)/shard_map/ppermute | solution.py:345
  68.7 0.8 collective-permute-start.23
  69.5 1.4 %collective-permute-start.24 = (bf16[256,256]{1,0:T(8,128)(2,1)S(1)}, bf16[256,256]{1,0:T(8,128)(2,1)S(1)}, u32[]{:S(2)}, u32[]{:S(2)}) collective-permute-start(bf16[256,256]{1,0:T(8,128)(2,1)S(1)} %get-tuple-element.39), channel_id=1, source_target_pairs={{0,6},{2,4},{4,2},{6,0},{8,14},{10,12},{12,10},{14,8},{16,22},{18,... | collective-permute-start | bytes 393224 | tf_op jit(solution)/shard_map/ppermute | solution.py:345
  70.9 2.7 %collective-permute-done.22.refs_1_ = bf16[256,256]{1,0:T(8,128)(2,1)S(1)} collective-permute-done((bf16[256,256]{1,0:T(8,128)(2,1)S(1)}, bf16[256,256]{1,0:T(8,128)(2,1)S(1)}, u32[]{:S(2)}, u32[]{:S(2)}) %collective-permute-start.22) | collective-permute-done | bytes 131104 | tf_op jit(solution)/shard_map/ppermute | solution.py:345
  73.7 1.5 %collective-permute-done.23.refs_2_ = bf16[256,256]{1,0:T(8,128)(2,1)S(1)} collective-permute-done((bf16[256,256]{1,0:T(8,128)(2,1)S(1)}, bf16[256,256]{1,0:T(8,128)(2,1)S(1)}, u32[]{:S(2)}, u32[]{:S(2)}) %collective-permute-start.23) | collective-permute-done | bytes 131104 | tf_op jit(solution)/shard_map/ppermute | solution.py:345
  75.1 1.6 %collective-permute-done.24.refs_3_ = bf16[256,256]{1,0:T(8,128)(2,1)S(1)} collective-permute-done((bf16[256,256]{1,0:T(8,128)(2,1)S(1)}, bf16[256,256]{1,0:T(8,128)(2,1)S(1)}, u32[]{:S(2)}, u32[]{:S(2)}) %collective-permute-start.24) | collective-permute-done | bytes 131104 | tf_op jit(solution)/shard_map/ppermute | solution.py:345
  76.7 1.8 %basket_back.1.refs_0_ = bf16[256,256]{1,0:T(8,128)(2,1)S(1)} custom-call(f32[256,256]{1,0:T(8,128)S(1)} %get-tuple-element.36.refs_0_, bf16[256,256]{1,0:T(8,128)(2,1)S(1)} %collective-permute-done.22.refs_1_, bf16[256,256]{1,0:T(8,128)(2,1)S(1)} %collective-permute-done.23.refs_2_, bf16[256,256]{1,0:T(8,128)(2,1)S(1)} %collective-permute-done.24.refs_3_, ...), custom_call_target="tpu_custom_call" | custom-call | flops 1073741824 | bytes 1048576 | tf_op jit(solution)/shard_map/basket_back/pallas_call | solution.py:38
  78.5 0.9 collective-permute-start.25
  79.4 1.5 %collective-permute-start.26 = (bf16[256,256]{1,0:T(8,128)(2,1)S(1)}, bf16[256,256]{1,0:T(8,128)(2,1)S(1)}, u32[]{:S(2)}, u32[]{:S(2)}) collective-permute-start(bf16[256,256]{1,0:T(8,128)(2,1)S(1)} %basket_back.1.refs_0_), channel_id=1, source_target_pairs={{0,4},{2,6},{4,0},{6,2},{8,12},{10,14},{12,8},{14,10},{16,20},{18,... | collective-permute-start | bytes 393224 | tf_op jit(solution)/shard_map/ppermute | solution.py:345
  80.9 1.2 %collective-permute-start.27 = (bf16[256,256]{1,0:T(8,128)(2,1)S(1)}, bf16[256,256]{1,0:T(8,128)(2,1)S(1)}, u32[]{:S(2)}, u32[]{:S(2)}) collective-permute-start(bf16[256,256]{1,0:T(8,128)(2,1)S(1)} %basket_back.1.refs_0_), channel_id=1, source_target_pairs={{0,6},{2,4},{4,2},{6,0},{8,14},{10,12},{12,10},{14,8},{16,22},{18,... | collective-permute-start | bytes 393224 | tf_op jit(solution)/shard_map/ppermute | solution.py:345
  82.1 2.6 %collective-permute-done.25.refs_1_ = bf16[256,256]{1,0:T(8,128)(2,1)S(1)} collective-permute-done((bf16[256,256]{1,0:T(8,128)(2,1)S(1)}, bf16[256,256]{1,0:T(8,128)(2,1)S(1)}, u32[]{:S(2)}, u32[]{:S(2)}) %collective-permute-start.25) | collective-permute-done | bytes 131104 | tf_op jit(solution)/shard_map/ppermute | solution.py:345
  84.7 2.3 %collective-permute-done.26.refs_2_ = bf16[256,256]{1,0:T(8,128)(2,1)S(1)} collective-permute-done((bf16[256,256]{1,0:T(8,128)(2,1)S(1)}, bf16[256,256]{1,0:T(8,128)(2,1)S(1)}, u32[]{:S(2)}, u32[]{:S(2)}) %collective-permute-start.26) | collective-permute-done | bytes 131104 | tf_op jit(solution)/shard_map/ppermute | solution.py:345
  87.4 1.3 %collective-permute-done.28.other_ref = f32[256,128]{1,0:T(8,128)S(1)} collective-permute-done((f32[256,128]{1,0:T(8,128)S(1)}, f32[256,128]{1,0:T(8,128)S(1)}, u32[]{:S(2)}, u32[]{:S(2)}) %collective-permute-start.28) | collective-permute-done | bytes 131104 | tf_op jit(solution)/shard_map/ppermute | solution.py:333
  88.8 0.8 adam.1
  (66 shorter events, 2.3 us)
Async XLA Ops:
  0.6 0.8 copy-start
  1.5 0.9 %copy-start.3 = (f32[256,128]{1,0:T(8,128)S(1)}, f32[256,128]{1,0:T(8,128)}, u32[]{:S(2)}) copy-start(f32[256,128]{1,0:T(8,128)} %rows_ref.3) | copy-start | bytes 393220
  2.4 0.8 copy-start.10
  3.2 0.7 copy-start.12
  3.9 0.7 copy-start.13
  5.2 6.0 %collective-permute-start = (bf16[400,128]{1,0:T(8,128)(2,1)S(1)}, bf16[400,128]{1,0:T(8,128)(2,1)S(1)}, u32[]{:S(2)}, u32[]{:S(2)}) collective-permute-start(bf16[400,128]{1,0:T(8,128)(2,1)S(1)} %get-tuple-element.24.pack_ref.refs_0_), channel_id=1, source_target_pairs={{0,8},{2,10},{4,12},{6,14},{8,0},{10,2},{12,4},{14,6},{16,24},{18,... | collective-permute-start | bytes 307208 | tf_op jit(solution)/shard_map/ppermute | solution.py:337
  8.3 10.7 %collective-permute-start.1 = (bf16[400,128]{1,0:T(8,128)(2,1)S(1)}, bf16[400,128]{1,0:T(8,128)(2,1)S(1)}, u32[]{:S(2)}, u32[]{:S(2)}) collective-permute-start(bf16[400,128]{1,0:T(8,128)(2,1)S(1)} %get-tuple-element.24.pack_ref.refs_0_), channel_id=1, source_target_pairs={{0,16},{2,18},{4,20},{6,22},{8,24},{10,26},{12,28},{14,30},{16,0},... | collective-permute-start | bytes 307208 | tf_op jit(solution)/shard_map/ppermute | solution.py:337
  10.9 8.1 %collective-permute-start.2 = (bf16[400,128]{1,0:T(8,128)(2,1)S(1)}, bf16[400,128]{1,0:T(8,128)(2,1)S(1)}, u32[]{:S(2)}, u32[]{:S(2)}) collective-permute-start(bf16[400,128]{1,0:T(8,128)(2,1)S(1)} %get-tuple-element.24.pack_ref.refs_0_), channel_id=1, source_target_pairs={{0,24},{2,26},{4,28},{6,30},{8,16},{10,18},{12,20},{14,22},{16,8},... | collective-permute-start | bytes 307208 | tf_op jit(solution)/shard_map/ppermute | solution.py:337
  19.1 1.6 %collective-permute-start.3 = (bf16[1024,128]{1,0:T(8,128)(2,1)S(1)}, bf16[1024,128]{1,0:T(8,128)(2,1)S(1)}, u32[]{:S(2)}, u32[]{:S(2)}) collective-permute-start(bf16[1024,128]{1,0:T(8,128)(2,1)S(1)} %pad_maximum_fusion), channel_id=1, source_target_pairs={{0,1},{1,0},{2,3},{3,2},{4,5},{5,4},{6,7},{7,6},{8,9},{9,8},{10,11... | collective-permute-start | bytes 786440 | tf_op jit(solution)/shard_map/ppermute | solution.py:333
  19.2 20.2 %collective-permute-start.10 = (bf16[256,1024]{1,0:T(8,128)(2,1)}, bf16[256,1024]{1,0:T(8,128)(2,1)S(1)}, u32[]{:S(2)}, u32[]{:S(2)}) collective-permute-start(bf16[256,1024]{1,0:T(8,128)(2,1)} %refs_10_.1), channel_id=1, source_target_pairs={{0,1},{1,0},{2,3},{3,2},{4,5},{5,4},{6,7},{7,6},{8,9},{9,8},{10,11... | collective-permute-start | bytes 1572872 | tf_op jit(solution)/shard_map/ppermute | solution.py:333
  19.9 4.6 %copy-start.7 = (bf16[1024,256]{1,0:T(8,128)(2,1)S(1)}, bf16[1024,256]{1,0:T(8,128)(2,1)}, u32[]{:S(2)}) copy-start(bf16[1024,256]{1,0:T(8,128)(2,1)} %refs_12_.1) | copy-start | bytes 1572868
  19.9 4.6 %copy-start.5 = (bf16[256,1024]{1,0:T(8,128)(2,1)S(1)}, bf16[256,1024]{1,0:T(8,128)(2,1)}, u32[]{:S(2)}) copy-start(bf16[256,1024]{1,0:T(8,128)(2,1)} %refs_8_.1) | copy-start | bytes 1572868
  19.9 5.1 %copy-start.2 = (bf16[1024,256]{1,0:T(8,128)(2,1)S(1)}, bf16[1024,256]{1,0:T(8,128)(2,1)}, u32[]{:S(2)}) copy-start(bf16[1024,256]{1,0:T(8,128)(2,1)} %down_a.1) | copy-start | bytes 1572868
  19.9 19.5 %copy-start.14 = (bf16[256,1024]{1,0:T(8,128)(2,1)S(1)}, bf16[256,1024]{1,0:T(8,128)(2,1)}, u32[]{:S(2)}) copy-start(bf16[256,1024]{1,0:T(8,128)(2,1)} %gate_a.1) | copy-start | bytes 1572868
  19.9 19.5 %copy-start.15 = (bf16[256,1024]{1,0:T(8,128)(2,1)S(1)}, bf16[256,1024]{1,0:T(8,128)(2,1)}, u32[]{:S(2)}) copy-start(bf16[256,1024]{1,0:T(8,128)(2,1)} %up_a.1) | copy-start | bytes 1572868
  20.0 20.0 %copy-start.6 = (bf16[256,1024]{1,0:T(8,128)(2,1)S(1)}, bf16[256,1024]{1,0:T(8,128)(2,1)}, u32[]{:S(2)}) copy-start(bf16[256,1024]{1,0:T(8,128)(2,1)} %refs_10_.1) | copy-start | bytes 1572868
  20.0 20.0 %copy-start.11 = (f32[256]{0:T(256)S(1)}, f32[256]{0:T(256)}, u32[]{:S(2)}) copy-start(f32[256]{0:T(256)} %param.22) | copy-start | bytes 3076
  22.9 22.2 %copy-start.1 = (bf16[256,128]{1,0:T(8,128)(2,1)S(1)}, bf16[256,128]{1,0:T(8,128)(2,1)}, u32[]{:S(2)}) copy-start(bf16[256,128]{1,0:T(8,128)(2,1)} %cot_ref.3) | copy-start | bytes 196612
  23.0 5.6 %collective-permute-start.6 = (bf16[256,256]{1,0:T(8,128)(2,1)S(1)}, bf16[256,256]{1,0:T(8,128)(2,1)S(1)}, u32[]{:S(2)}, u32[]{:S(2)}) collective-permute-start(bf16[256,256]{1,0:T(8,128)(2,1)S(1)} %get-tuple-element.29), channel_id=1, source_target_pairs={{0,2},{2,0},{4,6},{6,4},{8,10},{10,8},{12,14},{14,12},{16,18},{18,... | collective-permute-start | bytes 393224 | tf_op jit(solution)/shard_map/ppermute | solution.py:345
  24.5 15.4 %collective-permute-start.11 = (bf16[1024,256]{1,0:T(8,128)(2,1)S(1)}, bf16[1024,256]{1,0:T(8,128)(2,1)S(1)}, u32[]{:S(2)}, u32[]{:S(2)}) collective-permute-start(bf16[1024,256]{1,0:T(8,128)(2,1)S(1)} %copy-done.7), channel_id=1, source_target_pairs={{0,1},{1,0},{2,3},{3,2},{4,5},{5,4},{6,7},{7,6},{8,9},{9,8},{10,11... | collective-permute-start | bytes 1572872 | tf_op jit(solution)/shard_map/ppermute | solution.py:333
  24.5 15.5 %collective-permute-start.9 = (bf16[256,1024]{1,0:T(8,128)(2,1)S(1)}, bf16[256,1024]{1,0:T(8,128)(2,1)S(1)}, u32[]{:S(2)}, u32[]{:S(2)}) collective-permute-start(bf16[256,1024]{1,0:T(8,128)(2,1)S(1)} %copy-done.5), channel_id=1, source_target_pairs={{0,1},{1,0},{2,3},{3,2},{4,5},{5,4},{6,7},{7,6},{8,9},{9,8},{10,11... | collective-permute-start | bytes 1572872 | tf_op jit(solution)/shard_map/ppermute | solution.py:333
  25.0 19.6 %collective-permute-start.5 = (bf16[1024,256]{1,0:T(8,128)(2,1)S(1)}, bf16[1024,256]{1,0:T(8,128)(2,1)S(1)}, u32[]{:S(2)}, u32[]{:S(2)}) collective-permute-start(bf16[1024,256]{1,0:T(8,128)(2,1)S(1)} %copy-done.2), channel_id=1, source_target_pairs={{0,1},{1,0},{2,3},{3,2},{4,5},{5,4},{6,7},{7,6},{8,9},{9,8},{10,11... | collective-permute-start | bytes 1572872 | tf_op jit(solution)/shard_map/ppermute | solution.py:333
  28.6 5.0 %collective-permute-start.7 = (bf16[256,256]{1,0:T(8,128)(2,1)S(1)}, bf16[256,256]{1,0:T(8,128)(2,1)S(1)}, u32[]{:S(2)}, u32[]{:S(2)}) collective-permute-start(bf16[256,256]{1,0:T(8,128)(2,1)S(1)} %get-tuple-element.30), channel_id=1, source_target_pairs={{0,4},{2,6},{4,0},{6,2},{8,12},{10,14},{12,8},{14,10},{16,20},{18,... | collective-permute-start | bytes 393224 | tf_op jit(solution)/shard_map/ppermute | solution.py:345
  33.5 5.9 %collective-permute-start.8 = (bf16[256,256]{1,0:T(8,128)(2,1)S(1)}, bf16[256,256]{1,0:T(8,128)(2,1)S(1)}, u32[]{:S(2)}, u32[]{:S(2)}) collective-permute-start(bf16[256,256]{1,0:T(8,128)(2,1)S(1)} %get-tuple-element.31), channel_id=1, source_target_pairs={{0,6},{2,4},{4,2},{6,0},{8,14},{10,12},{12,10},{14,8},{16,22},{18,... | collective-permute-start | bytes 393224 | tf_op jit(solution)/shard_map/ppermute | solution.py:345
  39.4 12.5 %collective-permute-start.16 = (bf16[256,1024]{1,0:T(8,128)(2,1)S(1)}, bf16[256,1024]{1,0:T(8,128)(2,1)S(1)}, u32[]{:S(2)}, u32[]{:S(2)}) collective-permute-start(bf16[256,1024]{1,0:T(8,128)(2,1)S(1)} %copy-done.14), channel_id=1, source_target_pairs={{0,1},{1,0},{2,3},{3,2},{4,5},{5,4},{6,7},{7,6},{8,9},{9,8},{10,11... | collective-permute-start | bytes 1572872 | tf_op jit(solution)/shard_map/ppermute | solution.py:333
  39.4 12.5 %collective-permute-start.17 = (bf16[256,1024]{1,0:T(8,128)(2,1)S(1)}, bf16[256,1024]{1,0:T(8,128)(2,1)S(1)}, u32[]{:S(2)}, u32[]{:S(2)}) collective-permute-start(bf16[256,1024]{1,0:T(8,128)(2,1)S(1)} %copy-done.15), channel_id=1, source_target_pairs={{0,1},{1,0},{2,3},{3,2},{4,5},{5,4},{6,7},{7,6},{8,9},{9,8},{10,11... | collective-permute-start | bytes 1572872 | tf_op jit(solution)/shard_map/ppermute | solution.py:333
  39.9 3.2 %collective-permute-start.4 = (bf16[128,128]{1,0:T(8,128)(2,1)S(1)}, bf16[128,128]{1,0:T(8,128)(2,1)S(1)}, u32[]{:S(2)}, u32[]{:S(2)}) collective-permute-start(bf16[128,128]{1,0:T(8,128)(2,1)S(1)} %get-tuple-element.26), channel_id=1, source_target_pairs={{0,1},{1,0},{2,3},{3,2},{4,5},{5,4},{6,7},{7,6},{8,9},{9,8},{10,11... | collective-permute-start | bytes 98312 | tf_op jit(solution)/shard_map/ppermute | solution.py:333
  41.6 6.3 %collective-permute-start.12 = (bf16[256,256]{1,0:T(8,128)(2,1)S(1)}, bf16[256,256]{1,0:T(8,128)(2,1)S(1)}, u32[]{:S(2)}, u32[]{:S(2)}) collective-permute-start(bf16[256,256]{1,0:T(8,128)(2,1)S(1)} %get-tuple-element.32.refs_0_), channel_id=1, source_target_pairs={{0,2},{2,0},{4,6},{6,4},{8,10},{10,8},{12,14},{14,12},{16,18},{18,... | collective-permute-start | bytes 393224 | tf_op jit(solution)/shard_map/ppermute | solution.py:345
  43.1 8.4 %collective-permute-start.13 = (bf16[256,256]{1,0:T(8,128)(2,1)S(1)}, bf16[256,256]{1,0:T(8,128)(2,1)S(1)}, u32[]{:S(2)}, u32[]{:S(2)}) collective-permute-start(bf16[256,256]{1,0:T(8,128)(2,1)S(1)} %get-tuple-element.32.refs_0_), channel_id=1, source_target_pairs={{0,4},{2,6},{4,0},{6,2},{8,12},{10,14},{12,8},{14,10},{16,20},{18,... | collective-permute-start | bytes 393224 | tf_op jit(solution)/shard_map/ppermute | solution.py:345
  44.6 6.8 %collective-permute-start.14 = (bf16[256,256]{1,0:T(8,128)(2,1)S(1)}, bf16[256,256]{1,0:T(8,128)(2,1)S(1)}, u32[]{:S(2)}, u32[]{:S(2)}) collective-permute-start(bf16[256,256]{1,0:T(8,128)(2,1)S(1)} %get-tuple-element.32.refs_0_), channel_id=1, source_target_pairs={{0,6},{2,4},{4,2},{6,0},{8,14},{10,12},{12,10},{14,8},{16,22},{18,... | collective-permute-start | bytes 393224 | tf_op jit(solution)/shard_map/ppermute | solution.py:345
  45.1 8.1 %copy-start.16 = (f32[256]{0:T(256)S(1)}, f32[256]{0:T(256)}, u32[]{:S(2)}) copy-start(f32[256]{0:T(256)} %param.23) | copy-start | bytes 3076
  51.8 1.4 %collective-permute-start.15 = (f32[128,256]{1,0:T(8,128)S(1)}, f32[128,256]{1,0:T(8,128)S(1)}, u32[]{:S(2)}, u32[]{:S(2)}) collective-permute-start(f32[128,256]{1,0:T(8,128)S(1)} %get-tuple-element.34), channel_id=1, source_target_pairs={{0,1},{1,0},{2,3},{3,2},{4,5},{5,4},{6,7},{7,6},{8,9},{9,8},{10,11... | collective-permute-start | bytes 393224 | tf_op jit(solution)/shard_map/ppermute | solution.py:333
  55.1 4.5 %collective-permute-start.18 = (bf16[128,256]{1,0:T(8,128)(2,1)S(1)}, bf16[128,256]{1,0:T(8,128)(2,1)S(1)}, u32[]{:S(2)}, u32[]{:S(2)}) collective-permute-start(bf16[128,256]{1,0:T(8,128)(2,1)S(1)} %item.1.refs_0_), channel_id=1, source_target_pairs={{0,8},{2,10},{4,12},{6,14},{8,0},{10,2},{12,4},{14,6},{16,24},{18,... | collective-permute-start | bytes 196616 | tf_op jit(solution)/shard_map/ppermute | solution.py:337
  56.8 8.2 %collective-permute-start.19 = (bf16[128,256]{1,0:T(8,128)(2,1)S(1)}, bf16[128,256]{1,0:T(8,128)(2,1)S(1)}, u32[]{:S(2)}, u32[]{:S(2)}) collective-permute-start(bf16[128,256]{1,0:T(8,128)(2,1)S(1)} %item.1.refs_0_), channel_id=1, source_target_pairs={{0,16},{2,18},{4,20},{6,22},{8,24},{10,26},{12,28},{14,30},{16,0},... | collective-permute-start | bytes 196616 | tf_op jit(solution)/shard_map/ppermute | solution.py:337
  58.2 6.8 %collective-permute-start.20 = (bf16[128,256]{1,0:T(8,128)(2,1)S(1)}, bf16[128,256]{1,0:T(8,128)(2,1)S(1)}, u32[]{:S(2)}, u32[]{:S(2)}) collective-permute-start(bf16[128,256]{1,0:T(8,128)(2,1)S(1)} %item.1.refs_0_), channel_id=1, source_target_pairs={{0,24},{2,26},{4,28},{6,30},{8,16},{10,18},{12,20},{14,22},{16,8},... | collective-permute-start | bytes 196616 | tf_op jit(solution)/shard_map/ppermute | solution.py:337
  65.0 1.6 %collective-permute-start.21 = (bf16[512,256]{1,0:T(8,128)(2,1)S(1)}, bf16[512,256]{1,0:T(8,128)(2,1)S(1)}, u32[]{:S(2)}, u32[]{:S(2)}) collective-permute-start(bf16[512,256]{1,0:T(8,128)(2,1)S(1)} %pad_maximum_fusion.1), channel_id=1, source_target_pairs={{0,1},{1,0},{2,3},{3,2},{4,5},{5,4},{6,7},{7,6},{8,9},{9,8},{10,11... | collective-permute-start | bytes 786440 | tf_op jit(solution)/shard_map/ppermute | solution.py:333
  67.4 6.3 %collective-permute-start.22 = (bf16[256,256]{1,0:T(8,128)(2,1)S(1)}, bf16[256,256]{1,0:T(8,128)(2,1)S(1)}, u32[]{:S(2)}, u32[]{:S(2)}) collective-permute-start(bf16[256,256]{1,0:T(8,128)(2,1)S(1)} %get-tuple-element.37), channel_id=1, source_target_pairs={{0,2},{2,0},{4,6},{6,4},{8,10},{10,8},{12,14},{14,12},{16,18},{18,... | collective-permute-start | bytes 393224 | tf_op jit(solution)/shard_map/ppermute | solution.py:345
  68.7 6.5 %collective-permute-start.23 = (bf16[256,256]{1,0:T(8,128)(2,1)S(1)}, bf16[256,256]{1,0:T(8,128)(2,1)S(1)}, u32[]{:S(2)}, u32[]{:S(2)}) collective-permute-start(bf16[256,256]{1,0:T(8,128)(2,1)S(1)} %get-tuple-element.38), channel_id=1, source_target_pairs={{0,4},{2,6},{4,0},{6,2},{8,12},{10,14},{12,8},{14,10},{16,20},{18,... | collective-permute-start | bytes 393224 | tf_op jit(solution)/shard_map/ppermute | solution.py:345
  69.5 7.2 %collective-permute-start.24 = (bf16[256,256]{1,0:T(8,128)(2,1)S(1)}, bf16[256,256]{1,0:T(8,128)(2,1)S(1)}, u32[]{:S(2)}, u32[]{:S(2)}) collective-permute-start(bf16[256,256]{1,0:T(8,128)(2,1)S(1)} %get-tuple-element.39), channel_id=1, source_target_pairs={{0,6},{2,4},{4,2},{6,0},{8,14},{10,12},{12,10},{14,8},{16,22},{18,... | collective-permute-start | bytes 393224 | tf_op jit(solution)/shard_map/ppermute | solution.py:345
  76.7 12.0 %copy-start.4 = (f32[256,128]{1,0:T(8,128)S(1)}, f32[256,128]{1,0:T(8,128)}, u32[]{:S(2)}) copy-start(f32[256,128]{1,0:T(8,128)} %rows_ref.3) | copy-start | bytes 393220
  76.7 12.0 %copy-start.8 = (f32[256,128]{1,0:T(8,128)S(1)}, f32[256,128]{1,0:T(8,128)}, u32[]{:S(2)}) copy-start(f32[256,128]{1,0:T(8,128)} %first_ref.1) | copy-start | bytes 393220
  76.7 12.0 %copy-start.9 = (f32[256,128]{1,0:T(8,128)S(1)}, f32[256,128]{1,0:T(8,128)}, u32[]{:S(2)}) copy-start(f32[256,128]{1,0:T(8,128)} %second_ref.1) | copy-start | bytes 393220
  78.5 6.2 %collective-permute-start.25 = (bf16[256,256]{1,0:T(8,128)(2,1)S(1)}, bf16[256,256]{1,0:T(8,128)(2,1)S(1)}, u32[]{:S(2)}, u32[]{:S(2)}) collective-permute-start(bf16[256,256]{1,0:T(8,128)(2,1)S(1)} %basket_back.1.refs_0_), channel_id=1, source_target_pairs={{0,2},{2,0},{4,6},{6,4},{8,10},{10,8},{12,14},{14,12},{16,18},{18,... | collective-permute-start | bytes 393224 | tf_op jit(solution)/shard_map/ppermute | solution.py:345
  79.4 7.6 %collective-permute-start.26 = (bf16[256,256]{1,0:T(8,128)(2,1)S(1)}, bf16[256,256]{1,0:T(8,128)(2,1)S(1)}, u32[]{:S(2)}, u32[]{:S(2)}) collective-permute-start(bf16[256,256]{1,0:T(8,128)(2,1)S(1)} %basket_back.1.refs_0_), channel_id=1, source_target_pairs={{0,4},{2,6},{4,0},{6,2},{8,12},{10,14},{12,8},{14,10},{16,20},{18,... | collective-permute-start | bytes 393224 | tf_op jit(solution)/shard_map/ppermute | solution.py:345
  80.9 6.1 %collective-permute-start.27 = (bf16[256,256]{1,0:T(8,128)(2,1)S(1)}, bf16[256,256]{1,0:T(8,128)(2,1)S(1)}, u32[]{:S(2)}, u32[]{:S(2)}) collective-permute-start(bf16[256,256]{1,0:T(8,128)(2,1)S(1)} %basket_back.1.refs_0_), channel_id=1, source_target_pairs={{0,6},{2,4},{4,2},{6,0},{8,14},{10,12},{12,10},{14,8},{16,22},{18,... | collective-permute-start | bytes 393224 | tf_op jit(solution)/shard_map/ppermute | solution.py:345
  87.3 1.4 %collective-permute-start.28 = (f32[256,128]{1,0:T(8,128)S(1)}, f32[256,128]{1,0:T(8,128)S(1)}, u32[]{:S(2)}, u32[]{:S(2)}) collective-permute-start(f32[256,128]{1,0:T(8,128)S(1)} %get-tuple-element.44), channel_id=1, source_target_pairs={{0,1},{1,0},{2,3},{3,2},{4,5},{5,4},{6,7},{7,6},{8,9},{9,8},{10,11... | collective-permute-start | bytes 393224 | tf_op jit(solution)/shard_map/ppermute | solution.py:333

commit v2 on v1

--- a/solution.py
+++ b/solution.py
@@ -8,6 +8,7 @@
 from jax.experimental.pallas import tpu as pltpu
 from jax.sharding import PartitionSpec as P
 
+
 BLOCK = 128
 GATHER = 4
 CHUNK = 256
@@ -31,11 +32,13 @@
     return int(np.prod(x.shape)) * jnp.dtype(x.dtype).itemsize
 
 
-def run(body, outs, smem, args, scratch=(), flops=1 << 20, name=None):
-    limit = sum(nbytes(x) for x in (*args, *jax.tree.leaves(outs), *scratch)) + (4 << 20)
-    specs = [pl.BlockSpec(memory_space=pltpu.SMEM)] * len(smem)
+def run(body, outs, smem, args, scratch=(), flops=1 << 20, far=(), limit=0):
+    held = [x for x in scratch if isinstance(x.dtype, np.dtype) or x.dtype in (F32, BF16)]
+    limit = limit or sum(nbytes(x) for x in (*args, *jax.tree.leaves(outs), *held)) + (4 << 20)
+    specs = [pl.BlockSpec(memory_space=pltpu.HBM)] * len(far)
+    specs += [pl.BlockSpec(memory_space=pltpu.SMEM)] * len(smem)
     specs += [pl.BlockSpec(memory_space=pltpu.VMEM)] * len(args)
-    return pl.pallas_call(
+    call = pl.pallas_call(
         body,
         out_shape=outs,
         in_specs=specs,
@@ -43,8 +46,9 @@
         scratch_shapes=list(scratch),
         cost_estimate=pl.CostEstimate(flops=flops, bytes_accessed=1 << 20, transcendentals=0),
         compiler_params=pltpu.CompilerParams(vmem_limit_bytes=min(limit, 60 * 1024 * 1024)),
-        name=name,
-    )(*smem, *args)
+    )
+    far = [pltpu.with_memory_space_constraint(x, pltpu.HBM) for x in far]
+    return call(*far, *smem, *args)
 
 
 def dot(a, b):
@@ -60,19 +64,52 @@
 
 
 def pack_body(
-    dest_ref, item_ref, rows_ref, words_ref, cot_ref, pack_ref, send_ref, lo_ref, hi_ref, *, half, members, groups
+    dest_hbm,
+    item_hbm,
+    words_hbm,
+    rows_hbm,
+    cot_hbm,
+    pack_ref,
+    send_ref,
+    dest_ref,
+    item_ref,
+    words_ref,
+    rows_ref,
+    turned_ref,
+    sems,
+    *,
+    half,
+    members,
+    groups,
 ):
     items = rows_ref.shape[0]
     tiles = dest_ref.shape[0]
     core = lax.axis_index("mp")
     place = lax.axis_index("shard") % groups
     start = pl.multiple_of(core * half, half)
-    pack_ref[0:items, :] = rows_ref[...].astype(BF16)
-    words = words_ref[...]
-    lo_ref[...] = (words & 255).astype(F32).T
-    hi_ref[...] = (words >> 8).astype(F32).T
-    pack_ref[items : items + half, :] = lo_ref[pl.ds(start, half), :].astype(BF16)
-    pack_ref[items + half : items + 2 * half, :] = hi_ref[pl.ds(start, half), :].astype(BF16)
+    rows = send_ref.shape[0]
+    theirs = pl.ds(pl.multiple_of((1 - core) * rows, rows), rows)
+    copies = [
+        pltpu.make_async_copy(src, dst, sems.at[i])
+        for i, (src, dst) in enumerate(
+            (
+                (words_hbm, words_ref),
+                (dest_hbm, dest_ref),
+                (item_hbm, item_ref),
+                (rows_hbm, rows_ref),
+                (cot_hbm.at[theirs, :], send_ref),
+            )
+        )
+    ]
+    for copy in copies:
+        copy.start()
+    copies[0].wait()
+    turned_ref[...] = words_ref[...].astype(F32).T
+    words = turned_ref[pl.ds(start, half), :].astype(jnp.int32)
+    pack_ref[items : items + half, :] = (words & 255).astype(F32).astype(BF16)
+    pack_ref[items + half : items + 2 * half, :] = (words >> 8).astype(F32).astype(BF16)
+    copies[1].wait()
+    copies[2].wait()
     lanes = lax.broadcasted_iota(jnp.int32, (16, pack_ref.shape[1]), 1)
     meta = jnp.zeros_like(lanes)
     for t in range(tiles):
@@ -81,8 +118,9 @@
         meta = jnp.where(lanes == t, slot, meta)
         meta = jnp.where(lanes == tiles + t, item_ref[t], meta)
     pack_ref[items + 2 * half :, :] = meta.astype(F32).astype(BF16)
-    rows = send_ref.shape[0]
-    send_ref[...] = cot_ref[pl.ds(pl.multiple_of((1 - core) * rows, rows), rows), :]
+    copies[3].wait()
+    pack_ref[0:items, :] = rows_ref[...].astype(BF16)
+    copies[4].wait()
 
 
 def spread_body(pack_ref, out_ref):
@@ -105,13 +143,9 @@
         ]
 
 
-def sums_body(idx_ref, *refs, members, groups, half, items, tiles):
+def masks_body(idx_ref, *refs, members, half, items, tiles):
     packs = refs[:members]
-    other_ref, spread_ref = refs[members : members + 2]
-    mt_ref = refs[members + 2]
-    out_refs = refs[members + 3 : members + 3 + groups]
-    rows_ref = refs[members + 3 + groups]
-    core = lax.axis_index("mp")
+    spread_ref, mt_ref = refs[members:]
     mt_ref[...] = jnp.zeros_like(mt_ref)
     byte_rows = jnp.concatenate(
         [
@@ -137,14 +171,27 @@
                     mt_ref[where]
                     + mask[l * half : (l + 1) * half, b * BLOCK : (b + 1) * BLOCK]
                 )
-    join_halves(core, rows_ref, packs, other_ref, items)
-    per = members * half
+
+
+def sums_body(mt_ref, *refs, members, groups, items):
+    packs = refs[:members]
+    other_ref = refs[members]
+    out_refs = refs[members + 1 : members + 1 + groups]
+    rows_ref = refs[members + 1 + groups]
+    join_halves(lax.axis_index("mp"), rows_ref, packs, other_ref, items)
+    per = out_refs[0].shape[0]
     for i in range(groups):
         total = dot(mt_ref[i * per : (i + 1) * per, :], rows_ref[...])
         out_refs[i][...] = total.astype(out_refs[i].dtype)
 
 
-def turn_body(mt_ref, mine_ref, other_ref, down_a, down_b, out_ref, hid_ref, cot_ref, *, items):
+def turn_body(mt_ref, out_ref, *, items):
+    for c in range(mt_ref.shape[0] // BLOCK):
+        block = mt_ref[c * BLOCK : (c + 1) * BLOCK, 0:items].astype(F32)
+        out_ref[:, c * BLOCK : (c + 1) * BLOCK] = block.T.astype(BF16)
+
+
+def item_hidden_body(mine_ref, other_ref, down_a, down_b, hid_ref, cot_ref):
     core = lax.axis_index("mp")
     width = mine_ref.shape[1]
     rows = other_ref.shape[0]
@@ -158,9 +205,6 @@
         for c in range(0, down.shape[0], CHUNK):
             hid_ref[:, at : at + CHUNK] = dot_nt(cot, down[c : c + CHUNK, :])
             at += CHUNK
-    for c in range(mt_ref.shape[0] // BLOCK):
-        block = mt_ref[c * BLOCK : (c + 1) * BLOCK, 0:items].astype(F32)
-        out_ref[:, c * BLOCK : (c + 1) * BLOCK] = block.T.astype(BF16)
 
 
 def add_all(refs):
@@ -329,74 +373,75 @@
     item_half = items // 2
     hidden = 2 * gate_basket.shape[1]
     per = members * half
+
     def swap(x):
         return lax.ppermute(x, "mp", [(0, 1), (1, 0)])
 
     def gather(x):
-        return [
-            lax.ppermute(
-                x, "shard", [(s, (((s // groups) ^ k) * groups) + s % groups) for s in range(shards)]
-            )
-            for k in range(1, members)
-        ]
+        got = []
+        for k in range(1, members):
+            pairs = [(s, ((s // groups) ^ k) * groups + s % groups) for s in range(shards)]
+            got.append(lax.ppermute(x, "shard", pairs))
+        return got
 
     def exchange(xs):
-        return [
-            lax.ppermute(
-                xs[k - 1],
-                "shard",
-                [(s, (s // groups) * groups + ((s % groups) ^ k)) for s in range(shards)],
-            )
-            for k in range(1, groups)
-        ]
+        got = []
+        for k in range(1, groups):
+            pairs = [(s, (s // groups) * groups + ((s % groups) ^ k)) for s in range(shards)]
+            got.append(lax.ppermute(xs[k - 1], "shard", pairs))
+        return got
 
     pack, cot_send = run(
         functools.partial(pack_body, half=half, members=members, groups=groups),
         [sds((items + 2 * half + 16, width), BF16), sds((item_half, width), BF16)],
-        (tile_dest, tile_item),
-        (item_rows, tile_bits.reshape(tiles * words, BLOCK), item_cot),
-        scratch=[pltpu.VMEM((BLOCK, tiles * words), F32)] * 2,
-        name="pack",
+        (),
+        (),
+        far=(tile_dest, tile_item, tile_bits.reshape(tiles * words, BLOCK), item_rows, item_cot),
+        scratch=[
+            pltpu.SMEM((tiles,), jnp.int32),
+            pltpu.SMEM((tiles,), jnp.int32),
+            pltpu.VMEM((tiles * words, BLOCK), jnp.int32),
+            pltpu.VMEM((items, width), F32),
+            pltpu.VMEM((BLOCK, tiles * words), F32),
+            pltpu.SemaphoreType.DMA((5,)),
+        ],
     )
     packs = [pack] + gather(pack)
     spread = run(
-        spread_body,
-        sds((2 * tiles * words, tiles * BLOCK), BF16),
-        (),
-        (pack,),
-        flops=1 << 29,
-        name="spread",
+        spread_body, sds((2 * tiles * words, tiles * BLOCK), BF16), (), (pack,), flops=1 << 29
     )
     cot_other = swap(cot_send)
     gate_b, up_b, down_b = gate_basket, up_basket, down_basket
     gate_bo, up_bo, down_bo = swap(gate_basket), swap(up_basket), swap(down_basket)
-    gate_io, up_io, down_io = swap(gate_item), swap(up_item), swap(down_item)
     rows_other = swap(jnp.concatenate([q[:items] for q in packs], axis=0))
     metas = [q[items + 2 * half : items + 2 * half + 1] for q in packs]
     idx = jnp.concatenate(metas, axis=0).astype(jnp.int32)
 
     part_shapes = [sds((per, features), F32)] + [sds((per, features), BF16)] * (groups - 1)
-    mt, *parts = run(
-        functools.partial(
-            sums_body, members=members, groups=groups, half=half, items=items, tiles=tiles
-        ),
-        [sds((shards * half, members * items), BF16)] + part_shapes,
+    mt = run(
+        functools.partial(masks_body, members=members, half=half, items=items, tiles=tiles),
+        sds((shards * half, members * items), BF16),
         (idx,),
-        (*packs, rows_other, spread),
+        (*packs, spread),
+        flops=1 << 29,
+    )
+    parts = run(
+        functools.partial(sums_body, members=members, groups=groups, items=items),
+        part_shapes,
+        (),
+        (mt, *packs, rows_other),
         scratch=[pltpu.VMEM((members * items, features), BF16)],
-        flops=1 << 30,
-        name="sums",
+        flops=1 << 29,
     )
     received = exchange(parts[1:])
-    mo, item_hidden = run(
+    mo = run(
         functools.partial(turn_body, items=items),
-        [sds((items, shards * half), BF16), sds((item_half, hidden), F32)],
-        (),
-        (mt, item_cot, cot_other, down_item, down_io),
-        scratch=[pltpu.VMEM((item_half, features), BF16)],
+        sds((items, shards * half), BF16),
+        (),
+        (mt,),
         flops=1 << 29,
-        name="turn",
-    )
+    )
+    gate_io, up_io, down_io = swap(gate_item), swap(up_item), swap(down_item)
     basket_out, basket_sum, value, slope = run(
         functools.partial(basket_body, groups=groups),
         [
@@ -418,9 +463,16 @@
             down_bo,
         ),
         flops=1 << 30,
-        name="basket",
     )
     outs = [basket_out] + exchange([basket_out] * (groups - 1))
+    item_hidden = run(
+        item_hidden_body,
+        sds((item_half, hidden), F32),
+        (),
+        (item_cot, cot_other, down_item, down_io),
+        scratch=[pltpu.VMEM((item_half, features), BF16)],
+        flops=1 << 29,
+    )
     message_mine, message_theirs = run(
         functools.partial(message_body, groups=groups),
         [sds((item_half, features), F32)] * 2,
@@ -428,7 +480,6 @@
         (mo, *outs),
         scratch=[pltpu.VMEM((items, features), F32)],
         flops=1 << 28,
-        name="message",
     )
     message_other = swap(message_theirs)
     grad_message = run(
@@ -446,7 +497,6 @@
             up_io,
         ),
         flops=1 << 30,
-        name="item",
     )
     grads = [grad_message] + gather(grad_message)
     grads_other = swap(jnp.concatenate(grads, axis=0))
@@ -457,7 +507,6 @@
         (mt, *grads, grads_other),
         scratch=[pltpu.VMEM((members * items, features), BF16)],
         flops=1 << 29,
-        name="grad_sums",
     )
     grad_received = exchange(grad_parts[1:])
     grad_sum = run(
@@ -479,7 +528,6 @@
             down_bo,
         ),
         flops=1 << 30,
-        name="basket_back",
     )
     sums = [grad_sum] + exchange([grad_sum] * (groups - 1))
     back_mine, back_theirs = run(
@@ -489,7 +537,6 @@
         (mo, *sums),
         scratch=[pltpu.VMEM((items, features), F32)],
         flops=1 << 28,
-        name="back",
     )
     back_other = swap(back_theirs)
     new_rows, new_first, new_second = run(
@@ -497,7 +544,6 @@
         [sds((items, width), F32)] * 3,
         (),
         (back_mine, back_other, item_cot, item_rows, first_moment, second_moment),
-        name="adam",
     )
     return (new_rows, new_first, new_second)
 

time: 89.8 us -> 83.6 us (0.931)
  waiting for transfers between devices: 45.4 us -> 40 us
  local copies, waits for them, and re-layouts: 3.98 us -> 0.1 us
  starting transfers between devices: 28.3 us -> 30.6 us
    ppermute x18, waiting for transfers between devices: 40.5 us -> 36.2 us  [the longest x12 22.5 us: exchange(): got.append(lax.ppermute(xs[k - 1], 'shard', pairs))]
    unnamed x34 -> x24, local copies, waits for them, and re-layouts: 3.95 us -> 0.07 us
    ppermute x18, starting transfers between devices: 26.3 us -> 28.3 us  [the longest x12 18.2 us: exchange(): got.append(lax.ppermute(xs[k - 1], 'shard', pairs))]
    ppermute x11, waiting for transfers between devices: 4.87 us -> 3.76 us  [swap(): return lax.ppermute(x, 'mp', [(0, 1), (1, 0)])]
    pallas_call x11 -> x13, Pallas kernels: 10.9 us -> 11.7 us  [run(): return call(*far, *smem, *args)]
  transfers between devices with their start and end apart: 29 -> 29, of which waited for: 17 -> 14; matrix products, arithmetic and copies ran while one was open for 0% -> 0% of each run, Pallas kernels for 5% -> 6%
where the time goes in v2:
time: 83.6 us; the launch traced here: 83.4 us
  waiting for transfers between devices  40 us (48%)
  starting transfers between devices  30.6 us (37%)
  Pallas kernels  11.7 us (14%)
  between operations  0.99 us (1%)
    ppermute x12, waiting for transfers between devices, exchange(): got.append(lax.ppermute(xs[k - 1], 'shard', pairs))  22.5 us
    ppermute x12, starting transfers between devices, exchange(): got.append(lax.ppermute(xs[k - 1], 'shard', pairs))  18.2 us
    ppermute x6, waiting for transfers between devices, gather(): got.append(lax.ppermute(x, 'shard', pairs))  13.7 us
    pallas_call x13, Pallas kernels, run(): return call(*far, *smem, *args)  11.7 us
    ppermute x6, starting transfers between devices, gather(): got.append(lax.ppermute(x, 'shard', pairs))  10.2 us
    ppermute x11, waiting for transfers between devices, swap(): return lax.ppermute(x, 'mp', [(0, 1), (1, 0)])  3.76 us
    ppermute x11, starting transfers between devices, swap(): return lax.ppermute(x, 'mp', [(0, 1), (1, 0)])  2.29 us
  transfers between devices with their start and end apart: 29, of which 14 were waited for; matrix products, arithmetic and copies ran while one was open for 0% of the time, Pallas kernels for 6%

profile of v2, /device:TPU:0, one launch (start us, length us, event | category | flops | bytes accessed | tf_op | source)
XLA Modules:
  0.0 83.4 jit_solution(2791790912800180730)
XLA Ops:
  0.6 1.1 %shard_map.166 = (bf16[400,128]{1,0:T(8,128)(2,1)S(1)}, bf16[128,128]{1,0:T(8,128)(2,1)S(1)}) custom-call(s32[16]{0:T(128)} %dest_hbm.1, s32[16]{0:T(128)} %item_hbm.1, s32[128,128]{1,0:T(8,128)} %bitcast.6, f32[256,128]{1,0:T(8,128)} %rows_ref.1, bf16[256,128]{1,0:T(8,128)(2,1)} %cot_ref.1), custom_call_target="tpu_custom_call" | custom-call | flops 1048576 | bytes 1048576 | tf_op jit(solution)/shard_map/pallas_call | solution.py:51
  1.8 3.1 %collective-permute-start = (bf16[400,128]{1,0:T(8,128)(2,1)S(1)}, bf16[400,128]{1,0:T(8,128)(2,1)S(1)}, u32[]{:S(2)}, u32[]{:S(2)}) collective-permute-start(bf16[400,128]{1,0:T(8,128)(2,1)S(1)} %get-tuple-element.21.pack_ref.refs_0_), channel_id=1, source_target_pairs={{0,8},{2,10},{4,12},{6,14},{8,0},{10,2},{12,4},{14,6},{16,24},{18,... | collective-permute-start | bytes 307208 | tf_op jit(solution)/shard_map/ppermute | solution.py:384
  4.9 2.6 %collective-permute-start.1 = (bf16[400,128]{1,0:T(8,128)(2,1)S(1)}, bf16[400,128]{1,0:T(8,128)(2,1)S(1)}, u32[]{:S(2)}, u32[]{:S(2)}) collective-permute-start(bf16[400,128]{1,0:T(8,128)(2,1)S(1)} %get-tuple-element.21.pack_ref.refs_0_), channel_id=1, source_target_pairs={{0,16},{2,18},{4,20},{6,22},{8,24},{10,26},{12,28},{14,30},{16,0},... | collective-permute-start | bytes 307208 | tf_op jit(solution)/shard_map/ppermute | solution.py:384
  7.5 0.3 collective-permute-done.refs_1_
  7.8 7.8 %collective-permute-done.1.refs_2_ = bf16[400,128]{1,0:T(8,128)(2,1)S(1)} collective-permute-done((bf16[400,128]{1,0:T(8,128)(2,1)S(1)}, bf16[400,128]{1,0:T(8,128)(2,1)S(1)}, u32[]{:S(2)}, u32[]{:S(2)}) %collective-permute-start.1) | collective-permute-done | bytes 102432 | tf_op jit(solution)/shard_map/ppermute | solution.py:384
  15.8 0.5 collective-permute-start.7
  16.3 0.4 collective-permute-start.9
  16.8 0.2 shard_map.167.refs_4_
  17.0 1.5 %shard_map.168.mt_ref = bf16[1024,1024]{1,0:T(8,128)(2,1)S(1)} custom-call(s32[4,128]{1,0:T(4,128)S(1)} %maximum_convert_fusion.idx_ref, bf16[400,128]{1,0:T(8,128)(2,1)S(1)} %get-tuple-element.21.pack_ref.refs_0_, bf16[400,128]{1,0:T(8,128)(2,1)S(1)} %collective-permute-done.refs_1_, bf16[400,128]{1,0:T(8,128)(2,1)S(1)} %collective-permute-done.1.refs_2_, ...), custom_call_target="tpu_custom_call" | custom-call | flops 536870912 | bytes 1048576 | tf_op jit(solution)/shard_map/pallas_call | solution.py:51
  18.6 0.8 shard_map.170
  19.4 1.6 %collective-permute-start.4 = (bf16[256,256]{1,0:T(8,128)(2,1)S(1)}, bf16[256,256]{1,0:T(8,128)(2,1)S(1)}, u32[]{:S(2)}, u32[]{:S(2)}) collective-permute-start(bf16[256,256]{1,0:T(8,128)(2,1)S(1)} %get-tuple-element.23), channel_id=1, source_target_pairs={{0,2},{2,0},{4,6},{6,4},{8,10},{10,8},{12,14},{14,12},{16,18},{18,... | collective-permute-start | bytes 393224 | tf_op jit(solution)/shard_map/ppermute | solution.py:391
  21.0 1.5 %collective-permute-start.5 = (bf16[256,256]{1,0:T(8,128)(2,1)S(1)}, bf16[256,256]{1,0:T(8,128)(2,1)S(1)}, u32[]{:S(2)}, u32[]{:S(2)}) collective-permute-start(bf16[256,256]{1,0:T(8,128)(2,1)S(1)} %get-tuple-element.24), channel_id=1, source_target_pairs={{0,4},{2,6},{4,0},{6,2},{8,12},{10,14},{12,8},{14,10},{16,20},{18,... | collective-permute-start | bytes 393224 | tf_op jit(solution)/shard_map/ppermute | solution.py:391
  22.5 2.5 %collective-permute-done.4.refs_1_ = bf16[256,256]{1,0:T(8,128)(2,1)S(1)} collective-permute-done((bf16[256,256]{1,0:T(8,128)(2,1)S(1)}, bf16[256,256]{1,0:T(8,128)(2,1)S(1)}, u32[]{:S(2)}, u32[]{:S(2)}) %collective-permute-start.4) | collective-permute-done | bytes 131104 | tf_op jit(solution)/shard_map/ppermute | solution.py:391
  25.0 2.5 %collective-permute-start.6 = (bf16[256,256]{1,0:T(8,128)(2,1)S(1)}, bf16[256,256]{1,0:T(8,128)(2,1)S(1)}, u32[]{:S(2)}, u32[]{:S(2)}) collective-permute-start(bf16[256,256]{1,0:T(8,128)(2,1)S(1)} %get-tuple-element.25), channel_id=1, source_target_pairs={{0,6},{2,4},{4,2},{6,0},{8,14},{10,12},{12,10},{14,8},{16,22},{18,... | collective-permute-start | bytes 393224 | tf_op jit(solution)/shard_map/ppermute | solution.py:391
  27.4 3.4 %collective-permute-done.6.refs_3_ = bf16[256,256]{1,0:T(8,128)(2,1)S(1)} collective-permute-done((bf16[256,256]{1,0:T(8,128)(2,1)S(1)}, bf16[256,256]{1,0:T(8,128)(2,1)S(1)}, u32[]{:S(2)}, u32[]{:S(2)}) %collective-permute-start.6) | collective-permute-done | bytes 131104 | tf_op jit(solution)/shard_map/ppermute | solution.py:391
  30.9 0.5 collective-permute-start.17
  31.4 1.6 %shard_map.171 = (bf16[256,256]{1,0:T(8,128)(2,1)S(1)}, f32[256,256]{1,0:T(8,128)S(1)}, bf16[256,2048]{1,0:T(8,128)(2,1)S(1)}, bf16[256,2048]{1,0:T(8,128)(2,1)S(1)}) custom-call(f32[256,256]{1,0:T(8,128)S(1)} %get-tuple-element.22.refs_0_, bf16[256,256]{1,0:T(8,128)(2,1)S(1)} %collective-permute-done.4.refs_1_, ...), custom_call_target="tpu_custom_call" | custom-call | flops 1073741824 | bytes 1048576 | tf_op jit(solution)/shard_map/pallas_call | solution.py:51
  33.0 1.6 %collective-permute-start.10 = (bf16[256,256]{1,0:T(8,128)(2,1)S(1)}, bf16[256,256]{1,0:T(8,128)(2,1)S(1)}, u32[]{:S(2)}, u32[]{:S(2)}) collective-permute-start(bf16[256,256]{1,0:T(8,128)(2,1)S(1)} %get-tuple-element.26.refs_0_), channel_id=1, source_target_pairs={{0,2},{2,0},{4,6},{6,4},{8,10},{10,8},{12,14},{14,12},{16,18},{18,... | collective-permute-start | bytes 393224 | tf_op jit(solution)/shard_map/ppermute | solution.py:391
  34.5 1.5 %collective-permute-start.11 = (bf16[256,256]{1,0:T(8,128)(2,1)S(1)}, bf16[256,256]{1,0:T(8,128)(2,1)S(1)}, u32[]{:S(2)}, u32[]{:S(2)}) collective-permute-start(bf16[256,256]{1,0:T(8,128)(2,1)S(1)} %get-tuple-element.26.refs_0_), channel_id=1, source_target_pairs={{0,4},{2,6},{4,0},{6,2},{8,12},{10,14},{12,8},{14,10},{16,20},{18,... | collective-permute-start | bytes 393224 | tf_op jit(solution)/shard_map/ppermute | solution.py:391
  36.0 2.5 %collective-permute-done.10.refs_1_ = bf16[256,256]{1,0:T(8,128)(2,1)S(1)} collective-permute-done((bf16[256,256]{1,0:T(8,128)(2,1)S(1)}, bf16[256,256]{1,0:T(8,128)(2,1)S(1)}, u32[]{:S(2)}, u32[]{:S(2)}) %collective-permute-start.10) | collective-permute-done | bytes 131104 | tf_op jit(solution)/shard_map/ppermute | solution.py:391
  38.5 2.5 %collective-permute-start.12 = (bf16[256,256]{1,0:T(8,128)(2,1)S(1)}, bf16[256,256]{1,0:T(8,128)(2,1)S(1)}, u32[]{:S(2)}, u32[]{:S(2)}) collective-permute-start(bf16[256,256]{1,0:T(8,128)(2,1)S(1)} %get-tuple-element.26.refs_0_), channel_id=1, source_target_pairs={{0,6},{2,4},{4,2},{6,0},{8,14},{10,12},{12,10},{14,8},{16,22},{18,... | collective-permute-start | bytes 393224 | tf_op jit(solution)/shard_map/ppermute | solution.py:391
  41.0 0.2 shard_map.169.mo_ref
  41.2 3.2 %collective-permute-done.12.refs_3_ = bf16[256,256]{1,0:T(8,128)(2,1)S(1)} collective-permute-done((bf16[256,256]{1,0:T(8,128)(2,1)S(1)}, bf16[256,256]{1,0:T(8,128)(2,1)S(1)}, u32[]{:S(2)}, u32[]{:S(2)}) %collective-permute-start.12) | collective-permute-done | bytes 131104 | tf_op jit(solution)/shard_map/ppermute | solution.py:391
  44.4 0.3 shard_map.172
  44.8 0.5 collective-permute-start.14
  45.3 0.9 %collective-permute-done.14.other_ref = bf16[128,128]{1,0:T(8,128)(2,1)S(1)} collective-permute-done((bf16[128,128]{1,0:T(8,128)(2,1)S(1)}, bf16[128,128]{1,0:T(8,128)(2,1)S(1)}, u32[]{:S(2)}, u32[]{:S(2)}) %collective-permute-start.14) | collective-permute-done | bytes 32800 | tf_op jit(solution)/shard_map/ppermute | solution.py:378
  46.2 0.5 shard_map.173.hidden_ref
  46.7 1.8 %shard_map.174.refs_0_ = bf16[128,256]{1,0:T(8,128)(2,1)S(1)} custom-call(f32[128,256]{1,0:T(8,128)S(1)} %get-tuple-element.27.mine_ref, f32[128,256]{1,0:T(8,128)S(1)} %collective-permute-done.13.other_ref, f32[128,2048]{1,0:T(8,128)S(1)} %shard_map.173.hidden_ref, f32[1,256]{1,0:T(1,128)S(1)} %bitcast.5, bf16[256,1024]{1,0:T(8,128)(2,1)S(1)} %copy-done.9, ...), custom_call_target="tpu_custom_call" | custom-call | flops 1073741824 | bytes 1048576 | tf_op jit(solution)/shard_map/pallas_call | solution.py:51
  48.5 1.7 %collective-permute-start.18 = (bf16[128,256]{1,0:T(8,128)(2,1)S(1)}, bf16[128,256]{1,0:T(8,128)(2,1)S(1)}, u32[]{:S(2)}, u32[]{:S(2)}) collective-permute-start(bf16[128,256]{1,0:T(8,128)(2,1)S(1)} %shard_map.174.refs_0_), channel_id=1, source_target_pairs={{0,8},{2,10},{4,12},{6,14},{8,0},{10,2},{12,4},{14,6},{16,24},{18,... | collective-permute-start | bytes 196616 | tf_op jit(solution)/shard_map/ppermute | solution.py:384
  50.2 1.4 %collective-permute-start.19 = (bf16[128,256]{1,0:T(8,128)(2,1)S(1)}, bf16[128,256]{1,0:T(8,128)(2,1)S(1)}, u32[]{:S(2)}, u32[]{:S(2)}) collective-permute-start(bf16[128,256]{1,0:T(8,128)(2,1)S(1)} %shard_map.174.refs_0_), channel_id=1, source_target_pairs={{0,16},{2,18},{4,20},{6,22},{8,24},{10,26},{12,28},{14,30},{16,0},... | collective-permute-start | bytes 196616 | tf_op jit(solution)/shard_map/ppermute | solution.py:384
  51.6 1.3 %collective-permute-start.20 = (bf16[128,256]{1,0:T(8,128)(2,1)S(1)}, bf16[128,256]{1,0:T(8,128)(2,1)S(1)}, u32[]{:S(2)}, u32[]{:S(2)}) collective-permute-start(bf16[128,256]{1,0:T(8,128)(2,1)S(1)} %shard_map.174.refs_0_), channel_id=1, source_target_pairs={{0,24},{2,26},{4,28},{6,30},{8,16},{10,18},{12,20},{14,22},{16,8},... | collective-permute-start | bytes 196616 | tf_op jit(solution)/shard_map/ppermute | solution.py:384
  53.0 5.6 %collective-permute-done.19.refs_2_ = bf16[128,256]{1,0:T(8,128)(2,1)S(1)} collective-permute-done((bf16[128,256]{1,0:T(8,128)(2,1)S(1)}, bf16[128,256]{1,0:T(8,128)(2,1)S(1)}, u32[]{:S(2)}, u32[]{:S(2)}) %collective-permute-start.19) | collective-permute-done | bytes 65568 | tf_op jit(solution)/shard_map/ppermute | solution.py:384
  58.7 1.5 %collective-permute-done.21.refs_4_ = bf16[512,256]{1,0:T(8,128)(2,1)S(1)} collective-permute-done((bf16[512,256]{1,0:T(8,128)(2,1)S(1)}, bf16[512,256]{1,0:T(8,128)(2,1)S(1)}, u32[]{:S(2)}, u32[]{:S(2)}) %collective-permute-start.21) | collective-permute-done | bytes 262176 | tf_op jit(solution)/shard_map/ppermute | solution.py:378
  60.2 0.7 shard_map.175
  60.9 1.6 %collective-permute-start.22 = (bf16[256,256]{1,0:T(8,128)(2,1)S(1)}, bf16[256,256]{1,0:T(8,128)(2,1)S(1)}, u32[]{:S(2)}, u32[]{:S(2)}) collective-permute-start(bf16[256,256]{1,0:T(8,128)(2,1)S(1)} %get-tuple-element.31), channel_id=1, source_target_pairs={{0,2},{2,0},{4,6},{6,4},{8,10},{10,8},{12,14},{14,12},{16,18},{18,... | collective-permute-start | bytes 393224 | tf_op jit(solution)/shard_map/ppermute | solution.py:391
  62.5 1.5 %collective-permute-start.23 = (bf16[256,256]{1,0:T(8,128)(2,1)S(1)}, bf16[256,256]{1,0:T(8,128)(2,1)S(1)}, u32[]{:S(2)}, u32[]{:S(2)}) collective-permute-start(bf16[256,256]{1,0:T(8,128)(2,1)S(1)} %get-tuple-element.32), channel_id=1, source_target_pairs={{0,4},{2,6},{4,0},{6,2},{8,12},{10,14},{12,8},{14,10},{16,20},{18,... | collective-permute-start | bytes 393224 | tf_op jit(solution)/shard_map/ppermute | solution.py:391
  64.0 0.5 collective-permute-start.24
  64.5 2.5 %collective-permute-done.22.refs_1_ = bf16[256,256]{1,0:T(8,128)(2,1)S(1)} collective-permute-done((bf16[256,256]{1,0:T(8,128)(2,1)S(1)}, bf16[256,256]{1,0:T(8,128)(2,1)S(1)}, u32[]{:S(2)}, u32[]{:S(2)}) %collective-permute-start.22) | collective-permute-done | bytes 131104 | tf_op jit(solution)/shard_map/ppermute | solution.py:391
  66.9 3.6 %collective-permute-done.23.refs_2_ = bf16[256,256]{1,0:T(8,128)(2,1)S(1)} collective-permute-done((bf16[256,256]{1,0:T(8,128)(2,1)S(1)}, bf16[256,256]{1,0:T(8,128)(2,1)S(1)}, u32[]{:S(2)}, u32[]{:S(2)}) %collective-permute-start.23) | collective-permute-done | bytes 131104 | tf_op jit(solution)/shard_map/ppermute | solution.py:391
  70.6 1.8 %shard_map.176.refs_0_ = bf16[256,256]{1,0:T(8,128)(2,1)S(1)} custom-call(f32[256,256]{1,0:T(8,128)S(1)} %get-tuple-element.30.refs_0_, bf16[256,256]{1,0:T(8,128)(2,1)S(1)} %collective-permute-done.22.refs_1_, bf16[256,256]{1,0:T(8,128)(2,1)S(1)} %collective-permute-done.23.refs_2_, bf16[256,256]{1,0:T(8,128)(2,1)S(1)} %collective-permute-done.24.refs_3_, ...), custom_call_target="tpu_custom_call" | custom-call | flops 1073741824 | bytes 1048576 | tf_op jit(solution)/shard_map/pallas_call | solution.py:51
  72.3 1.3 %collective-permute-start.25 = (bf16[256,256]{1,0:T(8,128)(2,1)S(1)}, bf16[256,256]{1,0:T(8,128)(2,1)S(1)}, u32[]{:S(2)}, u32[]{:S(2)}) collective-permute-start(bf16[256,256]{1,0:T(8,128)(2,1)S(1)} %shard_map.176.refs_0_), channel_id=1, source_target_pairs={{0,2},{2,0},{4,6},{6,4},{8,10},{10,8},{12,14},{14,12},{16,18},{18,... | collective-permute-start | bytes 393224 | tf_op jit(solution)/shard_map/ppermute | solution.py:391
  73.6 0.8 collective-permute-start.26
  74.5 1.4 %collective-permute-start.27 = (bf16[256,256]{1,0:T(8,128)(2,1)S(1)}, bf16[256,256]{1,0:T(8,128)(2,1)S(1)}, u32[]{:S(2)}, u32[]{:S(2)}) collective-permute-start(bf16[256,256]{1,0:T(8,128)(2,1)S(1)} %shard_map.176.refs_0_), channel_id=1, source_target_pairs={{0,6},{2,4},{4,2},{6,0},{8,14},{10,12},{12,10},{14,8},{16,22},{18,... | collective-permute-start | bytes 393224 | tf_op jit(solution)/shard_map/ppermute | solution.py:391
  75.9 2.4 %collective-permute-done.25.refs_1_ = bf16[256,256]{1,0:T(8,128)(2,1)S(1)} collective-permute-done((bf16[256,256]{1,0:T(8,128)(2,1)S(1)}, bf16[256,256]{1,0:T(8,128)(2,1)S(1)}, u32[]{:S(2)}, u32[]{:S(2)}) %collective-permute-start.25) | collective-permute-done | bytes 131104 | tf_op jit(solution)/shard_map/ppermute | solution.py:391
  78.3 2.5 %collective-permute-done.26.refs_2_ = bf16[256,256]{1,0:T(8,128)(2,1)S(1)} collective-permute-done((bf16[256,256]{1,0:T(8,128)(2,1)S(1)}, bf16[256,256]{1,0:T(8,128)(2,1)S(1)}, u32[]{:S(2)}, u32[]{:S(2)}) %collective-permute-start.26) | collective-permute-done | bytes 131104 | tf_op jit(solution)/shard_map/ppermute | solution.py:391
  80.8 0.4 shard_map.177
  81.3 1.3 %collective-permute-done.28.other_ref = f32[256,128]{1,0:T(8,128)S(1)} collective-permute-done((f32[256,128]{1,0:T(8,128)S(1)}, f32[256,128]{1,0:T(8,128)S(1)}, u32[]{:S(2)}, u32[]{:S(2)}) %collective-permute-start.28) | collective-permute-done | bytes 131104 | tf_op jit(solution)/shard_map/ppermute | solution.py:378
  82.6 0.8 shard_map.178
  (58 shorter events, 0.6 us)
Async XLA Ops:
  1.8 6.0 %collective-permute-start = (bf16[400,128]{1,0:T(8,128)(2,1)S(1)}, bf16[400,128]{1,0:T(8,128)(2,1)S(1)}, u32[]{:S(2)}, u32[]{:S(2)}) collective-permute-start(bf16[400,128]{1,0:T(8,128)(2,1)S(1)} %get-tuple-element.21.pack_ref.refs_0_), channel_id=1, source_target_pairs={{0,8},{2,10},{4,12},{6,14},{8,0},{10,2},{12,4},{14,6},{16,24},{18,... | collective-permute-start | bytes 307208 | tf_op jit(solution)/shard_map/ppermute | solution.py:384
  4.9 10.7 %collective-permute-start.1 = (bf16[400,128]{1,0:T(8,128)(2,1)S(1)}, bf16[400,128]{1,0:T(8,128)(2,1)S(1)}, u32[]{:S(2)}, u32[]{:S(2)}) collective-permute-start(bf16[400,128]{1,0:T(8,128)(2,1)S(1)} %get-tuple-element.21.pack_ref.refs_0_), channel_id=1, source_target_pairs={{0,16},{2,18},{4,20},{6,22},{8,24},{10,26},{12,28},{14,30},{16,0},... | collective-permute-start | bytes 307208 | tf_op jit(solution)/shard_map/ppermute | solution.py:384
  7.5 8.1 %collective-permute-start.2 = (bf16[400,128]{1,0:T(8,128)(2,1)S(1)}, bf16[400,128]{1,0:T(8,128)(2,1)S(1)}, u32[]{:S(2)}, u32[]{:S(2)}) collective-permute-start(bf16[400,128]{1,0:T(8,128)(2,1)S(1)} %get-tuple-element.21.pack_ref.refs_0_), channel_id=1, source_target_pairs={{0,24},{2,26},{4,28},{6,30},{8,16},{10,18},{12,20},{14,22},{16,8},... | collective-permute-start | bytes 307208 | tf_op jit(solution)/shard_map/ppermute | solution.py:384
  15.7 2.9 %collective-permute-start.3 = (bf16[1024,128]{1,0:T(8,128)(2,1)S(1)}, bf16[1024,128]{1,0:T(8,128)(2,1)S(1)}, u32[]{:S(2)}, u32[]{:S(2)}) collective-permute-start(bf16[1024,128]{1,0:T(8,128)(2,1)S(1)} %pad_maximum_fusion), channel_id=1, source_target_pairs={{0,1},{1,0},{2,3},{3,2},{4,5},{5,4},{6,7},{7,6},{8,9},{9,8},{10,11... | collective-permute-start | bytes 786440 | tf_op jit(solution)/shard_map/ppermute | solution.py:378
  15.8 15.1 %collective-permute-start.7 = (bf16[256,1024]{1,0:T(8,128)(2,1)}, bf16[256,1024]{1,0:T(8,128)(2,1)S(1)}, u32[]{:S(2)}, u32[]{:S(2)}) collective-permute-start(bf16[256,1024]{1,0:T(8,128)(2,1)} %refs_8_.1), channel_id=1, source_target_pairs={{0,1},{1,0},{2,3},{3,2},{4,5},{5,4},{6,7},{7,6},{8,9},{9,8},{10,11... | collective-permute-start | bytes 1572872 | tf_op jit(solution)/shard_map/ppermute | solution.py:378
  16.3 15.1 %collective-permute-start.8 = (bf16[256,1024]{1,0:T(8,128)(2,1)}, bf16[256,1024]{1,0:T(8,128)(2,1)S(1)}, u32[]{:S(2)}, u32[]{:S(2)}) collective-permute-start(bf16[256,1024]{1,0:T(8,128)(2,1)} %refs_10_.1), channel_id=1, source_target_pairs={{0,1},{1,0},{2,3},{3,2},{4,5},{5,4},{6,7},{7,6},{8,9},{9,8},{10,11... | collective-permute-start | bytes 1572872 | tf_op jit(solution)/shard_map/ppermute | solution.py:378
  16.3 15.0 %collective-permute-start.9 = (bf16[1024,256]{1,0:T(8,128)(2,1)}, bf16[1024,256]{1,0:T(8,128)(2,1)S(1)}, u32[]{:S(2)}, u32[]{:S(2)}) collective-permute-start(bf16[1024,256]{1,0:T(8,128)(2,1)} %refs_12_.1), channel_id=1, source_target_pairs={{0,1},{1,0},{2,3},{3,2},{4,5},{5,4},{6,7},{7,6},{8,9},{9,8},{10,11... | collective-permute-start | bytes 1572872 | tf_op jit(solution)/shard_map/ppermute | solution.py:378
  17.0 13.8 %copy-start.10 = (bf16[256,1024]{1,0:T(8,128)(2,1)S(1)}, bf16[256,1024]{1,0:T(8,128)(2,1)}, u32[]{:S(2)}) copy-start(bf16[256,1024]{1,0:T(8,128)(2,1)} %up_a.1) | copy-start | bytes 1572868
  18.5 8.9 %copy-start.2 = (bf16[1024,256]{1,0:T(8,128)(2,1)S(1)}, bf16[1024,256]{1,0:T(8,128)(2,1)}, u32[]{:S(2)}) copy-start(bf16[1024,256]{1,0:T(8,128)(2,1)} %down_a.1) | copy-start | bytes 1572868
  18.5 12.3 %copy-start.9 = (bf16[256,1024]{1,0:T(8,128)(2,1)S(1)}, bf16[256,1024]{1,0:T(8,128)(2,1)}, u32[]{:S(2)}) copy-start(bf16[256,1024]{1,0:T(8,128)(2,1)} %gate_a.1) | copy-start | bytes 1572868
  18.6 12.8 %copy-start.3 = (bf16[256,1024]{1,0:T(8,128)(2,1)S(1)}, bf16[256,1024]{1,0:T(8,128)(2,1)}, u32[]{:S(2)}) copy-start(bf16[256,1024]{1,0:T(8,128)(2,1)} %refs_8_.1) | copy-start | bytes 1572868
  18.6 12.8 %copy-start.4 = (bf16[256,1024]{1,0:T(8,128)(2,1)S(1)}, bf16[256,1024]{1,0:T(8,128)(2,1)}, u32[]{:S(2)}) copy-start(bf16[256,1024]{1,0:T(8,128)(2,1)} %refs_10_.1) | copy-start | bytes 1572868
  18.6 12.8 %copy-start.5 = (bf16[1024,256]{1,0:T(8,128)(2,1)S(1)}, bf16[1024,256]{1,0:T(8,128)(2,1)}, u32[]{:S(2)}) copy-start(bf16[1024,256]{1,0:T(8,128)(2,1)} %refs_12_.1) | copy-start | bytes 1572868
  18.6 12.8 %copy-start.8 = (f32[256]{0:T(256)S(1)}, f32[256]{0:T(256)}, u32[]{:S(2)}) copy-start(f32[256]{0:T(256)} %param.22) | copy-start | bytes 3076
  19.4 5.5 %collective-permute-start.4 = (bf16[256,256]{1,0:T(8,128)(2,1)S(1)}, bf16[256,256]{1,0:T(8,128)(2,1)S(1)}, u32[]{:S(2)}, u32[]{:S(2)}) collective-permute-start(bf16[256,256]{1,0:T(8,128)(2,1)S(1)} %get-tuple-element.23), channel_id=1, source_target_pairs={{0,2},{2,0},{4,6},{6,4},{8,10},{10,8},{12,14},{14,12},{16,18},{18,... | collective-permute-start | bytes 393224 | tf_op jit(solution)/shard_map/ppermute | solution.py:391
  21.0 6.4 %collective-permute-start.5 = (bf16[256,256]{1,0:T(8,128)(2,1)S(1)}, bf16[256,256]{1,0:T(8,128)(2,1)S(1)}, u32[]{:S(2)}, u32[]{:S(2)}) collective-permute-start(bf16[256,256]{1,0:T(8,128)(2,1)S(1)} %get-tuple-element.24), channel_id=1, source_target_pairs={{0,4},{2,6},{4,0},{6,2},{8,12},{10,14},{12,8},{14,10},{16,20},{18,... | collective-permute-start | bytes 393224 | tf_op jit(solution)/shard_map/ppermute | solution.py:391
  25.0 5.9 %collective-permute-start.6 = (bf16[256,256]{1,0:T(8,128)(2,1)S(1)}, bf16[256,256]{1,0:T(8,128)(2,1)S(1)}, u32[]{:S(2)}, u32[]{:S(2)}) collective-permute-start(bf16[256,256]{1,0:T(8,128)(2,1)S(1)} %get-tuple-element.25), channel_id=1, source_target_pairs={{0,6},{2,4},{4,2},{6,0},{8,14},{10,12},{12,10},{14,8},{16,22},{18,... | collective-permute-start | bytes 393224 | tf_op jit(solution)/shard_map/ppermute | solution.py:391
  27.4 18.8 %collective-permute-start.15 = (bf16[1024,256]{1,0:T(8,128)(2,1)S(1)}, bf16[1024,256]{1,0:T(8,128)(2,1)S(1)}, u32[]{:S(2)}, u32[]{:S(2)}) collective-permute-start(bf16[1024,256]{1,0:T(8,128)(2,1)S(1)} %copy-done.2), channel_id=1, source_target_pairs={{0,1},{1,0},{2,3},{3,2},{4,5},{5,4},{6,7},{7,6},{8,9},{9,8},{10,11... | collective-permute-start | bytes 1572872 | tf_op jit(solution)/shard_map/ppermute | solution.py:378
  30.8 15.8 %collective-permute-start.16 = (bf16[256,1024]{1,0:T(8,128)(2,1)S(1)}, bf16[256,1024]{1,0:T(8,128)(2,1)S(1)}, u32[]{:S(2)}, u32[]{:S(2)}) collective-permute-start(bf16[256,1024]{1,0:T(8,128)(2,1)S(1)} %copy-done.9), channel_id=1, source_target_pairs={{0,1},{1,0},{2,3},{3,2},{4,5},{5,4},{6,7},{7,6},{8,9},{9,8},{10,11... | collective-permute-start | bytes 1572872 | tf_op jit(solution)/shard_map/ppermute | solution.py:378
  30.9 15.8 %collective-permute-start.17 = (bf16[256,1024]{1,0:T(8,128)(2,1)S(1)}, bf16[256,1024]{1,0:T(8,128)(2,1)S(1)}, u32[]{:S(2)}, u32[]{:S(2)}) collective-permute-start(bf16[256,1024]{1,0:T(8,128)(2,1)S(1)} %copy-done.10), channel_id=1, source_target_pairs={{0,1},{1,0},{2,3},{3,2},{4,5},{5,4},{6,7},{7,6},{8,9},{9,8},{10,11... | collective-permute-start | bytes 1572872 | tf_op jit(solution)/shard_map/ppermute | solution.py:378
  33.0 13.2 %copy-start = (bf16[256,128]{1,0:T(8,128)(2,1)S(1)}, bf16[256,128]{1,0:T(8,128)(2,1)}, u32[]{:S(2)}) copy-start(bf16[256,128]{1,0:T(8,128)(2,1)} %cot_ref.1) | copy-start | bytes 196612
  33.0 5.5 %collective-permute-start.10 = (bf16[256,256]{1,0:T(8,128)(2,1)S(1)}, bf16[256,256]{1,0:T(8,128)(2,1)S(1)}, u32[]{:S(2)}, u32[]{:S(2)}) collective-permute-start(bf16[256,256]{1,0:T(8,128)(2,1)S(1)} %get-tuple-element.26.refs_0_), channel_id=1, source_target_pairs={{0,2},{2,0},{4,6},{6,4},{8,10},{10,8},{12,14},{14,12},{16,18},{18,... | collective-permute-start | bytes 393224 | tf_op jit(solution)/shard_map/ppermute | solution.py:391
  34.5 6.7 %collective-permute-start.11 = (bf16[256,256]{1,0:T(8,128)(2,1)S(1)}, bf16[256,256]{1,0:T(8,128)(2,1)S(1)}, u32[]{:S(2)}, u32[]{:S(2)}) collective-permute-start(bf16[256,256]{1,0:T(8,128)(2,1)S(1)} %get-tuple-element.26.refs_0_), channel_id=1, source_target_pairs={{0,4},{2,6},{4,0},{6,2},{8,12},{10,14},{12,8},{14,10},{16,20},{18,... | collective-permute-start | bytes 393224 | tf_op jit(solution)/shard_map/ppermute | solution.py:391
  38.5 5.9 %collective-permute-start.12 = (bf16[256,256]{1,0:T(8,128)(2,1)S(1)}, bf16[256,256]{1,0:T(8,128)(2,1)S(1)}, u32[]{:S(2)}, u32[]{:S(2)}) collective-permute-start(bf16[256,256]{1,0:T(8,128)(2,1)S(1)} %get-tuple-element.26.refs_0_), channel_id=1, source_target_pairs={{0,6},{2,4},{4,2},{6,0},{8,14},{10,12},{12,10},{14,8},{16,22},{18,... | collective-permute-start | bytes 393224 | tf_op jit(solution)/shard_map/ppermute | solution.py:391
  41.2 5.5 %copy-start.11 = (f32[256]{0:T(256)S(1)}, f32[256]{0:T(256)}, u32[]{:S(2)}) copy-start(f32[256]{0:T(256)} %param.23) | copy-start | bytes 3076
  44.7 2.0 %collective-permute-start.13 = (f32[128,256]{1,0:T(8,128)S(1)}, f32[128,256]{1,0:T(8,128)S(1)}, u32[]{:S(2)}, u32[]{:S(2)}) collective-permute-start(f32[128,256]{1,0:T(8,128)S(1)} %get-tuple-element.28), channel_id=1, source_target_pairs={{0,1},{1,0},{2,3},{3,2},{4,5},{5,4},{6,7},{7,6},{8,9},{9,8},{10,11... | collective-permute-start | bytes 393224 | tf_op jit(solution)/shard_map/ppermute | solution.py:378
  44.8 1.4 %collective-permute-start.14 = (bf16[128,128]{1,0:T(8,128)(2,1)S(1)}, bf16[128,128]{1,0:T(8,128)(2,1)S(1)}, u32[]{:S(2)}, u32[]{:S(2)}) collective-permute-start(bf16[128,128]{1,0:T(8,128)(2,1)S(1)} %get-tuple-element.29), channel_id=1, source_target_pairs={{0,1},{1,0},{2,3},{3,2},{4,5},{5,4},{6,7},{7,6},{8,9},{9,8},{10,11... | collective-permute-start | bytes 98312 | tf_op jit(solution)/shard_map/ppermute | solution.py:378
  48.5 4.5 %collective-permute-start.18 = (bf16[128,256]{1,0:T(8,128)(2,1)S(1)}, bf16[128,256]{1,0:T(8,128)(2,1)S(1)}, u32[]{:S(2)}, u32[]{:S(2)}) collective-permute-start(bf16[128,256]{1,0:T(8,128)(2,1)S(1)} %shard_map.174.refs_0_), channel_id=1, source_target_pairs={{0,8},{2,10},{4,12},{6,14},{8,0},{10,2},{12,4},{14,6},{16,24},{18,... | collective-permute-start | bytes 196616 | tf_op jit(solution)/shard_map/ppermute | solution.py:384
  50.2 8.3 %collective-permute-start.19 = (bf16[128,256]{1,0:T(8,128)(2,1)S(1)}, bf16[128,256]{1,0:T(8,128)(2,1)S(1)}, u32[]{:S(2)}, u32[]{:S(2)}) collective-permute-start(bf16[128,256]{1,0:T(8,128)(2,1)S(1)} %shard_map.174.refs_0_), channel_id=1, source_target_pairs={{0,16},{2,18},{4,20},{6,22},{8,24},{10,26},{12,28},{14,30},{16,0},... | collective-permute-start | bytes 196616 | tf_op jit(solution)/shard_map/ppermute | solution.py:384
  51.6 6.9 %collective-permute-start.20 = (bf16[128,256]{1,0:T(8,128)(2,1)S(1)}, bf16[128,256]{1,0:T(8,128)(2,1)S(1)}, u32[]{:S(2)}, u32[]{:S(2)}) collective-permute-start(bf16[128,256]{1,0:T(8,128)(2,1)S(1)} %shard_map.174.refs_0_), channel_id=1, source_target_pairs={{0,24},{2,26},{4,28},{6,30},{8,16},{10,18},{12,20},{14,22},{16,8},... | collective-permute-start | bytes 196616 | tf_op jit(solution)/shard_map/ppermute | solution.py:384
  58.6 1.6 %collective-permute-start.21 = (bf16[512,256]{1,0:T(8,128)(2,1)S(1)}, bf16[512,256]{1,0:T(8,128)(2,1)S(1)}, u32[]{:S(2)}, u32[]{:S(2)}) collective-permute-start(bf16[512,256]{1,0:T(8,128)(2,1)S(1)} %pad_maximum_fusion.1), channel_id=1, source_target_pairs={{0,1},{1,0},{2,3},{3,2},{4,5},{5,4},{6,7},{7,6},{8,9},{9,8},{10,11... | collective-permute-start | bytes 786440 | tf_op jit(solution)/shard_map/ppermute | solution.py:378
  60.9 6.0 %collective-permute-start.22 = (bf16[256,256]{1,0:T(8,128)(2,1)S(1)}, bf16[256,256]{1,0:T(8,128)(2,1)S(1)}, u32[]{:S(2)}, u32[]{:S(2)}) collective-permute-start(bf16[256,256]{1,0:T(8,128)(2,1)S(1)} %get-tuple-element.31), channel_id=1, source_target_pairs={{0,2},{2,0},{4,6},{6,4},{8,10},{10,8},{12,14},{14,12},{16,18},{18,... | collective-permute-start | bytes 393224 | tf_op jit(solution)/shard_map/ppermute | solution.py:391
  62.5 8.1 %collective-permute-start.23 = (bf16[256,256]{1,0:T(8,128)(2,1)S(1)}, bf16[256,256]{1,0:T(8,128)(2,1)S(1)}, u32[]{:S(2)}, u32[]{:S(2)}) collective-permute-start(bf16[256,256]{1,0:T(8,128)(2,1)S(1)} %get-tuple-element.32), channel_id=1, source_target_pairs={{0,4},{2,6},{4,0},{6,2},{8,12},{10,14},{12,8},{14,10},{16,20},{18,... | collective-permute-start | bytes 393224 | tf_op jit(solution)/shard_map/ppermute | solution.py:391
  64.0 6.5 %collective-permute-start.24 = (bf16[256,256]{1,0:T(8,128)(2,1)S(1)}, bf16[256,256]{1,0:T(8,128)(2,1)S(1)}, u32[]{:S(2)}, u32[]{:S(2)}) collective-permute-start(bf16[256,256]{1,0:T(8,128)(2,1)S(1)} %get-tuple-element.33), channel_id=1, source_target_pairs={{0,6},{2,4},{4,2},{6,0},{8,14},{10,12},{12,10},{14,8},{16,22},{18,... | collective-permute-start | bytes 393224 | tf_op jit(solution)/shard_map/ppermute | solution.py:391
  70.6 12.1 %copy-start.1 = (f32[256,128]{1,0:T(8,128)S(1)}, f32[256,128]{1,0:T(8,128)}, u32[]{:S(2)}) copy-start(f32[256,128]{1,0:T(8,128)} %rows_ref.1) | copy-start | bytes 393220
  70.6 12.1 %copy-start.6 = (f32[256,128]{1,0:T(8,128)S(1)}, f32[256,128]{1,0:T(8,128)}, u32[]{:S(2)}) copy-start(f32[256,128]{1,0:T(8,128)} %first_ref.1) | copy-start | bytes 393220
  70.6 12.1 %copy-start.7 = (f32[256,128]{1,0:T(8,128)S(1)}, f32[256,128]{1,0:T(8,128)}, u32[]{:S(2)}) copy-start(f32[256,128]{1,0:T(8,128)} %second_ref.1) | copy-start | bytes 393220
  72.3 6.0 %collective-permute-start.25 = (bf16[256,256]{1,0:T(8,128)(2,1)S(1)}, bf16[256,256]{1,0:T(8,128)(2,1)S(1)}, u32[]{:S(2)}, u32[]{:S(2)}) collective-permute-start(bf16[256,256]{1,0:T(8,128)(2,1)S(1)} %shard_map.176.refs_0_), channel_id=1, source_target_pairs={{0,2},{2,0},{4,6},{6,4},{8,10},{10,8},{12,14},{14,12},{16,18},{18,... | collective-permute-start | bytes 393224 | tf_op jit(solution)/shard_map/ppermute | solution.py:391
  73.6 7.2 %collective-permute-start.26 = (bf16[256,256]{1,0:T(8,128)(2,1)S(1)}, bf16[256,256]{1,0:T(8,128)(2,1)S(1)}, u32[]{:S(2)}, u32[]{:S(2)}) collective-permute-start(bf16[256,256]{1,0:T(8,128)(2,1)S(1)} %shard_map.176.refs_0_), channel_id=1, source_target_pairs={{0,4},{2,6},{4,0},{6,2},{8,12},{10,14},{12,8},{14,10},{16,20},{18,... | collective-permute-start | bytes 393224 | tf_op jit(solution)/shard_map/ppermute | solution.py:391
  74.5 6.4 %collective-permute-start.27 = (bf16[256,256]{1,0:T(8,128)(2,1)S(1)}, bf16[256,256]{1,0:T(8,128)(2,1)S(1)}, u32[]{:S(2)}, u32[]{:S(2)}) collective-permute-start(bf16[256,256]{1,0:T(8,128)(2,1)S(1)} %shard_map.176.refs_0_), channel_id=1, source_target_pairs={{0,6},{2,4},{4,2},{6,0},{8,14},{10,12},{12,10},{14,8},{16,22},{18,... | collective-permute-start | bytes 393224 | tf_op jit(solution)/shard_map/ppermute | solution.py:391
  81.2 1.4 %collective-permute-start.28 = (f32[256,128]{1,0:T(8,128)S(1)}, f32[256,128]{1,0:T(8,128)S(1)}, u32[]{:S(2)}, u32[]{:S(2)}) collective-permute-start(f32[256,128]{1,0:T(8,128)S(1)} %get-tuple-element.38), channel_id=1, source_target_pairs={{0,1},{1,0},{2,3},{3,2},{4,5},{5,4},{6,7},{7,6},{8,9},{9,8},{10,11... | collective-permute-start | bytes 393224 | tf_op jit(solution)/shard_map/ppermute | solution.py:378

commit v3 on v2

--- a/solution.py
+++ b/solution.py
@@ -70,6 +70,7 @@
     rows_hbm,
     cot_hbm,
     pack_ref,
+    inc_ref,
     send_ref,
     dest_ref,
     item_ref,
@@ -118,6 +119,7 @@
         meta = jnp.where(lanes == t, slot, meta)
         meta = jnp.where(lanes == tiles + t, item_ref[t], meta)
     pack_ref[items + 2 * half :, :] = meta.astype(F32).astype(BF16)
+    inc_ref[...] = pack_ref[items:, :]
     copies[3].wait()
     pack_ref[0:items, :] = rows_ref[...].astype(BF16)
     copies[4].wait()
@@ -143,28 +145,32 @@
         ]
 
 
-def masks_body(idx_ref, *refs, members, half, items, tiles):
-    packs = refs[:members]
-    spread_ref, mt_ref = refs[members:]
+def masks_body(idx_ref, *refs, per, half, items, tiles, own):
+    incs = refs[:-2]
+    spread_ref, mt_ref = refs[-2:]
+    first = incs[0].shape[0] - 2 * half - 16
     mt_ref[...] = jnp.zeros_like(mt_ref)
     byte_rows = jnp.concatenate(
         [
             jnp.concatenate(
-                [p[items : items + half, :], p[items + half : items + 2 * half, :]], axis=1
+                [p[first : first + half, :], p[first + half : first + 2 * half, :]], axis=1
             )
-            for p in packs
+            for p in incs
         ],
         axis=0,
     )
-    shift = lax.broadcasted_iota(jnp.int32, (members * half, 2 * BLOCK), 1) % 8
+    shift = lax.broadcasted_iota(jnp.int32, (len(incs) * half, 2 * BLOCK), 1) % 8
     for q in range(tiles // 2):
         spread = dot(byte_rows, spread_ref[:, q * 2 * BLOCK : (q + 1) * 2 * BLOCK])
         bits = jnp.right_shift(spread.astype(jnp.int32), shift) & 1
         mask = bits.astype(F32).astype(BF16)
-        for l in range(members):
+        for l in range(len(incs)):
             for b in range(2):
                 t = 2 * q + b
-                row = pl.multiple_of(idx_ref[l, t] * half, half)
+                slot = idx_ref[l, t]
+                if own:
+                    slot = jnp.where(slot // per == l, slot % per, per)
+                row = pl.multiple_of(slot * half, half)
                 lane = pl.multiple_of(idx_ref[l, tiles + t] * BLOCK + l * items, BLOCK)
                 where = (pl.ds(row, half), pl.ds(lane, BLOCK))
                 mt_ref[where] = (
@@ -185,10 +191,9 @@
         out_refs[i][...] = total.astype(out_refs[i].dtype)
 
 
-def turn_body(mt_ref, out_ref, *, items):
-    for c in range(mt_ref.shape[0] // BLOCK):
-        block = mt_ref[c * BLOCK : (c + 1) * BLOCK, 0:items].astype(F32)
-        out_ref[:, c * BLOCK : (c + 1) * BLOCK] = block.T.astype(BF16)
+def turn_body(mt_ref, out_ref):
+    for c in range(0, out_ref.shape[1], BLOCK):
+        out_ref[:, c : c + BLOCK] = mt_ref[c : c + BLOCK, :].astype(F32).T.astype(BF16)
 
 
 def item_hidden_body(mine_ref, other_ref, down_a, down_b, hid_ref, cot_ref):
@@ -241,22 +246,27 @@
     out_ref[...] = acc.astype(BF16)
 
 
-def message_body(mo_ref, *refs, groups):
-    parts = refs[:groups]
-    mine_ref, theirs_ref, all_ref = refs[groups:]
-    per = parts[0].shape[0]
-    total = dot(mo_ref[:, 0:per], parts[0][...])
-    for i in range(1, groups):
-        total = total + dot(mo_ref[:, i * per : (i + 1) * per], parts[i][...])
-    all_ref[...] = total
-    rows = mine_ref.shape[0]
+def message_body(mo_ref, out_ref, mine_ref, theirs_ref, all_ref, *, peers):
+    all_ref[...] = dot(mo_ref[...], out_ref[...])
+    rows = mine_ref.shape[0] // peers
     core = lax.axis_index("mp")
-    mine_ref[...] = all_ref[pl.ds(pl.multiple_of(core * rows, rows), rows), :]
-    theirs_ref[...] = all_ref[pl.ds(pl.multiple_of((1 - core) * rows, rows), rows), :]
-
-
-def item_body(mine_ref, other_ref, hidden_ref, gain_ref, gate_a, gate_b, up_a, up_b, out_ref):
-    message = mine_ref[...] + other_ref[...]
+    for l in range(peers):
+        mine = pl.multiple_of((2 * l + core) * rows, rows)
+        theirs = pl.multiple_of((2 * l + 1 - core) * rows, rows)
+        mine_ref[l * rows : (l + 1) * rows, :] = all_ref[pl.ds(mine, rows), :]
+        theirs_ref[l * rows : (l + 1) * rows, :] = all_ref[pl.ds(theirs, rows), :].astype(BF16)
+
+
+def join_body(mine_ref, other_ref, *out_refs):
+    rows = out_refs[0].shape[0]
+    for l, out in enumerate(out_refs):
+        at = slice(l * rows, (l + 1) * rows)
+        out[...] = (mine_ref[at, :] + other_ref[at, :].astype(F32)).astype(out.dtype)
+
+
+def item_body(*refs, peers):
+    hidden_ref, gain_ref, gate_a, gate_b, up_a, up_b, out_ref = refs[peers:]
+    message = add_all(refs[:peers])
     scale = rms(message)
     gain = gain_ref[...]
     query = (message * scale * gain).astype(BF16)
@@ -323,22 +333,18 @@
     out_ref[...] = (scale * weighted - total * (cubed * inner)).astype(BF16)
 
 
-def back_body(mo_ref, *refs, groups):
-    parts = refs[:groups]
-    mine_ref, theirs_ref, all_ref = refs[groups:]
-    per = parts[0].shape[0]
-    total = dot(mo_ref[:, 0:per], parts[0][...])
-    for i in range(1, groups):
-        total = total + dot(mo_ref[:, i * per : (i + 1) * per], parts[i][...])
-    all_ref[...] = total
+def back_body(mo_ref, sum_ref, mine_ref, theirs_ref, all_ref):
+    all_ref[...] = dot(mo_ref[...], sum_ref[...])
     width = mine_ref.shape[1]
     core = lax.axis_index("mp")
     mine_ref[...] = all_ref[:, pl.ds(pl.multiple_of(core * width, width), width)]
-    theirs_ref[...] = all_ref[:, pl.ds(pl.multiple_of((1 - core) * width, width), width)]
-
-
-def adam_body(back_ref, other_ref, cot_ref, rows_ref, first_ref, second_ref, r_ref, f_ref, s_ref):
-    gradient = cot_ref[...].astype(F32) + (back_ref[...] + other_ref[...])
+    theirs = all_ref[:, pl.ds(pl.multiple_of((1 - core) * width, width), width)]
+    theirs_ref[...] = theirs.astype(BF16)
+
+
+def adam_body(*refs, peers):
+    cot_ref, rows_ref, first_ref, second_ref, r_ref, f_ref, s_ref = refs[peers:]
+    gradient = cot_ref[...].astype(F32) + add_all(refs[:peers])
     first = BETA_FIRST * first_ref[...] + (1.0 - BETA_FIRST) * gradient
     second = BETA_SECOND * second_ref[...] + (1.0 - BETA_SECOND) * gradient * gradient
     f_ref[...] = first
@@ -385,15 +391,19 @@
         return got
 
     def exchange(xs):
-        got = []
+        got = [xs[0]]
         for k in range(1, groups):
             pairs = [(s, (s // groups) * groups + ((s % groups) ^ k)) for s in range(shards)]
-            got.append(lax.ppermute(xs[k - 1], "shard", pairs))
+            got.append(lax.ppermute(xs[k], "shard", pairs))
         return got
 
-    pack, cot_send = run(
+    pack, inc, cot_send = run(
         functools.partial(pack_body, half=half, members=members, groups=groups),
-        [sds((items + 2 * half + 16, width), BF16), sds((item_half, width), BF16)],
+        [
+            sds((items + 2 * half + 16, width), BF16),
+            sds((2 * half + 16, width), BF16),
+            sds((item_half, width), BF16),
+        ],
         (),
         (),
         far=(tile_dest, tile_item, tile_bits.reshape(tiles * words, BLOCK), item_rows, item_cot),
@@ -414,12 +424,17 @@
     gate_b, up_b, down_b = gate_basket, up_basket, down_basket
     gate_bo, up_bo, down_bo = swap(gate_basket), swap(up_basket), swap(down_basket)
     rows_other = swap(jnp.concatenate([q[:items] for q in packs], axis=0))
+    incs = exchange([inc] * groups)
     metas = [q[items + 2 * half : items + 2 * half + 1] for q in packs]
     idx = jnp.concatenate(metas, axis=0).astype(jnp.int32)
+    metas = [q[2 * half : 2 * half + 1] for q in incs]
+    idx_plane = jnp.concatenate(metas, axis=0).astype(jnp.int32)
 
     part_shapes = [sds((per, features), F32)] + [sds((per, features), BF16)] * (groups - 1)
     mt = run(
-        functools.partial(masks_body, members=members, half=half, items=items, tiles=tiles),
+        functools.partial(
+            masks_body, per=members, half=half, items=items, tiles=tiles, own=False
+        ),
         sds((shards * half, members * items), BF16),
         (idx,),
         (*packs, spread),
@@ -433,14 +448,17 @@
         scratch=[pltpu.VMEM((members * items, features), BF16)],
         flops=1 << 29,
     )
-    received = exchange(parts[1:])
-    mo = run(
-        functools.partial(turn_body, items=items),
-        sds((items, shards * half), BF16),
-        (),
-        (mt,),
+    received = exchange(parts)
+    mt_plane = run(
+        functools.partial(
+            masks_body, per=members, half=half, items=items, tiles=tiles, own=True
+        ),
+        sds(((members + 1) * half, groups * items), BF16),
+        (idx_plane,),
+        (*incs, spread),
         flops=1 << 29,
     )
+    mo = run(turn_body, sds((groups * items, per), BF16), (), (mt_plane,), flops=1 << 28)
     gate_io, up_io, down_io = swap(gate_item), swap(up_item), swap(down_item)
     basket_out, basket_sum, value, slope = run(
         functools.partial(basket_body, groups=groups),
@@ -452,7 +470,6 @@
         ],
         (),
         (
-            parts[0],
             *received,
             basket_gain.reshape(1, features),
             gate_b,
@@ -464,7 +481,15 @@
         ),
         flops=1 << 30,
     )
-    outs = [basket_out] + exchange([basket_out] * (groups - 1))
+    message_mine, message_theirs = run(
+        functools.partial(message_body, peers=groups),
+        [sds((groups * item_half, features), F32), sds((groups * item_half, features), BF16)],
+        (),
+        (mo, basket_out),
+        scratch=[pltpu.VMEM((groups * items, features), F32)],
+        flops=1 << 28,
+    )
+    message_other = swap(message_theirs)
     item_hidden = run(
         item_hidden_body,
         sds((item_half, hidden), F32),
@@ -473,22 +498,18 @@
         scratch=[pltpu.VMEM((item_half, features), BF16)],
         flops=1 << 29,
     )
-    message_mine, message_theirs = run(
-        functools.partial(message_body, groups=groups),
-        [sds((item_half, features), F32)] * 2,
-        (),
-        (mo, *outs),
-        scratch=[pltpu.VMEM((items, features), F32)],
-        flops=1 << 28,
-    )
-    message_other = swap(message_theirs)
+    messages = run(
+        join_body,
+        [sds((item_half, features), F32)] + [sds((item_half, features), BF16)] * (groups - 1),
+        (),
+        (message_mine, message_other),
+    )
     grad_message = run(
-        item_body,
+        functools.partial(item_body, peers=groups),
         sds((item_half, features), BF16),
         (),
         (
-            message_mine,
-            message_other,
+            *exchange(messages),
             item_hidden,
             item_gain.reshape(1, features),
             gate_item,
@@ -508,13 +529,12 @@
         scratch=[pltpu.VMEM((members * items, features), BF16)],
         flops=1 << 29,
     )
-    grad_received = exchange(grad_parts[1:])
+    grad_received = exchange(grad_parts)
     grad_sum = run(
         functools.partial(basket_back_body, groups=groups),
         sds((per, features), BF16),
         (),
         (
-            grad_parts[0],
             *grad_received,
             basket_sum,
             value,
@@ -529,21 +549,26 @@
         ),
         flops=1 << 30,
     )
-    sums = [grad_sum] + exchange([grad_sum] * (groups - 1))
     back_mine, back_theirs = run(
-        functools.partial(back_body, groups=groups),
-        [sds((items, width), F32)] * 2,
-        (),
-        (mo, *sums),
-        scratch=[pltpu.VMEM((items, features), F32)],
+        back_body,
+        [sds((groups * items, width), F32), sds((groups * items, width), BF16)],
+        (),
+        (mo, grad_sum),
+        scratch=[pltpu.VMEM((groups * items, features), F32)],
         flops=1 << 28,
     )
     back_other = swap(back_theirs)
+    backs = run(
+        join_body,
+        [sds((items, width), F32)] + [sds((items, width), BF16)] * (groups - 1),
+        (),
+        (back_mine, back_other),
+    )
     new_rows, new_first, new_second = run(
-        adam_body,
+        functools.partial(adam_body, peers=groups),
         [sds((items, width), F32)] * 3,
         (),
-        (back_mine, back_other, item_cot, item_rows, first_moment, second_moment),
+        (*exchange(backs), item_cot, item_rows, first_moment, second_moment),
     )
     return (new_rows, new_first, new_second)
 

time: 83.6 us -> 84.2 us (level)
  waiting for transfers between devices: 40 us -> 37 us
  starting transfers between devices: 30.6 us -> 32.5 us
  Pallas kernels: 11.7 us -> 13.3 us
    ppermute x12 -> x15, waiting for transfers between devices: 22.5 us -> 20.1 us  [exchange(): got.append(lax.ppermute(xs[k], 'shard', pairs))]
    ppermute x12 -> x15, starting transfers between devices: 18.2 us -> 20.1 us  [exchange(): got.append(lax.ppermute(xs[k], 'shard', pairs))]
    pallas_call x13 -> x16, Pallas kernels: 11.7 us -> 13.3 us  [run(): return call(*far, *smem, *args)]
    ppermute x6, waiting for transfers between devices: 13.7 us -> 12.8 us  [gather(): got.append(lax.ppermute(x, 'shard', pairs))]
  transfers between devices with their start and end apart: 29 -> 32, of which waited for: 14 -> 23; matrix products, arithmetic and copies ran while one was open for 0% -> 0% of each run, Pallas kernels for 6% -> 8%
where the time goes in v3:
time: 84.2 us; the launch traced here: 84 us
  waiting for transfers between devices  37 us (44%)
  starting transfers between devices  32.5 us (39%)
  Pallas kernels  13.3 us (16%)
  between operations  0.99 us (1%)
    ppermute x15, waiting for transfers between devices, exchange(): got.append(lax.ppermute(xs[k], 'shard', pairs))  20.1 us
    ppermute x15, starting transfers between devices, exchange(): got.append(lax.ppermute(xs[k], 'shard', pairs))  20.1 us
    pallas_call x16, Pallas kernels, run(): return call(*far, *smem, *args)  13.3 us
    ppermute x6, waiting for transfers between devices, gather(): got.append(lax.ppermute(x, 'shard', pairs))  12.8 us
    ppermute x6, starting transfers between devices, gather(): got.append(lax.ppermute(x, 'shard', pairs))  10.2 us
    ppermute x11, waiting for transfers between devices, swap(): return lax.ppermute(x, 'mp', [(0, 1), (1, 0)])  4.09 us
    ppermute x11, starting transfers between devices, swap(): return lax.ppermute(x, 'mp', [(0, 1), (1, 0)])  2.3 us
  transfers between devices with their start and end apart: 32, of which 23 were waited for; matrix products, arithmetic and copies ran while one was open for 0% of the time, Pallas kernels for 8%

profile of v3, /device:TPU:0, one launch (start us, length us, event | category | flops | bytes accessed | tf_op | source)
XLA Modules:
  0.0 84.0 jit_solution(1469654415439295789)
XLA Ops:
  0.6 1.2 %shard_map.166 = (bf16[400,128]{1,0:T(8,128)(2,1)S(1)}, bf16[144,128]{1,0:T(8,128)(2,1)S(1)}, bf16[128,128]{1,0:T(8,128)(2,1)S(1)}) custom-call(s32[16]{0:T(128)} %dest_hbm.1, s32[16]{0:T(128)} %item_hbm.1, s32[128,128]{1,0:T(8,128)} %bitcast.6, f32[256,128]{1,0:T(8,128)} %refs_5_.3, bf16[256,128]{1,0:T(8,128)(2,1)} %refs_4_.1), custom_call_target="tpu_custom_call" | custom-call | flops 1048576 | bytes 1048576 | tf_op jit(solution)/shard_map/pallas_call | solution.py:51
  1.8 3.1 %collective-permute-start.3 = (bf16[400,128]{1,0:T(8,128)(2,1)S(1)}, bf16[400,128]{1,0:T(8,128)(2,1)S(1)}, u32[]{:S(2)}, u32[]{:S(2)}) collective-permute-start(bf16[400,128]{1,0:T(8,128)(2,1)S(1)} %get-tuple-element.31.pack_ref.refs_0_), channel_id=1, source_target_pairs={{0,8},{2,10},{4,12},{6,14},{8,0},{10,2},{12,4},{14,6},{16,24},{18,... | collective-permute-start | bytes 307208 | tf_op jit(solution)/shard_map/ppermute | solution.py:390
  4.9 2.6 %collective-permute-start.4 = (bf16[400,128]{1,0:T(8,128)(2,1)S(1)}, bf16[400,128]{1,0:T(8,128)(2,1)S(1)}, u32[]{:S(2)}, u32[]{:S(2)}) collective-permute-start(bf16[400,128]{1,0:T(8,128)(2,1)S(1)} %get-tuple-element.31.pack_ref.refs_0_), channel_id=1, source_target_pairs={{0,16},{2,18},{4,20},{6,22},{8,24},{10,26},{12,28},{14,30},{16,0},... | collective-permute-start | bytes 307208 | tf_op jit(solution)/shard_map/ppermute | solution.py:390
  7.8 7.8 %collective-permute-done.4.refs_2_ = bf16[400,128]{1,0:T(8,128)(2,1)S(1)} collective-permute-done((bf16[400,128]{1,0:T(8,128)(2,1)S(1)}, bf16[400,128]{1,0:T(8,128)(2,1)S(1)}, u32[]{:S(2)}, u32[]{:S(2)}) %collective-permute-start.4) | collective-permute-done | bytes 102432 | tf_op jit(solution)/shard_map/ppermute | solution.py:390
  15.8 0.5 collective-permute-start.10
  16.8 1.5 %collective-permute-start = (bf16[144,128]{1,0:T(8,128)(2,1)S(1)}, bf16[144,128]{1,0:T(8,128)(2,1)S(1)}, u32[]{:S(2)}, u32[]{:S(2)}) collective-permute-start(bf16[144,128]{1,0:T(8,128)(2,1)S(1)} %get-tuple-element.30.refs_0_), channel_id=1, source_target_pairs={{0,2},{2,0},{4,6},{6,4},{8,10},{10,8},{12,14},{14,12},{16,18},{18,... | collective-permute-start | bytes 110600 | tf_op jit(solution)/shard_map/ppermute | solution.py:397
  18.5 1.5 %shard_map.170.mt_ref = bf16[1024,1024]{1,0:T(8,128)(2,1)S(1)} custom-call(s32[4,128]{1,0:T(4,128)S(1)} %maximum_convert_fusion.1.idx_ref, bf16[400,128]{1,0:T(8,128)(2,1)S(1)} %get-tuple-element.31.pack_ref.refs_0_, bf16[400,128]{1,0:T(8,128)(2,1)S(1)} %collective-permute-done.3.refs_1_, bf16[400,128]{1,0:T(8,128)(2,1)S(1)} %collective-permute-done.4.refs_2_, ...), custom_call_target="tpu_custom_call" | custom-call | flops 536870912 | bytes 1048576 | tf_op jit(solution)/shard_map/pallas_call | solution.py:51
  20.1 0.7 collective-permute-done.refs_1_
  20.7 1.5 %collective-permute-start.1 = (bf16[144,128]{1,0:T(8,128)(2,1)S(1)}, bf16[144,128]{1,0:T(8,128)(2,1)S(1)}, u32[]{:S(2)}, u32[]{:S(2)}) collective-permute-start(bf16[144,128]{1,0:T(8,128)(2,1)S(1)} %get-tuple-element.30.refs_0_), channel_id=1, source_target_pairs={{0,4},{2,6},{4,0},{6,2},{8,12},{10,14},{12,8},{14,10},{16,20},{18,... | collective-permute-start | bytes 110600 | tf_op jit(solution)/shard_map/ppermute | solution.py:397
  22.3 1.4 %collective-permute-start.2 = (bf16[144,128]{1,0:T(8,128)(2,1)S(1)}, bf16[144,128]{1,0:T(8,128)(2,1)S(1)}, u32[]{:S(2)}, u32[]{:S(2)}) collective-permute-start(bf16[144,128]{1,0:T(8,128)(2,1)S(1)} %get-tuple-element.30.refs_0_), channel_id=1, source_target_pairs={{0,6},{2,4},{4,2},{6,0},{8,14},{10,12},{12,10},{14,8},{16,22},{18,... | collective-permute-start | bytes 110600 | tf_op jit(solution)/shard_map/ppermute | solution.py:397
  23.7 0.8 shard_map.171
  24.7 1.9 %collective-permute-start.7 = (bf16[256,256]{1,0:T(8,128)(2,1)S(1)}, bf16[256,256]{1,0:T(8,128)(2,1)S(1)}, u32[]{:S(2)}, u32[]{:S(2)}) collective-permute-start(bf16[256,256]{1,0:T(8,128)(2,1)S(1)} %get-tuple-element.33), channel_id=1, source_target_pairs={{0,2},{2,0},{4,6},{6,4},{8,10},{10,8},{12,14},{14,12},{16,18},{18,... | collective-permute-start | bytes 393224 | tf_op jit(solution)/shard_map/ppermute | solution.py:397
  26.6 0.9 %collective-permute-done.2.refs_3_ = bf16[144,128]{1,0:T(8,128)(2,1)S(1)} collective-permute-done((bf16[144,128]{1,0:T(8,128)(2,1)S(1)}, bf16[144,128]{1,0:T(8,128)(2,1)S(1)}, u32[]{:S(2)}, u32[]{:S(2)}) %collective-permute-start.2) | collective-permute-done | bytes 36896 | tf_op jit(solution)/shard_map/ppermute | solution.py:397
  27.5 0.5 collective-permute-start.8
  28.0 1.7 %collective-permute-done.7.refs_1_ = bf16[256,256]{1,0:T(8,128)(2,1)S(1)} collective-permute-done((bf16[256,256]{1,0:T(8,128)(2,1)S(1)}, bf16[256,256]{1,0:T(8,128)(2,1)S(1)}, u32[]{:S(2)}, u32[]{:S(2)}) %collective-permute-start.7) | collective-permute-done | bytes 131104 | tf_op jit(solution)/shard_map/ppermute | solution.py:397
  29.7 2.6 %collective-permute-start.9 = (bf16[256,256]{1,0:T(8,128)(2,1)S(1)}, bf16[256,256]{1,0:T(8,128)(2,1)S(1)}, u32[]{:S(2)}, u32[]{:S(2)}) collective-permute-start(bf16[256,256]{1,0:T(8,128)(2,1)S(1)} %get-tuple-element.35), channel_id=1, source_target_pairs={{0,6},{2,4},{4,2},{6,0},{8,14},{10,12},{12,10},{14,8},{16,22},{18,... | collective-permute-start | bytes 393224 | tf_op jit(solution)/shard_map/ppermute | solution.py:397
  32.3 1.5 %collective-permute-done.8.refs_2_ = bf16[256,256]{1,0:T(8,128)(2,1)S(1)} collective-permute-done((bf16[256,256]{1,0:T(8,128)(2,1)S(1)}, bf16[256,256]{1,0:T(8,128)(2,1)S(1)}, u32[]{:S(2)}, u32[]{:S(2)}) %collective-permute-start.8) | collective-permute-done | bytes 131104 | tf_op jit(solution)/shard_map/ppermute | solution.py:397
  33.8 1.7 %collective-permute-done.9.refs_3_ = bf16[256,256]{1,0:T(8,128)(2,1)S(1)} collective-permute-done((bf16[256,256]{1,0:T(8,128)(2,1)S(1)}, bf16[256,256]{1,0:T(8,128)(2,1)S(1)}, u32[]{:S(2)}, u32[]{:S(2)}) %collective-permute-start.9) | collective-permute-done | bytes 131104 | tf_op jit(solution)/shard_map/ppermute | solution.py:397
  35.6 0.5 collective-permute-start.20
  36.1 1.4 %shard_map.168.mt_ref = bf16[320,1024]{1,0:T(8,128)(2,1)S(1)} custom-call(s32[4,128]{1,0:T(4,128)S(1)} %maximum_convert_fusion.idx_ref, bf16[144,128]{1,0:T(8,128)(2,1)S(1)} %get-tuple-element.30.refs_0_, bf16[144,128]{1,0:T(8,128)(2,1)S(1)} %collective-permute-done.refs_1_, bf16[144,128]{1,0:T(8,128)(2,1)S(1)} %collective-permute-done.1.refs_2_, ...), custom_call_target="tpu_custom_call" | custom-call | flops 536870912 | bytes 1048576 | tf_op jit(solution)/shard_map/pallas_call | solution.py:51
  37.8 1.6 %shard_map.172 = (bf16[256,256]{1,0:T(8,128)(2,1)S(1)}, f32[256,256]{1,0:T(8,128)S(1)}, bf16[256,2048]{1,0:T(8,128)(2,1)S(1)}, bf16[256,2048]{1,0:T(8,128)(2,1)S(1)}) custom-call(f32[256,256]{1,0:T(8,128)S(1)} %get-tuple-element.32.refs_0_, bf16[256,256]{1,0:T(8,128)(2,1)S(1)} %collective-permute-done.7.refs_1_, ...), custom_call_target="tpu_custom_call" | custom-call | flops 1073741824 | bytes 1048576 | tf_op jit(solution)/shard_map/pallas_call | solution.py:51
  40.3 1.0 %collective-permute-done.13.other_ref = bf16[512,256]{1,0:T(8,128)(2,1)S(1)} collective-permute-done((bf16[512,256]{1,0:T(8,128)(2,1)S(1)}, bf16[512,256]{1,0:T(8,128)(2,1)S(1)}, u32[]{:S(2)}, u32[]{:S(2)}) %collective-permute-start.13) | collective-permute-done | bytes 262176 | tf_op jit(solution)/shard_map/ppermute | solution.py:384
  41.4 1.9 %collective-permute-start.14 = (bf16[128,256]{1,0:T(8,128)(2,1)S(1)}, bf16[128,256]{1,0:T(8,128)(2,1)S(1)}, u32[]{:S(2)}, u32[]{:S(2)}) collective-permute-start(bf16[128,256]{1,0:T(8,128)(2,1)S(1)} %get-tuple-element.40), channel_id=1, source_target_pairs={{0,2},{2,0},{4,6},{6,4},{8,10},{10,8},{12,14},{14,12},{16,18},{18,... | collective-permute-start | bytes 196616 | tf_op jit(solution)/shard_map/ppermute | solution.py:397
  43.4 1.3 %collective-permute-start.15 = (bf16[128,256]{1,0:T(8,128)(2,1)S(1)}, bf16[128,256]{1,0:T(8,128)(2,1)S(1)}, u32[]{:S(2)}, u32[]{:S(2)}) collective-permute-start(bf16[128,256]{1,0:T(8,128)(2,1)S(1)} %get-tuple-element.41), channel_id=1, source_target_pairs={{0,4},{2,6},{4,0},{6,2},{8,12},{10,14},{12,8},{14,10},{16,20},{18,... | collective-permute-start | bytes 196616 | tf_op jit(solution)/shard_map/ppermute | solution.py:397
  45.8 1.9 %collective-permute-done.15.refs_2_ = bf16[128,256]{1,0:T(8,128)(2,1)S(1)} collective-permute-done((bf16[128,256]{1,0:T(8,128)(2,1)S(1)}, bf16[128,256]{1,0:T(8,128)(2,1)S(1)}, u32[]{:S(2)}, u32[]{:S(2)}) %collective-permute-start.15) | collective-permute-done | bytes 65568 | tf_op jit(solution)/shard_map/ppermute | solution.py:397
  47.6 2.2 %collective-permute-done.16.refs_3_ = bf16[128,256]{1,0:T(8,128)(2,1)S(1)} collective-permute-done((bf16[128,256]{1,0:T(8,128)(2,1)S(1)}, bf16[128,256]{1,0:T(8,128)(2,1)S(1)}, u32[]{:S(2)}, u32[]{:S(2)}) %collective-permute-start.16) | collective-permute-done | bytes 65568 | tf_op jit(solution)/shard_map/ppermute | solution.py:397
  49.8 1.8 %shard_map.176.refs_0_ = bf16[128,256]{1,0:T(8,128)(2,1)S(1)} custom-call(f32[128,256]{1,0:T(8,128)S(1)} %get-tuple-element.39.refs_0_, bf16[128,256]{1,0:T(8,128)(2,1)S(1)} %collective-permute-done.14.refs_1_, bf16[128,256]{1,0:T(8,128)(2,1)S(1)} %collective-permute-done.15.refs_2_, bf16[128,256]{1,0:T(8,128)(2,1)S(1)} %collective-permute-done.16.refs_3_, ...), custom_call_target="tpu_custom_call" | custom-call | flops 1073741824 | bytes 1048576 | tf_op jit(solution)/shard_map/pallas_call | solution.py:51
  51.6 1.7 %collective-permute-start.21 = (bf16[128,256]{1,0:T(8,128)(2,1)S(1)}, bf16[128,256]{1,0:T(8,128)(2,1)S(1)}, u32[]{:S(2)}, u32[]{:S(2)}) collective-permute-start(bf16[128,256]{1,0:T(8,128)(2,1)S(1)} %shard_map.176.refs_0_), channel_id=1, source_target_pairs={{0,8},{2,10},{4,12},{6,14},{8,0},{10,2},{12,4},{14,6},{16,24},{18,... | collective-permute-start | bytes 196616 | tf_op jit(solution)/shard_map/ppermute | solution.py:390
  53.3 1.4 %collective-permute-start.22 = (bf16[128,256]{1,0:T(8,128)(2,1)S(1)}, bf16[128,256]{1,0:T(8,128)(2,1)S(1)}, u32[]{:S(2)}, u32[]{:S(2)}) collective-permute-start(bf16[128,256]{1,0:T(8,128)(2,1)S(1)} %shard_map.176.refs_0_), channel_id=1, source_target_pairs={{0,16},{2,18},{4,20},{6,22},{8,24},{10,26},{12,28},{14,30},{16,0},... | collective-permute-start | bytes 196616 | tf_op jit(solution)/shard_map/ppermute | solution.py:390
  54.7 1.4 %collective-permute-start.23 = (bf16[128,256]{1,0:T(8,128)(2,1)S(1)}, bf16[128,256]{1,0:T(8,128)(2,1)S(1)}, u32[]{:S(2)}, u32[]{:S(2)}) collective-permute-start(bf16[128,256]{1,0:T(8,128)(2,1)S(1)} %shard_map.176.refs_0_), channel_id=1, source_target_pairs={{0,24},{2,26},{4,28},{6,30},{8,16},{10,18},{12,20},{14,22},{16,8},... | collective-permute-start | bytes 196616 | tf_op jit(solution)/shard_map/ppermute | solution.py:390
  56.3 3.0 %collective-permute-done.22.refs_2_ = bf16[128,256]{1,0:T(8,128)(2,1)S(1)} collective-permute-done((bf16[128,256]{1,0:T(8,128)(2,1)S(1)}, bf16[128,256]{1,0:T(8,128)(2,1)S(1)}, u32[]{:S(2)}, u32[]{:S(2)}) %collective-permute-start.22) | collective-permute-done | bytes 65568 | tf_op jit(solution)/shard_map/ppermute | solution.py:390
  59.3 1.5 %collective-permute-done.23.refs_3_ = bf16[128,256]{1,0:T(8,128)(2,1)S(1)} collective-permute-done((bf16[128,256]{1,0:T(8,128)(2,1)S(1)}, bf16[128,256]{1,0:T(8,128)(2,1)S(1)}, u32[]{:S(2)}, u32[]{:S(2)}) %collective-permute-start.23) | collective-permute-done | bytes 65568 | tf_op jit(solution)/shard_map/ppermute | solution.py:390
  60.9 1.5 %collective-permute-done.24.refs_4_ = bf16[512,256]{1,0:T(8,128)(2,1)S(1)} collective-permute-done((bf16[512,256]{1,0:T(8,128)(2,1)S(1)}, bf16[512,256]{1,0:T(8,128)(2,1)S(1)}, u32[]{:S(2)}, u32[]{:S(2)}) %collective-permute-start.24) | collective-permute-done | bytes 262176 | tf_op jit(solution)/shard_map/ppermute | solution.py:384
  62.4 0.7 shard_map.177
  63.2 0.6 collective-permute-start.25
  63.7 0.5 collective-permute-start.26
  64.3 2.5 %collective-permute-start.27 = (bf16[256,256]{1,0:T(8,128)(2,1)S(1)}, bf16[256,256]{1,0:T(8,128)(2,1)S(1)}, u32[]{:S(2)}, u32[]{:S(2)}) collective-permute-start(bf16[256,256]{1,0:T(8,128)(2,1)S(1)} %get-tuple-element.47), channel_id=1, source_target_pairs={{0,6},{2,4},{4,2},{6,0},{8,14},{10,12},{12,10},{14,8},{16,22},{18,... | collective-permute-start | bytes 393224 | tf_op jit(solution)/shard_map/ppermute | solution.py:397
  66.7 2.9 %collective-permute-done.25.refs_1_ = bf16[256,256]{1,0:T(8,128)(2,1)S(1)} collective-permute-done((bf16[256,256]{1,0:T(8,128)(2,1)S(1)}, bf16[256,256]{1,0:T(8,128)(2,1)S(1)}, u32[]{:S(2)}, u32[]{:S(2)}) %collective-permute-start.25) | collective-permute-done | bytes 131104 | tf_op jit(solution)/shard_map/ppermute | solution.py:397
  69.8 2.0 %collective-permute-done.27.refs_3_ = bf16[256,256]{1,0:T(8,128)(2,1)S(1)} collective-permute-done((bf16[256,256]{1,0:T(8,128)(2,1)S(1)}, bf16[256,256]{1,0:T(8,128)(2,1)S(1)}, u32[]{:S(2)}, u32[]{:S(2)}) %collective-permute-start.27) | collective-permute-done | bytes 131104 | tf_op jit(solution)/shard_map/ppermute | solution.py:397
  71.8 1.8 %shard_map.178.sum_ref = bf16[256,256]{1,0:T(8,128)(2,1)S(1)} custom-call(f32[256,256]{1,0:T(8,128)S(1)} %get-tuple-element.44.refs_0_, bf16[256,256]{1,0:T(8,128)(2,1)S(1)} %collective-permute-done.25.refs_1_, bf16[256,256]{1,0:T(8,128)(2,1)S(1)} %collective-permute-done.26.refs_2_, bf16[256,256]{1,0:T(8,128)(2,1)S(1)} %collective-permute-done.27.refs_3_, ...), custom_call_target="tpu_custom_call" | custom-call | flops 1073741824 | bytes 1048576 | tf_op jit(solution)/shard_map/pallas_call | solution.py:51
  74.1 1.5 %collective-permute-done.28.other_ref = bf16[1024,128]{1,0:T(8,128)(2,1)S(1)} collective-permute-done((bf16[1024,128]{1,0:T(8,128)(2,1)S(1)}, bf16[1024,128]{1,0:T(8,128)(2,1)S(1)}, u32[]{:S(2)}, u32[]{:S(2)}) %collective-permute-start.28) | collective-permute-done | bytes 262176 | tf_op jit(solution)/shard_map/ppermute | solution.py:384
  75.6 1.6 %collective-permute-start.29 = (bf16[256,128]{1,0:T(8,128)(2,1)S(1)}, bf16[256,128]{1,0:T(8,128)(2,1)S(1)}, u32[]{:S(2)}, u32[]{:S(2)}) collective-permute-start(bf16[256,128]{1,0:T(8,128)(2,1)S(1)} %get-tuple-element.54), channel_id=1, source_target_pairs={{0,2},{2,0},{4,6},{6,4},{8,10},{10,8},{12,14},{14,12},{16,18},{18,... | collective-permute-start | bytes 196616 | tf_op jit(solution)/shard_map/ppermute | solution.py:397
  77.2 0.8 collective-permute-start.30
  78.0 1.2 %collective-permute-start.31 = (bf16[256,128]{1,0:T(8,128)(2,1)S(1)}, bf16[256,128]{1,0:T(8,128)(2,1)S(1)}, u32[]{:S(2)}, u32[]{:S(2)}) collective-permute-start(bf16[256,128]{1,0:T(8,128)(2,1)S(1)} %get-tuple-element.56), channel_id=1, source_target_pairs={{0,6},{2,4},{4,2},{6,0},{8,14},{10,12},{12,10},{14,8},{16,22},{18,... | collective-permute-start | bytes 196616 | tf_op jit(solution)/shard_map/ppermute | solution.py:397
  79.2 0.8 collective-permute-done.29.refs_1_
  80.0 2.2 %collective-permute-done.30.refs_2_ = bf16[256,128]{1,0:T(8,128)(2,1)S(1)} collective-permute-done((bf16[256,128]{1,0:T(8,128)(2,1)S(1)}, bf16[256,128]{1,0:T(8,128)(2,1)S(1)}, u32[]{:S(2)}, u32[]{:S(2)}) %collective-permute-start.30) | collective-permute-done | bytes 65568 | tf_op jit(solution)/shard_map/ppermute | solution.py:397
  82.2 1.0 %collective-permute-done.31.refs_3_ = bf16[256,128]{1,0:T(8,128)(2,1)S(1)} collective-permute-done((bf16[256,128]{1,0:T(8,128)(2,1)S(1)}, bf16[256,128]{1,0:T(8,128)(2,1)S(1)}, u32[]{:S(2)}, u32[]{:S(2)}) %collective-permute-start.31) | collective-permute-done | bytes 65568 | tf_op jit(solution)/shard_map/ppermute | solution.py:397
  83.2 0.8 shard_map.181
  (72 shorter events, 4.7 us)
Async XLA Ops:
  1.8 6.0 %collective-permute-start.3 = (bf16[400,128]{1,0:T(8,128)(2,1)S(1)}, bf16[400,128]{1,0:T(8,128)(2,1)S(1)}, u32[]{:S(2)}, u32[]{:S(2)}) collective-permute-start(bf16[400,128]{1,0:T(8,128)(2,1)S(1)} %get-tuple-element.31.pack_ref.refs_0_), channel_id=1, source_target_pairs={{0,8},{2,10},{4,12},{6,14},{8,0},{10,2},{12,4},{14,6},{16,24},{18,... | collective-permute-start | bytes 307208 | tf_op jit(solution)/shard_map/ppermute | solution.py:390
  4.9 10.7 %collective-permute-start.4 = (bf16[400,128]{1,0:T(8,128)(2,1)S(1)}, bf16[400,128]{1,0:T(8,128)(2,1)S(1)}, u32[]{:S(2)}, u32[]{:S(2)}) collective-permute-start(bf16[400,128]{1,0:T(8,128)(2,1)S(1)} %get-tuple-element.31.pack_ref.refs_0_), channel_id=1, source_target_pairs={{0,16},{2,18},{4,20},{6,22},{8,24},{10,26},{12,28},{14,30},{16,0},... | collective-permute-start | bytes 307208 | tf_op jit(solution)/shard_map/ppermute | solution.py:390
  7.5 8.1 %collective-permute-start.5 = (bf16[400,128]{1,0:T(8,128)(2,1)S(1)}, bf16[400,128]{1,0:T(8,128)(2,1)S(1)}, u32[]{:S(2)}, u32[]{:S(2)}) collective-permute-start(bf16[400,128]{1,0:T(8,128)(2,1)S(1)} %get-tuple-element.31.pack_ref.refs_0_), channel_id=1, source_target_pairs={{0,24},{2,26},{4,28},{6,30},{8,16},{10,18},{12,20},{14,22},{16,8},... | collective-permute-start | bytes 307208 | tf_op jit(solution)/shard_map/ppermute | solution.py:390
  15.7 6.6 %collective-permute-start.6 = (bf16[1024,128]{1,0:T(8,128)(2,1)S(1)}, bf16[1024,128]{1,0:T(8,128)(2,1)S(1)}, u32[]{:S(2)}, u32[]{:S(2)}) collective-permute-start(bf16[1024,128]{1,0:T(8,128)(2,1)S(1)} %pad_maximum_fusion), channel_id=1, source_target_pairs={{0,1},{1,0},{2,3},{3,2},{4,5},{5,4},{6,7},{7,6},{8,9},{9,8},{10,11... | collective-permute-start | bytes 786440 | tf_op jit(solution)/shard_map/ppermute | solution.py:384
  15.8 19.8 %collective-permute-start.10 = (bf16[256,1024]{1,0:T(8,128)(2,1)}, bf16[256,1024]{1,0:T(8,128)(2,1)S(1)}, u32[]{:S(2)}, u32[]{:S(2)}) collective-permute-start(bf16[256,1024]{1,0:T(8,128)(2,1)} %refs_8_.3), channel_id=1, source_target_pairs={{0,1},{1,0},{2,3},{3,2},{4,5},{5,4},{6,7},{7,6},{8,9},{9,8},{10,11... | collective-permute-start | bytes 1572872 | tf_op jit(solution)/shard_map/ppermute | solution.py:384
  16.3 21.4 %collective-permute-start.11 = (bf16[256,1024]{1,0:T(8,128)(2,1)}, bf16[256,1024]{1,0:T(8,128)(2,1)S(1)}, u32[]{:S(2)}, u32[]{:S(2)}) collective-permute-start(bf16[256,1024]{1,0:T(8,128)(2,1)} %refs_10_.1), channel_id=1, source_target_pairs={{0,1},{1,0},{2,3},{3,2},{4,5},{5,4},{6,7},{7,6},{8,9},{9,8},{10,11... | collective-permute-start | bytes 1572872 | tf_op jit(solution)/shard_map/ppermute | solution.py:384
  16.4 21.4 %collective-permute-start.12 = (bf16[1024,256]{1,0:T(8,128)(2,1)}, bf16[1024,256]{1,0:T(8,128)(2,1)S(1)}, u32[]{:S(2)}, u32[]{:S(2)}) collective-permute-start(bf16[1024,256]{1,0:T(8,128)(2,1)} %refs_12_.1), channel_id=1, source_target_pairs={{0,1},{1,0},{2,3},{3,2},{4,5},{5,4},{6,7},{7,6},{8,9},{9,8},{10,11... | collective-permute-start | bytes 1572872 | tf_op jit(solution)/shard_map/ppermute | solution.py:384
  16.8 4.0 %collective-permute-start = (bf16[144,128]{1,0:T(8,128)(2,1)S(1)}, bf16[144,128]{1,0:T(8,128)(2,1)S(1)}, u32[]{:S(2)}, u32[]{:S(2)}) collective-permute-start(bf16[144,128]{1,0:T(8,128)(2,1)S(1)} %get-tuple-element.30.refs_0_), channel_id=1, source_target_pairs={{0,2},{2,0},{4,6},{6,4},{8,10},{10,8},{12,14},{14,12},{16,18},{18,... | collective-permute-start | bytes 110600 | tf_op jit(solution)/shard_map/ppermute | solution.py:397
  20.0 13.8 %copy-start.2 = (bf16[1024,256]{1,0:T(8,128)(2,1)S(1)}, bf16[1024,256]{1,0:T(8,128)(2,1)}, u32[]{:S(2)}) copy-start(bf16[1024,256]{1,0:T(8,128)(2,1)} %down_a.1) | copy-start | bytes 1572868
  20.0 15.5 %copy-start.9 = (bf16[256,1024]{1,0:T(8,128)(2,1)S(1)}, bf16[256,1024]{1,0:T(8,128)(2,1)}, u32[]{:S(2)}) copy-start(bf16[256,1024]{1,0:T(8,128)(2,1)} %refs_6_.2) | copy-start | bytes 1572868
  20.0 15.5 %copy-start.10 = (bf16[256,1024]{1,0:T(8,128)(2,1)S(1)}, bf16[256,1024]{1,0:T(8,128)(2,1)}, u32[]{:S(2)}) copy-start(bf16[256,1024]{1,0:T(8,128)(2,1)} %refs_8_.2) | copy-start | bytes 1572868
  20.7 4.0 %collective-permute-start.1 = (bf16[144,128]{1,0:T(8,128)(2,1)S(1)}, bf16[144,128]{1,0:T(8,128)(2,1)S(1)}, u32[]{:S(2)}, u32[]{:S(2)}) collective-permute-start(bf16[144,128]{1,0:T(8,128)(2,1)S(1)} %get-tuple-element.30.refs_0_), channel_id=1, source_target_pairs={{0,4},{2,6},{4,0},{6,2},{8,12},{10,14},{12,8},{14,10},{16,20},{18,... | collective-permute-start | bytes 110600 | tf_op jit(solution)/shard_map/ppermute | solution.py:397
  22.3 5.3 %collective-permute-start.2 = (bf16[144,128]{1,0:T(8,128)(2,1)S(1)}, bf16[144,128]{1,0:T(8,128)(2,1)S(1)}, u32[]{:S(2)}, u32[]{:S(2)}) collective-permute-start(bf16[144,128]{1,0:T(8,128)(2,1)S(1)} %get-tuple-element.30.refs_0_), channel_id=1, source_target_pairs={{0,6},{2,4},{4,2},{6,0},{8,14},{10,12},{12,10},{14,8},{16,22},{18,... | collective-permute-start | bytes 110600 | tf_op jit(solution)/shard_map/ppermute | solution.py:397
  24.5 13.2 %copy-start.3 = (bf16[256,1024]{1,0:T(8,128)(2,1)S(1)}, bf16[256,1024]{1,0:T(8,128)(2,1)}, u32[]{:S(2)}) copy-start(bf16[256,1024]{1,0:T(8,128)(2,1)} %refs_8_.3) | copy-start | bytes 1572868
  24.5 13.2 %copy-start.4 = (bf16[256,1024]{1,0:T(8,128)(2,1)S(1)}, bf16[256,1024]{1,0:T(8,128)(2,1)}, u32[]{:S(2)}) copy-start(bf16[256,1024]{1,0:T(8,128)(2,1)} %refs_10_.1) | copy-start | bytes 1572868
  24.5 13.2 %copy-start.5 = (bf16[1024,256]{1,0:T(8,128)(2,1)S(1)}, bf16[1024,256]{1,0:T(8,128)(2,1)}, u32[]{:S(2)}) copy-start(bf16[1024,256]{1,0:T(8,128)(2,1)} %refs_12_.1) | copy-start | bytes 1572868
  24.5 13.2 %copy-start.8 = (f32[256]{0:T(256)S(1)}, f32[256]{0:T(256)}, u32[]{:S(2)}) copy-start(f32[256]{0:T(256)} %param.22) | copy-start | bytes 3076
  24.7 5.0 %collective-permute-start.7 = (bf16[256,256]{1,0:T(8,128)(2,1)S(1)}, bf16[256,256]{1,0:T(8,128)(2,1)S(1)}, u32[]{:S(2)}, u32[]{:S(2)}) collective-permute-start(bf16[256,256]{1,0:T(8,128)(2,1)S(1)} %get-tuple-element.33), channel_id=1, source_target_pairs={{0,2},{2,0},{4,6},{6,4},{8,10},{10,8},{12,14},{14,12},{16,18},{18,... | collective-permute-start | bytes 393224 | tf_op jit(solution)/shard_map/ppermute | solution.py:397
  27.5 6.3 %collective-permute-start.8 = (bf16[256,256]{1,0:T(8,128)(2,1)S(1)}, bf16[256,256]{1,0:T(8,128)(2,1)S(1)}, u32[]{:S(2)}, u32[]{:S(2)}) collective-permute-start(bf16[256,256]{1,0:T(8,128)(2,1)S(1)} %get-tuple-element.34), channel_id=1, source_target_pairs={{0,4},{2,6},{4,0},{6,2},{8,12},{10,14},{12,8},{14,10},{16,20},{18,... | collective-permute-start | bytes 393224 | tf_op jit(solution)/shard_map/ppermute | solution.py:397
  29.7 5.9 %collective-permute-start.9 = (bf16[256,256]{1,0:T(8,128)(2,1)S(1)}, bf16[256,256]{1,0:T(8,128)(2,1)S(1)}, u32[]{:S(2)}, u32[]{:S(2)}) collective-permute-start(bf16[256,256]{1,0:T(8,128)(2,1)S(1)} %get-tuple-element.35), channel_id=1, source_target_pairs={{0,6},{2,4},{4,2},{6,0},{8,14},{10,12},{12,10},{14,8},{16,22},{18,... | collective-permute-start | bytes 393224 | tf_op jit(solution)/shard_map/ppermute | solution.py:397
  33.8 10.8 %collective-permute-start.18 = (bf16[1024,256]{1,0:T(8,128)(2,1)S(1)}, bf16[1024,256]{1,0:T(8,128)(2,1)S(1)}, u32[]{:S(2)}, u32[]{:S(2)}) collective-permute-start(bf16[1024,256]{1,0:T(8,128)(2,1)S(1)} %copy-done.2), channel_id=1, source_target_pairs={{0,1},{1,0},{2,3},{3,2},{4,5},{5,4},{6,7},{7,6},{8,9},{9,8},{10,11... | collective-permute-start | bytes 1572872 | tf_op jit(solution)/shard_map/ppermute | solution.py:384
  35.5 9.9 %collective-permute-start.19 = (bf16[256,1024]{1,0:T(8,128)(2,1)S(1)}, bf16[256,1024]{1,0:T(8,128)(2,1)S(1)}, u32[]{:S(2)}, u32[]{:S(2)}) collective-permute-start(bf16[256,1024]{1,0:T(8,128)(2,1)S(1)} %copy-done.9), channel_id=1, source_target_pairs={{0,1},{1,0},{2,3},{3,2},{4,5},{5,4},{6,7},{7,6},{8,9},{9,8},{10,11... | collective-permute-start | bytes 1572872 | tf_op jit(solution)/shard_map/ppermute | solution.py:384
  35.6 9.9 %collective-permute-start.20 = (bf16[256,1024]{1,0:T(8,128)(2,1)S(1)}, bf16[256,1024]{1,0:T(8,128)(2,1)S(1)}, u32[]{:S(2)}, u32[]{:S(2)}) collective-permute-start(bf16[256,1024]{1,0:T(8,128)(2,1)S(1)} %copy-done.10), channel_id=1, source_target_pairs={{0,1},{1,0},{2,3},{3,2},{4,5},{5,4},{6,7},{7,6},{8,9},{9,8},{10,11... | collective-permute-start | bytes 1572872 | tf_op jit(solution)/shard_map/ppermute | solution.py:384
  37.8 7.2 %copy-start = (bf16[256,128]{1,0:T(8,128)(2,1)S(1)}, bf16[256,128]{1,0:T(8,128)(2,1)}, u32[]{:S(2)}) copy-start(bf16[256,128]{1,0:T(8,128)(2,1)} %refs_4_.1) | copy-start | bytes 196612
  39.3 10.5 %copy-start.11 = (f32[256]{0:T(256)S(1)}, f32[256]{0:T(256)}, u32[]{:S(2)}) copy-start(f32[256]{0:T(256)} %param.23) | copy-start | bytes 3076
  39.8 1.6 %collective-permute-start.13 = (bf16[512,256]{1,0:T(8,128)(2,1)S(1)}, bf16[512,256]{1,0:T(8,128)(2,1)S(1)}, u32[]{:S(2)}, u32[]{:S(2)}) collective-permute-start(bf16[512,256]{1,0:T(8,128)(2,1)S(1)} %get-tuple-element.38), channel_id=1, source_target_pairs={{0,1},{1,0},{2,3},{3,2},{4,5},{5,4},{6,7},{7,6},{8,9},{9,8},{10,11... | collective-permute-start | bytes 786440 | tf_op jit(solution)/shard_map/ppermute | solution.py:384
  39.9 3.5 %collective-permute-start.17 = (bf16[128,128]{1,0:T(8,128)(2,1)S(1)}, bf16[128,128]{1,0:T(8,128)(2,1)S(1)}, u32[]{:S(2)}, u32[]{:S(2)}) collective-permute-start(bf16[128,128]{1,0:T(8,128)(2,1)S(1)} %get-tuple-element.43), channel_id=1, source_target_pairs={{0,1},{1,0},{2,3},{3,2},{4,5},{5,4},{6,7},{7,6},{8,9},{9,8},{10,11... | collective-permute-start | bytes 98312 | tf_op jit(solution)/shard_map/ppermute | solution.py:384
  41.4 4.3 %collective-permute-start.14 = (bf16[128,256]{1,0:T(8,128)(2,1)S(1)}, bf16[128,256]{1,0:T(8,128)(2,1)S(1)}, u32[]{:S(2)}, u32[]{:S(2)}) collective-permute-start(bf16[128,256]{1,0:T(8,128)(2,1)S(1)} %get-tuple-element.40), channel_id=1, source_target_pairs={{0,2},{2,0},{4,6},{6,4},{8,10},{10,8},{12,14},{14,12},{16,18},{18,... | collective-permute-start | bytes 196616 | tf_op jit(solution)/shard_map/ppermute | solution.py:397
  43.4 4.3 %collective-permute-start.15 = (bf16[128,256]{1,0:T(8,128)(2,1)S(1)}, bf16[128,256]{1,0:T(8,128)(2,1)S(1)}, u32[]{:S(2)}, u32[]{:S(2)}) collective-permute-start(bf16[128,256]{1,0:T(8,128)(2,1)S(1)} %get-tuple-element.41), channel_id=1, source_target_pairs={{0,4},{2,6},{4,0},{6,2},{8,12},{10,14},{12,8},{14,10},{16,20},{18,... | collective-permute-start | bytes 196616 | tf_op jit(solution)/shard_map/ppermute | solution.py:397
  44.7 5.2 %collective-permute-start.16 = (bf16[128,256]{1,0:T(8,128)(2,1)S(1)}, bf16[128,256]{1,0:T(8,128)(2,1)S(1)}, u32[]{:S(2)}, u32[]{:S(2)}) collective-permute-start(bf16[128,256]{1,0:T(8,128)(2,1)S(1)} %get-tuple-element.42), channel_id=1, source_target_pairs={{0,6},{2,4},{4,2},{6,0},{8,14},{10,12},{12,10},{14,8},{16,22},{18,... | collective-permute-start | bytes 196616 | tf_op jit(solution)/shard_map/ppermute | solution.py:397
  51.6 4.7 %collective-permute-start.21 = (bf16[128,256]{1,0:T(8,128)(2,1)S(1)}, bf16[128,256]{1,0:T(8,128)(2,1)S(1)}, u32[]{:S(2)}, u32[]{:S(2)}) collective-permute-start(bf16[128,256]{1,0:T(8,128)(2,1)S(1)} %shard_map.176.refs_0_), channel_id=1, source_target_pairs={{0,8},{2,10},{4,12},{6,14},{8,0},{10,2},{12,4},{14,6},{16,24},{18,... | collective-permute-start | bytes 196616 | tf_op jit(solution)/shard_map/ppermute | solution.py:390
  53.3 6.0 %collective-permute-start.22 = (bf16[128,256]{1,0:T(8,128)(2,1)S(1)}, bf16[128,256]{1,0:T(8,128)(2,1)S(1)}, u32[]{:S(2)}, u32[]{:S(2)}) collective-permute-start(bf16[128,256]{1,0:T(8,128)(2,1)S(1)} %shard_map.176.refs_0_), channel_id=1, source_target_pairs={{0,16},{2,18},{4,20},{6,22},{8,24},{10,26},{12,28},{14,30},{16,0},... | collective-permute-start | bytes 196616 | tf_op jit(solution)/shard_map/ppermute | solution.py:390
  54.7 6.1 %collective-permute-start.23 = (bf16[128,256]{1,0:T(8,128)(2,1)S(1)}, bf16[128,256]{1,0:T(8,128)(2,1)S(1)}, u32[]{:S(2)}, u32[]{:S(2)}) collective-permute-start(bf16[128,256]{1,0:T(8,128)(2,1)S(1)} %shard_map.176.refs_0_), channel_id=1, source_target_pairs={{0,24},{2,26},{4,28},{6,30},{8,16},{10,18},{12,20},{14,22},{16,8},... | collective-permute-start | bytes 196616 | tf_op jit(solution)/shard_map/ppermute | solution.py:390
  60.8 1.6 %collective-permute-start.24 = (bf16[512,256]{1,0:T(8,128)(2,1)S(1)}, bf16[512,256]{1,0:T(8,128)(2,1)S(1)}, u32[]{:S(2)}, u32[]{:S(2)}) collective-permute-start(bf16[512,256]{1,0:T(8,128)(2,1)S(1)} %pad_maximum_fusion.1), channel_id=1, source_target_pairs={{0,1},{1,0},{2,3},{3,2},{4,5},{5,4},{6,7},{7,6},{8,9},{9,8},{10,11... | collective-permute-start | bytes 786440 | tf_op jit(solution)/shard_map/ppermute | solution.py:384
  63.2 6.4 %collective-permute-start.25 = (bf16[256,256]{1,0:T(8,128)(2,1)S(1)}, bf16[256,256]{1,0:T(8,128)(2,1)S(1)}, u32[]{:S(2)}, u32[]{:S(2)}) collective-permute-start(bf16[256,256]{1,0:T(8,128)(2,1)S(1)} %get-tuple-element.45), channel_id=1, source_target_pairs={{0,2},{2,0},{4,6},{6,4},{8,10},{10,8},{12,14},{14,12},{16,18},{18,... | collective-permute-start | bytes 393224 | tf_op jit(solution)/shard_map/ppermute | solution.py:397
  63.7 6.1 %collective-permute-start.26 = (bf16[256,256]{1,0:T(8,128)(2,1)S(1)}, bf16[256,256]{1,0:T(8,128)(2,1)S(1)}, u32[]{:S(2)}, u32[]{:S(2)}) collective-permute-start(bf16[256,256]{1,0:T(8,128)(2,1)S(1)} %get-tuple-element.46), channel_id=1, source_target_pairs={{0,4},{2,6},{4,0},{6,2},{8,12},{10,14},{12,8},{14,10},{16,20},{18,... | collective-permute-start | bytes 393224 | tf_op jit(solution)/shard_map/ppermute | solution.py:397
  64.3 7.6 %collective-permute-start.27 = (bf16[256,256]{1,0:T(8,128)(2,1)S(1)}, bf16[256,256]{1,0:T(8,128)(2,1)S(1)}, u32[]{:S(2)}, u32[]{:S(2)}) collective-permute-start(bf16[256,256]{1,0:T(8,128)(2,1)S(1)} %get-tuple-element.47), channel_id=1, source_target_pairs={{0,6},{2,4},{4,2},{6,0},{8,14},{10,12},{12,10},{14,8},{16,22},{18,... | collective-permute-start | bytes 393224 | tf_op jit(solution)/shard_map/ppermute | solution.py:397
  71.8 11.4 %copy-start.1 = (f32[256,128]{1,0:T(8,128)S(1)}, f32[256,128]{1,0:T(8,128)}, u32[]{:S(2)}) copy-start(f32[256,128]{1,0:T(8,128)} %refs_5_.3) | copy-start | bytes 393220
  71.8 11.4 %copy-start.6 = (f32[256,128]{1,0:T(8,128)S(1)}, f32[256,128]{1,0:T(8,128)}, u32[]{:S(2)}) copy-start(f32[256,128]{1,0:T(8,128)} %refs_6_.3) | copy-start | bytes 393220
  71.8 11.4 %copy-start.7 = (f32[256,128]{1,0:T(8,128)S(1)}, f32[256,128]{1,0:T(8,128)}, u32[]{:S(2)}) copy-start(f32[256,128]{1,0:T(8,128)} %refs_7_.3) | copy-start | bytes 393220
  74.0 1.6 %collective-permute-start.28 = (bf16[1024,128]{1,0:T(8,128)(2,1)S(1)}, bf16[1024,128]{1,0:T(8,128)(2,1)S(1)}, u32[]{:S(2)}, u32[]{:S(2)}) collective-permute-start(bf16[1024,128]{1,0:T(8,128)(2,1)S(1)} %get-tuple-element.52), channel_id=1, source_target_pairs={{0,1},{1,0},{2,3},{3,2},{4,5},{5,4},{6,7},{7,6},{8,9},{9,8},{10,11... | collective-permute-start | bytes 786440 | tf_op jit(solution)/shard_map/ppermute | solution.py:384
  75.6 4.3 %collective-permute-start.29 = (bf16[256,128]{1,0:T(8,128)(2,1)S(1)}, bf16[256,128]{1,0:T(8,128)(2,1)S(1)}, u32[]{:S(2)}, u32[]{:S(2)}) collective-permute-start(bf16[256,128]{1,0:T(8,128)(2,1)S(1)} %get-tuple-element.54), channel_id=1, source_target_pairs={{0,2},{2,0},{4,6},{6,4},{8,10},{10,8},{12,14},{14,12},{16,18},{18,... | collective-permute-start | bytes 196616 | tf_op jit(solution)/shard_map/ppermute | solution.py:397
  77.2 5.0 %collective-permute-start.30 = (bf16[256,128]{1,0:T(8,128)(2,1)S(1)}, bf16[256,128]{1,0:T(8,128)(2,1)S(1)}, u32[]{:S(2)}, u32[]{:S(2)}) collective-permute-start(bf16[256,128]{1,0:T(8,128)(2,1)S(1)} %get-tuple-element.55), channel_id=1, source_target_pairs={{0,4},{2,6},{4,0},{6,2},{8,12},{10,14},{12,8},{14,10},{16,20},{18,... | collective-permute-start | bytes 196616 | tf_op jit(solution)/shard_map/ppermute | solution.py:397
  78.0 5.2 %collective-permute-start.31 = (bf16[256,128]{1,0:T(8,128)(2,1)S(1)}, bf16[256,128]{1,0:T(8,128)(2,1)S(1)}, u32[]{:S(2)}, u32[]{:S(2)}) collective-permute-start(bf16[256,128]{1,0:T(8,128)(2,1)S(1)} %get-tuple-element.56), channel_id=1, source_target_pairs={{0,6},{2,4},{4,2},{6,0},{8,14},{10,12},{12,10},{14,8},{16,22},{18,... | collective-permute-start | bytes 196616 | tf_op jit(solution)/shard_map/ppermute | solution.py:397

commit v4 on v3

--- a/solution.py
+++ b/solution.py
@@ -11,7 +11,7 @@
 
 BLOCK = 128
 GATHER = 4
-CHUNK = 256
+CHUNK = 1024
 
 NORM_EPSILON = 1e-05
 LEARNING_RATE = 0.01
@@ -61,6 +61,10 @@
 
 def sigmoid(v):
     return 0.5 * jnp.tanh(0.5 * v) + 0.5
+
+
+def crossed(k):
+    return (k & ~3) | ((k & 1) << 1) | ((k >> 1) & 1)
 
 
 def pack_body(
@@ -115,7 +119,9 @@
     meta = jnp.zeros_like(lanes)
     for t in range(tiles):
         dest = dest_ref[t]
-        slot = ((dest % groups) ^ place) * members + dest // groups
+        hop = (dest % groups) ^ place
+        hop = jnp.where(core == 1, crossed(hop), hop)
+        slot = hop * members + dest // groups
         meta = jnp.where(lanes == t, slot, meta)
         meta = jnp.where(lanes == tiles + t, item_ref[t], meta)
     pack_ref[items + 2 * half :, :] = meta.astype(F32).astype(BF16)
@@ -134,15 +140,24 @@
         out_ref[:, c : c + 2 * BLOCK] = jnp.where(hit, 1.0, 0.0).astype(BF16)
 
 
-def join_halves(core, whole_ref, own_ref_list, other_ref, rows):
+def join_halves(whole_ref, own_refs, other_ref, items):
+    core = lax.axis_index("mp")
     width = other_ref.shape[1]
-    mine = pl.multiple_of(core * width, width)
-    theirs = pl.multiple_of((1 - core) * width, width)
-    for l, own in enumerate(own_ref_list):
-        whole_ref[l * rows : (l + 1) * rows, pl.ds(mine, width)] = own[0:rows, :]
-        whole_ref[l * rows : (l + 1) * rows, pl.ds(theirs, width)] = other_ref[
-            l * rows : (l + 1) * rows, :
-        ]
+    rows = items // 2
+    mine = pl.ds(pl.multiple_of(core * width, width), width)
+    theirs = pl.ds(pl.multiple_of((1 - core) * width, width), width)
+    for part, half in ((0, core), (1, 1 - core)):
+        at = pl.multiple_of(half * rows, rows)
+        for l, own in enumerate(own_refs):
+            to = pl.ds((part * len(own_refs) + l) * rows, rows)
+            whole_ref[to, mine] = own[pl.ds(at, rows), :]
+            whole_ref[to, theirs] = other_ref[pl.ds(l * items + at, rows), :]
+
+
+def own_first(lane, l, members, rows):
+    at = lane - 2 * l * rows
+    mine = (at // rows) == lax.axis_index("mp")
+    return at % rows + l * rows + jnp.where(mine, 0, members * rows)
 
 
 def masks_body(idx_ref, *refs, per, half, items, tiles, own):
@@ -171,7 +186,10 @@
                 if own:
                     slot = jnp.where(slot // per == l, slot % per, per)
                 row = pl.multiple_of(slot * half, half)
-                lane = pl.multiple_of(idx_ref[l, tiles + t] * BLOCK + l * items, BLOCK)
+                lane = idx_ref[l, tiles + t] * BLOCK + l * items
+                if not own:
+                    lane = own_first(lane, l, len(incs), items // 2)
+                lane = pl.multiple_of(lane, BLOCK)
                 where = (pl.ds(row, half), pl.ds(lane, BLOCK))
                 mt_ref[where] = (
                     mt_ref[where]
@@ -179,16 +197,32 @@
                 )
 
 
-def sums_body(mt_ref, *refs, members, groups, items):
-    packs = refs[:members]
-    other_ref = refs[members]
-    out_refs = refs[members + 1 : members + 1 + groups]
-    rows_ref = refs[members + 1 + groups]
-    join_halves(lax.axis_index("mp"), rows_ref, packs, other_ref, items)
+def sums_body(mt_ref, *refs, members, items, first):
+    rows_ref, out_ref = refs[members + 1 :]
+    join_halves(rows_ref, refs[:members], refs[members], items)
+    per = out_ref.shape[0]
+    total = dot(mt_ref[first * per : (first + 1) * per, :], rows_ref[...])
+    out_ref[...] = total.astype(out_ref.dtype)
+
+
+def sums_rest_body(mt_ref, rows_ref, *out_refs, which):
     per = out_refs[0].shape[0]
-    for i in range(groups):
+    for i, out in zip(which, out_refs):
         total = dot(mt_ref[i * per : (i + 1) * per, :], rows_ref[...])
-        out_refs[i][...] = total.astype(out_refs[i].dtype)
+        out[...] = total.astype(out.dtype)
+
+
+def grad_own_body(mt_ref, own_ref, out_ref):
+    out_ref[...] = dot(mt_ref[:, 0 : own_ref.shape[0]], own_ref[...])
+
+
+def grad_sums_body(mt_ref, acc_ref, other_ref, *out_refs, which):
+    per = out_refs[0].shape[0]
+    wide = other_ref.shape[0]
+    for i, out in zip(which, out_refs):
+        at = slice(i * per, (i + 1) * per)
+        total = acc_ref[at, :] + dot(mt_ref[at, wide : 2 * wide], other_ref[...])
+        out[...] = total.astype(out.dtype)
 
 
 def turn_body(mt_ref, out_ref):
@@ -254,7 +288,8 @@
         mine = pl.multiple_of((2 * l + core) * rows, rows)
         theirs = pl.multiple_of((2 * l + 1 - core) * rows, rows)
         mine_ref[l * rows : (l + 1) * rows, :] = all_ref[pl.ds(mine, rows), :]
-        theirs_ref[l * rows : (l + 1) * rows, :] = all_ref[pl.ds(theirs, rows), :].astype(BF16)
+        to = slice(crossed(l) * rows, (crossed(l) + 1) * rows)
+        theirs_ref[to, :] = all_ref[pl.ds(theirs, rows), :].astype(BF16)
 
 
 def join_body(mine_ref, other_ref, *out_refs):
@@ -291,24 +326,6 @@
     out_ref[...] = (scale * weighted - message * (cubed * inner)).astype(BF16)
 
 
-def grad_sums_body(mt_ref, *refs, members, groups):
-    owns = refs[:members]
-    other_ref = refs[members]
-    out_refs = refs[members + 1 : members + 1 + groups]
-    rows_ref = refs[members + 1 + groups]
-    core = lax.axis_index("mp")
-    rows = owns[0].shape[0]
-    for l in range(members):
-        mine = pl.multiple_of((2 * l + core) * rows, rows)
-        theirs = pl.multiple_of((2 * l + 1 - core) * rows, rows)
-        rows_ref[pl.ds(mine, rows), :] = owns[l][...]
-        rows_ref[pl.ds(theirs, rows), :] = other_ref[l * rows : (l + 1) * rows, :]
-    per = out_refs[0].shape[0]
-    for i in range(groups):
-        total = dot(mt_ref[i * per : (i + 1) * per, :], rows_ref[...])
-        out_refs[i][...] = total.astype(out_refs[i].dtype)
-
-
 def basket_back_body(*refs, groups):
     parts = refs[:groups]
     sum_ref, value_ref, slope_ref, gain_ref = refs[groups : groups + 4]
@@ -333,13 +350,16 @@
     out_ref[...] = (scale * weighted - total * (cubed * inner)).astype(BF16)
 
 
-def back_body(mo_ref, sum_ref, mine_ref, theirs_ref, all_ref):
+def back_body(mo_ref, sum_ref, mine_ref, theirs_ref, all_ref, *, peers):
     all_ref[...] = dot(mo_ref[...], sum_ref[...])
     width = mine_ref.shape[1]
     core = lax.axis_index("mp")
     mine_ref[...] = all_ref[:, pl.ds(pl.multiple_of(core * width, width), width)]
-    theirs = all_ref[:, pl.ds(pl.multiple_of((1 - core) * width, width), width)]
-    theirs_ref[...] = theirs.astype(BF16)
+    rows = mine_ref.shape[0] // peers
+    theirs = pl.ds(pl.multiple_of((1 - core) * width, width), width)
+    for l in range(peers):
+        to = slice(crossed(l) * rows, (crossed(l) + 1) * rows)
+        theirs_ref[to, :] = all_ref[l * rows : (l + 1) * rows, theirs].astype(BF16)
 
 
 def adam_body(*refs, peers):
@@ -393,8 +413,12 @@
     def exchange(xs):
         got = [xs[0]]
         for k in range(1, groups):
-            pairs = [(s, (s // groups) * groups + ((s % groups) ^ k)) for s in range(shards)]
-            got.append(lax.ppermute(xs[k], "shard", pairs))
+            pairs = [
+                (2 * s + c, 2 * ((s // groups) * groups + ((s % groups) ^ hop)) + c)
+                for s in range(shards)
+                for c, hop in ((0, k), (1, crossed(k)))
+            ]
+            got.append(lax.ppermute(xs[k], ("shard", "mp"), pairs))
         return got
 
     pack, inc, cot_send = run(
@@ -430,7 +454,9 @@
     metas = [q[2 * half : 2 * half + 1] for q in incs]
     idx_plane = jnp.concatenate(metas, axis=0).astype(jnp.int32)
 
-    part_shapes = [sds((per, features), F32)] + [sds((per, features), BF16)] * (groups - 1)
+    lead = min(2, groups - 1)
+    rest = [i for i in range(groups) if i != lead]
+    rest_shapes = [sds((per, features), F32 if i == 0 else BF16) for i in rest]
     mt = run(
         functools.partial(
             masks_body, per=members, half=half, items=items, tiles=tiles, own=False
@@ -440,14 +466,21 @@
         (*packs, spread),
         flops=1 << 29,
     )
-    parts = run(
-        functools.partial(sums_body, members=members, groups=groups, items=items),
-        part_shapes,
+    whole_rows, lead_part = run(
+        functools.partial(sums_body, members=members, items=items, first=lead),
+        [sds((members * items, features), BF16), sds((per, features), BF16)],
         (),
         (mt, *packs, rows_other),
-        scratch=[pltpu.VMEM((members * items, features), BF16)],
-        flops=1 << 29,
-    )
+        flops=1 << 27,
+    )
+    rest_parts = run(
+        functools.partial(sums_rest_body, which=rest),
+        rest_shapes,
+        (),
+        (mt, whole_rows),
+        flops=1 << 28,
+    )
+    parts = dict(zip(rest, rest_parts)) | {lead: lead_part}
     received = exchange(parts)
     mt_plane = run(
         functools.partial(
@@ -520,15 +553,26 @@
         flops=1 << 30,
     )
     grads = [grad_message] + gather(grad_message)
-    grads_other = swap(jnp.concatenate(grads, axis=0))
-    grad_parts = run(
-        functools.partial(grad_sums_body, members=members, groups=groups),
-        part_shapes,
-        (),
-        (mt, *grads, grads_other),
-        scratch=[pltpu.VMEM((members * items, features), BF16)],
-        flops=1 << 29,
-    )
+    grads = jnp.concatenate(grads, axis=0)
+    grads_other = swap(grads)
+    grad_acc = run(
+        grad_own_body, sds((shards * half, features), F32), (), (mt, grads), flops=1 << 28
+    )
+    (lead_part,) = run(
+        functools.partial(grad_sums_body, which=[lead]),
+        [sds((per, features), BF16)],
+        (),
+        (mt, grad_acc, grads_other),
+        flops=1 << 27,
+    )
+    rest_parts = run(
+        functools.partial(grad_sums_body, which=rest),
+        rest_shapes,
+        (),
+        (mt, grad_acc, grads_other),
+        flops=1 << 28,
+    )
+    grad_parts = dict(zip(rest, rest_parts)) | {lead: lead_part}
     grad_received = exchange(grad_parts)
     grad_sum = run(
         functools.partial(basket_back_body, groups=groups),
@@ -550,7 +594,7 @@
         flops=1 << 30,
     )
     back_mine, back_theirs = run(
-        back_body,
+        functools.partial(back_body, peers=groups),
         [sds((groups * items, width), F32), sds((groups * items, width), BF16)],
         (),
         (mo, grad_sum),

time: 84.2 us -> 83.2 us (0.988)
  starting transfers between devices: 32.5 us -> 30.4 us
    ppermute x15, starting transfers between devices: 20.1 us -> 17.9 us  [exchange(): got.append(lax.ppermute(xs[k], ('shard', 'mp'), pairs))]
    ppermute x15, waiting for transfers between devices: 20.1 us -> 21.3 us  [exchange(): got.append(lax.ppermute(xs[k], ('shard', 'mp'), pairs))]
    pallas_call x16 -> x19, Pallas kernels: 13.3 us -> 13.6 us  [run(): return call(*far, *smem, *args)]
  transfers between devices with their start and end apart: 32 -> 32, of which waited for: 23 -> 22; matrix products, arithmetic and copies ran while one was open for 0% -> 0% of each run, Pallas kernels for 8% -> 9%
where the time goes in v4:
time: 83.2 us; the launch traced here: 83 us
  waiting for transfers between devices  37.8 us (45%)
  starting transfers between devices  30.4 us (37%)
  Pallas kernels  13.6 us (16%)
  between operations  1.02 us (1%)
    ppermute x15, waiting for transfers between devices, exchange(): got.append(lax.ppermute(xs[k], ('shard', 'mp'), pairs))  21.3 us
    ppermute x15, starting transfers between devices, exchange(): got.append(lax.ppermute(xs[k], ('shard', 'mp'), pairs))  17.9 us
    pallas_call x19, Pallas kernels, run(): return call(*far, *smem, *args)  13.6 us
    ppermute x6, waiting for transfers between devices, gather(): got.append(lax.ppermute(x, 'shard', pairs))  12.8 us
    ppermute x6, starting transfers between devices, gather(): got.append(lax.ppermute(x, 'shard', pairs))  10.2 us
    ppermute x11, waiting for transfers between devices, swap(): return lax.ppermute(x, 'mp', [(0, 1), (1, 0)])  3.65 us
    ppermute x11, starting transfers between devices, swap(): return lax.ppermute(x, 'mp', [(0, 1), (1, 0)])  2.3 us
  transfers between devices with their start and end apart: 32, of which 22 were waited for; matrix products, arithmetic and copies ran while one was open for 0% of the time, Pallas kernels for 9%

profile of v4, /device:TPU:0, one launch (start us, length us, event | category | flops | bytes accessed | tf_op | source)
XLA Modules:
  0.0 83.0 jit_solution(16592941441017182320)
XLA Ops:
  0.6 1.2 %shard_map.166 = (bf16[400,128]{1,0:T(8,128)(2,1)S(1)}, bf16[144,128]{1,0:T(8,128)(2,1)S(1)}, bf16[128,128]{1,0:T(8,128)(2,1)S(1)}) custom-call(s32[16]{0:T(128)} %dest_hbm.1, s32[16]{0:T(128)} %item_hbm.1, s32[128,128]{1,0:T(8,128)} %bitcast.6, f32[256,128]{1,0:T(8,128)} %refs_5_.3, bf16[256,128]{1,0:T(8,128)(2,1)} %refs_4_.1), custom_call_target="tpu_custom_call" | custom-call | flops 1048576 | bytes 1048576 | tf_op jit(solution)/shard_map/pallas_call | solution.py:51
  1.8 3.1 %collective-permute-start.3 = (bf16[400,128]{1,0:T(8,128)(2,1)S(1)}, bf16[400,128]{1,0:T(8,128)(2,1)S(1)}, u32[]{:S(2)}, u32[]{:S(2)}) collective-permute-start(bf16[400,128]{1,0:T(8,128)(2,1)S(1)} %get-tuple-element.31.pack_ref.refs_0_), channel_id=1, source_target_pairs={{0,8},{2,10},{4,12},{6,14},{8,0},{10,2},{12,4},{14,6},{16,24},{18,... | collective-permute-start | bytes 307208 | tf_op jit(solution)/shard_map/ppermute | solution.py:410
  5.0 2.6 %collective-permute-start.4 = (bf16[400,128]{1,0:T(8,128)(2,1)S(1)}, bf16[400,128]{1,0:T(8,128)(2,1)S(1)}, u32[]{:S(2)}, u32[]{:S(2)}) collective-permute-start(bf16[400,128]{1,0:T(8,128)(2,1)S(1)} %get-tuple-element.31.pack_ref.refs_0_), channel_id=1, source_target_pairs={{0,16},{2,18},{4,20},{6,22},{8,24},{10,26},{12,28},{14,30},{16,0},... | collective-permute-start | bytes 307208 | tf_op jit(solution)/shard_map/ppermute | solution.py:410
  7.8 7.8 %collective-permute-done.4.refs_2_ = bf16[400,128]{1,0:T(8,128)(2,1)S(1)} collective-permute-done((bf16[400,128]{1,0:T(8,128)(2,1)S(1)}, bf16[400,128]{1,0:T(8,128)(2,1)S(1)}, u32[]{:S(2)}, u32[]{:S(2)}) %collective-permute-start.4) | collective-permute-done | bytes 102432 | tf_op jit(solution)/shard_map/ppermute | solution.py:410
  15.8 0.5 collective-permute-start.10
  16.8 1.5 %collective-permute-start = (bf16[144,128]{1,0:T(8,128)(2,1)S(1)}, bf16[144,128]{1,0:T(8,128)(2,1)S(1)}, u32[]{:S(2)}, u32[]{:S(2)}) collective-permute-start(bf16[144,128]{1,0:T(8,128)(2,1)S(1)} %get-tuple-element.30.refs_0_), channel_id=1, source_target_pairs={{0,2},{1,5},{2,0},{3,7},{4,6},{5,1},{6,4},{7,3},{8,10},{9,13},{10,... | collective-permute-start | bytes 110600 | tf_op jit(solution)/shard_map/ppermute | solution.py:421
  18.6 1.6 %shard_map.170.mt_ref = bf16[1024,1024]{1,0:T(8,128)(2,1)S(1)} custom-call(s32[4,128]{1,0:T(4,128)S(1)} %maximum_convert_fusion.1.idx_ref, bf16[400,128]{1,0:T(8,128)(2,1)S(1)} %get-tuple-element.31.pack_ref.refs_0_, bf16[400,128]{1,0:T(8,128)(2,1)S(1)} %collective-permute-done.3.refs_1_, bf16[400,128]{1,0:T(8,128)(2,1)S(1)} %collective-permute-done.4.refs_2_, ...), custom_call_target="tpu_custom_call" | custom-call | flops 536870912 | bytes 1048576 | tf_op jit(solution)/shard_map/pallas_call | solution.py:51
  20.2 1.6 %collective-permute-start.1 = (bf16[144,128]{1,0:T(8,128)(2,1)S(1)}, bf16[144,128]{1,0:T(8,128)(2,1)S(1)}, u32[]{:S(2)}, u32[]{:S(2)}) collective-permute-start(bf16[144,128]{1,0:T(8,128)(2,1)S(1)} %get-tuple-element.30.refs_0_), channel_id=1, source_target_pairs={{0,4},{1,3},{2,6},{3,1},{4,0},{5,7},{6,2},{7,5},{8,12},{9,11},{10,... | collective-permute-start | bytes 110600 | tf_op jit(solution)/shard_map/ppermute | solution.py:421
  22.3 1.0 %collective-permute-start.2 = (bf16[144,128]{1,0:T(8,128)(2,1)S(1)}, bf16[144,128]{1,0:T(8,128)(2,1)S(1)}, u32[]{:S(2)}, u32[]{:S(2)}) collective-permute-start(bf16[144,128]{1,0:T(8,128)(2,1)S(1)} %get-tuple-element.30.refs_0_), channel_id=1, source_target_pairs={{0,6},{1,7},{2,4},{3,5},{4,2},{5,3},{6,0},{7,1},{8,14},{9,15},{10,... | collective-permute-start | bytes 110600 | tf_op jit(solution)/shard_map/ppermute | solution.py:421
  23.2 0.6 shard_map.172
  24.2 0.8 collective-permute-start.7
  25.0 2.3 %collective-permute-done.2.refs_3_ = bf16[144,128]{1,0:T(8,128)(2,1)S(1)} collective-permute-done((bf16[144,128]{1,0:T(8,128)(2,1)S(1)}, bf16[144,128]{1,0:T(8,128)(2,1)S(1)}, u32[]{:S(2)}, u32[]{:S(2)}) %collective-permute-start.2) | collective-permute-done | bytes 36896 | tf_op jit(solution)/shard_map/ppermute | solution.py:421
  27.3 0.8 %collective-permute-start.9 = (bf16[256,256]{1,0:T(8,128)(2,1)S(1)}, bf16[256,256]{1,0:T(8,128)(2,1)S(1)}, u32[]{:S(2)}, u32[]{:S(2)}) collective-permute-start(bf16[256,256]{1,0:T(8,128)(2,1)S(1)} %get-tuple-element.36), channel_id=1, source_target_pairs={{0,6},{1,7},{2,4},{3,5},{4,2},{5,3},{6,0},{7,1},{8,14},{9,15},{10,... | collective-permute-start | bytes 393224 | tf_op jit(solution)/shard_map/ppermute | solution.py:421
  28.1 2.2 %collective-permute-done.7.refs_1_ = bf16[256,256]{1,0:T(8,128)(2,1)S(1)} collective-permute-done((bf16[256,256]{1,0:T(8,128)(2,1)S(1)}, bf16[256,256]{1,0:T(8,128)(2,1)S(1)}, u32[]{:S(2)}, u32[]{:S(2)}) %collective-permute-start.7) | collective-permute-done | bytes 131104 | tf_op jit(solution)/shard_map/ppermute | solution.py:421
  30.3 1.5 %collective-permute-start.8 = (bf16[256,256]{1,0:T(8,128)(2,1)S(1)}, bf16[256,256]{1,0:T(8,128)(2,1)S(1)}, u32[]{:S(2)}, u32[]{:S(2)}) collective-permute-start(bf16[256,256]{1,0:T(8,128)(2,1)S(1)} %get-tuple-element.35), channel_id=1, source_target_pairs={{0,4},{1,3},{2,6},{3,1},{4,0},{5,7},{6,2},{7,5},{8,12},{9,11},{10,... | collective-permute-start | bytes 393224 | tf_op jit(solution)/shard_map/ppermute | solution.py:421
  31.8 2.6 %collective-permute-done.9.refs_3_ = bf16[256,256]{1,0:T(8,128)(2,1)S(1)} collective-permute-done((bf16[256,256]{1,0:T(8,128)(2,1)S(1)}, bf16[256,256]{1,0:T(8,128)(2,1)S(1)}, u32[]{:S(2)}, u32[]{:S(2)}) %collective-permute-start.9) | collective-permute-done | bytes 131104 | tf_op jit(solution)/shard_map/ppermute | solution.py:421
  34.5 1.1 %collective-permute-done.8.refs_2_ = bf16[256,256]{1,0:T(8,128)(2,1)S(1)} collective-permute-done((bf16[256,256]{1,0:T(8,128)(2,1)S(1)}, bf16[256,256]{1,0:T(8,128)(2,1)S(1)}, u32[]{:S(2)}, u32[]{:S(2)}) %collective-permute-start.8) | collective-permute-done | bytes 131104 | tf_op jit(solution)/shard_map/ppermute | solution.py:421
  35.6 0.5 collective-permute-start.20
  36.1 1.4 %shard_map.168.mt_ref = bf16[320,1024]{1,0:T(8,128)(2,1)S(1)} custom-call(s32[4,128]{1,0:T(4,128)S(1)} %maximum_convert_fusion.idx_ref, bf16[144,128]{1,0:T(8,128)(2,1)S(1)} %get-tuple-element.30.refs_0_, bf16[144,128]{1,0:T(8,128)(2,1)S(1)} %collective-permute-done.refs_1_, bf16[144,128]{1,0:T(8,128)(2,1)S(1)} %collective-permute-done.1.refs_2_, ...), custom_call_target="tpu_custom_call" | custom-call | flops 536870912 | bytes 1048576 | tf_op jit(solution)/shard_map/pallas_call | solution.py:51
  37.9 1.5 %shard_map.173 = (bf16[256,256]{1,0:T(8,128)(2,1)S(1)}, f32[256,256]{1,0:T(8,128)S(1)}, bf16[256,2048]{1,0:T(8,128)(2,1)S(1)}, bf16[256,2048]{1,0:T(8,128)(2,1)S(1)}) custom-call(f32[256,256]{1,0:T(8,128)S(1)} %get-tuple-element.33.refs_0_, bf16[256,256]{1,0:T(8,128)(2,1)S(1)} %collective-permute-done.7.refs_1_, ...), custom_call_target="tpu_custom_call" | custom-call | flops 1073741824 | bytes 1048576 | tf_op jit(solution)/shard_map/pallas_call | solution.py:51
  40.3 1.0 %collective-permute-done.13.other_ref = bf16[512,256]{1,0:T(8,128)(2,1)S(1)} collective-permute-done((bf16[512,256]{1,0:T(8,128)(2,1)S(1)}, bf16[512,256]{1,0:T(8,128)(2,1)S(1)}, u32[]{:S(2)}, u32[]{:S(2)}) %collective-permute-start.13) | collective-permute-done | bytes 262176 | tf_op jit(solution)/shard_map/ppermute | solution.py:404
  41.4 0.9 %collective-permute-start.14 = (bf16[128,256]{1,0:T(8,128)(2,1)S(1)}, bf16[128,256]{1,0:T(8,128)(2,1)S(1)}, u32[]{:S(2)}, u32[]{:S(2)}) collective-permute-start(bf16[128,256]{1,0:T(8,128)(2,1)S(1)} %get-tuple-element.41), channel_id=1, source_target_pairs={{0,2},{1,5},{2,0},{3,7},{4,6},{5,1},{6,4},{7,3},{8,10},{9,13},{10,... | collective-permute-start | bytes 196616 | tf_op jit(solution)/shard_map/ppermute | solution.py:421
  42.2 1.4 %collective-permute-start.15 = (bf16[128,256]{1,0:T(8,128)(2,1)S(1)}, bf16[128,256]{1,0:T(8,128)(2,1)S(1)}, u32[]{:S(2)}, u32[]{:S(2)}) collective-permute-start(bf16[128,256]{1,0:T(8,128)(2,1)S(1)} %get-tuple-element.42), channel_id=1, source_target_pairs={{0,4},{1,3},{2,6},{3,1},{4,0},{5,7},{6,2},{7,5},{8,12},{9,11},{10,... | collective-permute-start | bytes 196616 | tf_op jit(solution)/shard_map/ppermute | solution.py:421
  43.7 1.3 %collective-permute-start.16 = (bf16[128,256]{1,0:T(8,128)(2,1)S(1)}, bf16[128,256]{1,0:T(8,128)(2,1)S(1)}, u32[]{:S(2)}, u32[]{:S(2)}) collective-permute-start(bf16[128,256]{1,0:T(8,128)(2,1)S(1)} %get-tuple-element.43), channel_id=1, source_target_pairs={{0,6},{1,7},{2,4},{3,5},{4,2},{5,3},{6,0},{7,1},{8,14},{9,15},{10,... | collective-permute-start | bytes 196616 | tf_op jit(solution)/shard_map/ppermute | solution.py:421
  45.0 0.5 shard_map.176.refs_4_
  45.4 0.9 %collective-permute-done.14.refs_1_ = bf16[128,256]{1,0:T(8,128)(2,1)S(1)} collective-permute-done((bf16[128,256]{1,0:T(8,128)(2,1)S(1)}, bf16[128,256]{1,0:T(8,128)(2,1)S(1)}, u32[]{:S(2)}, u32[]{:S(2)}) %collective-permute-start.14) | collective-permute-done | bytes 65568 | tf_op jit(solution)/shard_map/ppermute | solution.py:421
  46.5 2.3 %collective-permute-done.16.refs_3_ = bf16[128,256]{1,0:T(8,128)(2,1)S(1)} collective-permute-done((bf16[128,256]{1,0:T(8,128)(2,1)S(1)}, bf16[128,256]{1,0:T(8,128)(2,1)S(1)}, u32[]{:S(2)}, u32[]{:S(2)}) %collective-permute-start.16) | collective-permute-done | bytes 65568 | tf_op jit(solution)/shard_map/ppermute | solution.py:421
  48.8 1.8 %shard_map.177 = bf16[128,256]{1,0:T(8,128)(2,1)S(1)} custom-call(f32[128,256]{1,0:T(8,128)S(1)} %get-tuple-element.40.refs_0_, bf16[128,256]{1,0:T(8,128)(2,1)S(1)} %collective-permute-done.14.refs_1_, bf16[128,256]{1,0:T(8,128)(2,1)S(1)} %collective-permute-done.15.refs_2_, bf16[128,256]{1,0:T(8,128)(2,1)S(1)} %collective-permute-done.16.refs_3_, ...), custom_call_target="tpu_custom_call" | custom-call | flops 1073741824 | bytes 1048576 | tf_op jit(solution)/shard_map/pallas_call | solution.py:51
  50.7 1.7 %collective-permute-start.21 = (bf16[128,256]{1,0:T(8,128)(2,1)S(1)}, bf16[128,256]{1,0:T(8,128)(2,1)S(1)}, u32[]{:S(2)}, u32[]{:S(2)}) collective-permute-start(bf16[128,256]{1,0:T(8,128)(2,1)S(1)} %shard_map.177), channel_id=1, source_target_pairs={{0,8},{2,10},{4,12},{6,14},{8,0},{10,2},{12,4},{14,6},{16,24},{18,... | collective-permute-start | bytes 196616 | tf_op jit(solution)/shard_map/ppermute | solution.py:410
  52.4 1.4 %collective-permute-start.22 = (bf16[128,256]{1,0:T(8,128)(2,1)S(1)}, bf16[128,256]{1,0:T(8,128)(2,1)S(1)}, u32[]{:S(2)}, u32[]{:S(2)}) collective-permute-start(bf16[128,256]{1,0:T(8,128)(2,1)S(1)} %shard_map.177), channel_id=1, source_target_pairs={{0,16},{2,18},{4,20},{6,22},{8,24},{10,26},{12,28},{14,30},{16,0},... | collective-permute-start | bytes 196616 | tf_op jit(solution)/shard_map/ppermute | solution.py:410
  53.8 1.3 %collective-permute-start.23 = (bf16[128,256]{1,0:T(8,128)(2,1)S(1)}, bf16[128,256]{1,0:T(8,128)(2,1)S(1)}, u32[]{:S(2)}, u32[]{:S(2)}) collective-permute-start(bf16[128,256]{1,0:T(8,128)(2,1)S(1)} %shard_map.177), channel_id=1, source_target_pairs={{0,24},{2,26},{4,28},{6,30},{8,16},{10,18},{12,20},{14,22},{16,8},... | collective-permute-start | bytes 196616 | tf_op jit(solution)/shard_map/ppermute | solution.py:410
  55.4 3.0 %collective-permute-done.22 = bf16[128,256]{1,0:T(8,128)(2,1)S(1)} collective-permute-done((bf16[128,256]{1,0:T(8,128)(2,1)S(1)}, bf16[128,256]{1,0:T(8,128)(2,1)S(1)}, u32[]{:S(2)}, u32[]{:S(2)}) %collective-permute-start.22) | collective-permute-done | bytes 65568 | tf_op jit(solution)/shard_map/ppermute | solution.py:410
  58.4 1.4 %collective-permute-done.23 = bf16[128,256]{1,0:T(8,128)(2,1)S(1)} collective-permute-done((bf16[128,256]{1,0:T(8,128)(2,1)S(1)}, bf16[128,256]{1,0:T(8,128)(2,1)S(1)}, u32[]{:S(2)}, u32[]{:S(2)}) %collective-permute-start.23) | collective-permute-done | bytes 65568 | tf_op jit(solution)/shard_map/ppermute | solution.py:410
  60.4 1.1 %collective-permute-done.24.other_ref = bf16[512,256]{1,0:T(8,128)(2,1)S(1)} collective-permute-done((bf16[512,256]{1,0:T(8,128)(2,1)S(1)}, bf16[512,256]{1,0:T(8,128)(2,1)S(1)}, u32[]{:S(2)}, u32[]{:S(2)}) %collective-permute-start.24) | collective-permute-done | bytes 262176 | tf_op jit(solution)/shard_map/ppermute | solution.py:404
  61.7 0.8 collective-permute-start.26
  62.8 1.3 %collective-permute-start.25 = (bf16[256,256]{1,0:T(8,128)(2,1)S(1)}, bf16[256,256]{1,0:T(8,128)(2,1)S(1)}, u32[]{:S(2)}, u32[]{:S(2)}) collective-permute-start(bf16[256,256]{1,0:T(8,128)(2,1)S(1)} %get-tuple-element.46), channel_id=1, source_target_pairs={{0,2},{1,5},{2,0},{3,7},{4,6},{5,1},{6,4},{7,3},{8,10},{9,13},{10,... | collective-permute-start | bytes 393224 | tf_op jit(solution)/shard_map/ppermute | solution.py:421
  64.2 1.5 %collective-permute-start.27 = (bf16[256,256]{1,0:T(8,128)(2,1)S(1)}, bf16[256,256]{1,0:T(8,128)(2,1)S(1)}, u32[]{:S(2)}, u32[]{:S(2)}) collective-permute-start(bf16[256,256]{1,0:T(8,128)(2,1)S(1)} %get-tuple-element.47), channel_id=1, source_target_pairs={{0,6},{1,7},{2,4},{3,5},{4,2},{5,3},{6,0},{7,1},{8,14},{9,15},{10,... | collective-permute-start | bytes 393224 | tf_op jit(solution)/shard_map/ppermute | solution.py:421
  65.7 2.7 %collective-permute-done.26.refs_2_ = bf16[256,256]{1,0:T(8,128)(2,1)S(1)} collective-permute-done((bf16[256,256]{1,0:T(8,128)(2,1)S(1)}, bf16[256,256]{1,0:T(8,128)(2,1)S(1)}, u32[]{:S(2)}, u32[]{:S(2)}) %collective-permute-start.26) | collective-permute-done | bytes 131104 | tf_op jit(solution)/shard_map/ppermute | solution.py:421
  68.4 0.5 collective-permute-done.25.refs_1_
  68.9 2.5 %collective-permute-done.27.refs_3_ = bf16[256,256]{1,0:T(8,128)(2,1)S(1)} collective-permute-done((bf16[256,256]{1,0:T(8,128)(2,1)S(1)}, bf16[256,256]{1,0:T(8,128)(2,1)S(1)}, u32[]{:S(2)}, u32[]{:S(2)}) %collective-permute-start.27) | collective-permute-done | bytes 131104 | tf_op jit(solution)/shard_map/ppermute | solution.py:421
  71.4 1.5 %shard_map.181.sum_ref = bf16[256,256]{1,0:T(8,128)(2,1)S(1)} custom-call(f32[256,256]{1,0:T(8,128)S(1)} %get-tuple-element.45.refs_0_, bf16[256,256]{1,0:T(8,128)(2,1)S(1)} %collective-permute-done.25.refs_1_, bf16[256,256]{1,0:T(8,128)(2,1)S(1)} %collective-permute-done.26.refs_2_, bf16[256,256]{1,0:T(8,128)(2,1)S(1)} %collective-permute-done.27.refs_3_, ...), custom_call_target="tpu_custom_call" | custom-call | flops 1073741824 | bytes 1048576 | tf_op jit(solution)/shard_map/pallas_call | solution.py:51
  73.4 1.5 %collective-permute-done.28.other_ref = bf16[1024,128]{1,0:T(8,128)(2,1)S(1)} collective-permute-done((bf16[1024,128]{1,0:T(8,128)(2,1)S(1)}, bf16[1024,128]{1,0:T(8,128)(2,1)S(1)}, u32[]{:S(2)}, u32[]{:S(2)}) %collective-permute-start.28) | collective-permute-done | bytes 262176 | tf_op jit(solution)/shard_map/ppermute | solution.py:404
  75.0 0.8 %collective-permute-start.29 = (bf16[256,128]{1,0:T(8,128)(2,1)S(1)}, bf16[256,128]{1,0:T(8,128)(2,1)S(1)}, u32[]{:S(2)}, u32[]{:S(2)}) collective-permute-start(bf16[256,128]{1,0:T(8,128)(2,1)S(1)} %get-tuple-element.54), channel_id=1, source_target_pairs={{0,2},{1,5},{2,0},{3,7},{4,6},{5,1},{6,4},{7,3},{8,10},{9,13},{10,... | collective-permute-start | bytes 196616 | tf_op jit(solution)/shard_map/ppermute | solution.py:421
  75.8 1.2 %collective-permute-start.30 = (bf16[256,128]{1,0:T(8,128)(2,1)S(1)}, bf16[256,128]{1,0:T(8,128)(2,1)S(1)}, u32[]{:S(2)}, u32[]{:S(2)}) collective-permute-start(bf16[256,128]{1,0:T(8,128)(2,1)S(1)} %get-tuple-element.55), channel_id=1, source_target_pairs={{0,4},{1,3},{2,6},{3,1},{4,0},{5,7},{6,2},{7,5},{8,12},{9,11},{10,... | collective-permute-start | bytes 196616 | tf_op jit(solution)/shard_map/ppermute | solution.py:421
  77.0 1.5 %collective-permute-start.31 = (bf16[256,128]{1,0:T(8,128)(2,1)S(1)}, bf16[256,128]{1,0:T(8,128)(2,1)S(1)}, u32[]{:S(2)}, u32[]{:S(2)}) collective-permute-start(bf16[256,128]{1,0:T(8,128)(2,1)S(1)} %get-tuple-element.56), channel_id=1, source_target_pairs={{0,6},{1,7},{2,4},{3,5},{4,2},{5,3},{6,0},{7,1},{8,14},{9,15},{10,... | collective-permute-start | bytes 196616 | tf_op jit(solution)/shard_map/ppermute | solution.py:421
  78.5 1.2 %collective-permute-done.29.refs_1_ = bf16[256,128]{1,0:T(8,128)(2,1)S(1)} collective-permute-done((bf16[256,128]{1,0:T(8,128)(2,1)S(1)}, bf16[256,128]{1,0:T(8,128)(2,1)S(1)}, u32[]{:S(2)}, u32[]{:S(2)}) %collective-permute-start.29) | collective-permute-done | bytes 65568 | tf_op jit(solution)/shard_map/ppermute | solution.py:421
  80.1 2.1 %collective-permute-done.31.refs_3_ = bf16[256,128]{1,0:T(8,128)(2,1)S(1)} collective-permute-done((bf16[256,128]{1,0:T(8,128)(2,1)S(1)}, bf16[256,128]{1,0:T(8,128)(2,1)S(1)}, u32[]{:S(2)}, u32[]{:S(2)}) %collective-permute-start.31) | collective-permute-done | bytes 65568 | tf_op jit(solution)/shard_map/ppermute | solution.py:421
  82.2 0.8 shard_map.184
  (75 shorter events, 5.6 us)
Async XLA Ops:
  1.8 6.0 %collective-permute-start.3 = (bf16[400,128]{1,0:T(8,128)(2,1)S(1)}, bf16[400,128]{1,0:T(8,128)(2,1)S(1)}, u32[]{:S(2)}, u32[]{:S(2)}) collective-permute-start(bf16[400,128]{1,0:T(8,128)(2,1)S(1)} %get-tuple-element.31.pack_ref.refs_0_), channel_id=1, source_target_pairs={{0,8},{2,10},{4,12},{6,14},{8,0},{10,2},{12,4},{14,6},{16,24},{18,... | collective-permute-start | bytes 307208 | tf_op jit(solution)/shard_map/ppermute | solution.py:410
  5.0 10.7 %collective-permute-start.4 = (bf16[400,128]{1,0:T(8,128)(2,1)S(1)}, bf16[400,128]{1,0:T(8,128)(2,1)S(1)}, u32[]{:S(2)}, u32[]{:S(2)}) collective-permute-start(bf16[400,128]{1,0:T(8,128)(2,1)S(1)} %get-tuple-element.31.pack_ref.refs_0_), channel_id=1, source_target_pairs={{0,16},{2,18},{4,20},{6,22},{8,24},{10,26},{12,28},{14,30},{16,0},... | collective-permute-start | bytes 307208 | tf_op jit(solution)/shard_map/ppermute | solution.py:410
  7.5 8.1 %collective-permute-start.5 = (bf16[400,128]{1,0:T(8,128)(2,1)S(1)}, bf16[400,128]{1,0:T(8,128)(2,1)S(1)}, u32[]{:S(2)}, u32[]{:S(2)}) collective-permute-start(bf16[400,128]{1,0:T(8,128)(2,1)S(1)} %get-tuple-element.31.pack_ref.refs_0_), channel_id=1, source_target_pairs={{0,24},{2,26},{4,28},{6,30},{8,16},{10,18},{12,20},{14,22},{16,8},... | collective-permute-start | bytes 307208 | tf_op jit(solution)/shard_map/ppermute | solution.py:410
  15.7 4.5 %collective-permute-start.6 = (bf16[1024,128]{1,0:T(8,128)(2,1)S(1)}, bf16[1024,128]{1,0:T(8,128)(2,1)S(1)}, u32[]{:S(2)}, u32[]{:S(2)}) collective-permute-start(bf16[1024,128]{1,0:T(8,128)(2,1)S(1)} %pad_maximum_fusion), channel_id=1, source_target_pairs={{0,1},{1,0},{2,3},{3,2},{4,5},{5,4},{6,7},{7,6},{8,9},{9,8},{10,11... | collective-permute-start | bytes 786440 | tf_op jit(solution)/shard_map/ppermute | solution.py:404
  15.8 19.8 %collective-permute-start.10 = (bf16[256,1024]{1,0:T(8,128)(2,1)}, bf16[256,1024]{1,0:T(8,128)(2,1)S(1)}, u32[]{:S(2)}, u32[]{:S(2)}) collective-permute-start(bf16[256,1024]{1,0:T(8,128)(2,1)} %refs_8_.3), channel_id=1, source_target_pairs={{0,1},{1,0},{2,3},{3,2},{4,5},{5,4},{6,7},{7,6},{8,9},{9,8},{10,11... | collective-permute-start | bytes 1572872 | tf_op jit(solution)/shard_map/ppermute | solution.py:404
  16.3 21.5 %collective-permute-start.11 = (bf16[256,1024]{1,0:T(8,128)(2,1)}, bf16[256,1024]{1,0:T(8,128)(2,1)S(1)}, u32[]{:S(2)}, u32[]{:S(2)}) collective-permute-start(bf16[256,1024]{1,0:T(8,128)(2,1)} %refs_10_.1), channel_id=1, source_target_pairs={{0,1},{1,0},{2,3},{3,2},{4,5},{5,4},{6,7},{7,6},{8,9},{9,8},{10,11... | collective-permute-start | bytes 1572872 | tf_op jit(solution)/shard_map/ppermute | solution.py:404
  16.4 21.4 %collective-permute-start.12 = (bf16[1024,256]{1,0:T(8,128)(2,1)}, bf16[1024,256]{1,0:T(8,128)(2,1)S(1)}, u32[]{:S(2)}, u32[]{:S(2)}) collective-permute-start(bf16[1024,256]{1,0:T(8,128)(2,1)} %refs_12_.1), channel_id=1, source_target_pairs={{0,1},{1,0},{2,3},{3,2},{4,5},{5,4},{6,7},{7,6},{8,9},{9,8},{10,11... | collective-permute-start | bytes 1572872 | tf_op jit(solution)/shard_map/ppermute | solution.py:404
  16.8 5.4 %collective-permute-start = (bf16[144,128]{1,0:T(8,128)(2,1)S(1)}, bf16[144,128]{1,0:T(8,128)(2,1)S(1)}, u32[]{:S(2)}, u32[]{:S(2)}) collective-permute-start(bf16[144,128]{1,0:T(8,128)(2,1)S(1)} %get-tuple-element.30.refs_0_), channel_id=1, source_target_pairs={{0,2},{1,5},{2,0},{3,7},{4,6},{5,1},{6,4},{7,3},{8,10},{9,13},{10,... | collective-permute-start | bytes 110600 | tf_op jit(solution)/shard_map/ppermute | solution.py:421
  20.2 14.3 %copy-start.2 = (bf16[1024,256]{1,0:T(8,128)(2,1)S(1)}, bf16[1024,256]{1,0:T(8,128)(2,1)}, u32[]{:S(2)}) copy-start(bf16[1024,256]{1,0:T(8,128)(2,1)} %down_a.1) | copy-start | bytes 1572868
  20.2 15.5 %copy-start.9 = (bf16[256,1024]{1,0:T(8,128)(2,1)S(1)}, bf16[256,1024]{1,0:T(8,128)(2,1)}, u32[]{:S(2)}) copy-start(bf16[256,1024]{1,0:T(8,128)(2,1)} %refs_6_.2) | copy-start | bytes 1572868
  20.2 15.5 %copy-start.10 = (bf16[256,1024]{1,0:T(8,128)(2,1)S(1)}, bf16[256,1024]{1,0:T(8,128)(2,1)}, u32[]{:S(2)}) copy-start(bf16[256,1024]{1,0:T(8,128)(2,1)} %refs_8_.2) | copy-start | bytes 1572868
  20.2 4.0 %collective-permute-start.1 = (bf16[144,128]{1,0:T(8,128)(2,1)S(1)}, bf16[144,128]{1,0:T(8,128)(2,1)S(1)}, u32[]{:S(2)}, u32[]{:S(2)}) collective-permute-start(bf16[144,128]{1,0:T(8,128)(2,1)S(1)} %get-tuple-element.30.refs_0_), channel_id=1, source_target_pairs={{0,4},{1,3},{2,6},{3,1},{4,0},{5,7},{6,2},{7,5},{8,12},{9,11},{10,... | collective-permute-start | bytes 110600 | tf_op jit(solution)/shard_map/ppermute | solution.py:421
  22.3 5.0 %collective-permute-start.2 = (bf16[144,128]{1,0:T(8,128)(2,1)S(1)}, bf16[144,128]{1,0:T(8,128)(2,1)S(1)}, u32[]{:S(2)}, u32[]{:S(2)}) collective-permute-start(bf16[144,128]{1,0:T(8,128)(2,1)S(1)} %get-tuple-element.30.refs_0_), channel_id=1, source_target_pairs={{0,6},{1,7},{2,4},{3,5},{4,2},{5,3},{6,0},{7,1},{8,14},{9,15},{10,... | collective-permute-start | bytes 110600 | tf_op jit(solution)/shard_map/ppermute | solution.py:421
  23.8 14.0 %copy-start.3 = (bf16[256,1024]{1,0:T(8,128)(2,1)S(1)}, bf16[256,1024]{1,0:T(8,128)(2,1)}, u32[]{:S(2)}) copy-start(bf16[256,1024]{1,0:T(8,128)(2,1)} %refs_8_.3) | copy-start | bytes 1572868
  23.8 14.0 %copy-start.4 = (bf16[256,1024]{1,0:T(8,128)(2,1)S(1)}, bf16[256,1024]{1,0:T(8,128)(2,1)}, u32[]{:S(2)}) copy-start(bf16[256,1024]{1,0:T(8,128)(2,1)} %refs_10_.1) | copy-start | bytes 1572868
  23.9 14.0 %copy-start.5 = (bf16[1024,256]{1,0:T(8,128)(2,1)S(1)}, bf16[1024,256]{1,0:T(8,128)(2,1)}, u32[]{:S(2)}) copy-start(bf16[1024,256]{1,0:T(8,128)(2,1)} %refs_12_.1) | copy-start | bytes 1572868
  23.9 14.0 %copy-start.8 = (f32[256]{0:T(256)S(1)}, f32[256]{0:T(256)}, u32[]{:S(2)}) copy-start(f32[256]{0:T(256)} %param.22) | copy-start | bytes 3076
  24.2 6.1 %collective-permute-start.7 = (bf16[256,256]{1,0:T(8,128)(2,1)S(1)}, bf16[256,256]{1,0:T(8,128)(2,1)S(1)}, u32[]{:S(2)}, u32[]{:S(2)}) collective-permute-start(bf16[256,256]{1,0:T(8,128)(2,1)S(1)} %get-tuple-element.34), channel_id=1, source_target_pairs={{0,2},{1,5},{2,0},{3,7},{4,6},{5,1},{6,4},{7,3},{8,10},{9,13},{10,... | collective-permute-start | bytes 393224 | tf_op jit(solution)/shard_map/ppermute | solution.py:421
  27.3 7.2 %collective-permute-start.9 = (bf16[256,256]{1,0:T(8,128)(2,1)S(1)}, bf16[256,256]{1,0:T(8,128)(2,1)S(1)}, u32[]{:S(2)}, u32[]{:S(2)}) collective-permute-start(bf16[256,256]{1,0:T(8,128)(2,1)S(1)} %get-tuple-element.36), channel_id=1, source_target_pairs={{0,6},{1,7},{2,4},{3,5},{4,2},{5,3},{6,0},{7,1},{8,14},{9,15},{10,... | collective-permute-start | bytes 393224 | tf_op jit(solution)/shard_map/ppermute | solution.py:421
  30.3 5.3 %collective-permute-start.8 = (bf16[256,256]{1,0:T(8,128)(2,1)S(1)}, bf16[256,256]{1,0:T(8,128)(2,1)S(1)}, u32[]{:S(2)}, u32[]{:S(2)}) collective-permute-start(bf16[256,256]{1,0:T(8,128)(2,1)S(1)} %get-tuple-element.35), channel_id=1, source_target_pairs={{0,4},{1,3},{2,6},{3,1},{4,0},{5,7},{6,2},{7,5},{8,12},{9,11},{10,... | collective-permute-start | bytes 393224 | tf_op jit(solution)/shard_map/ppermute | solution.py:421
  34.5 9.2 %collective-permute-start.18 = (bf16[1024,256]{1,0:T(8,128)(2,1)S(1)}, bf16[1024,256]{1,0:T(8,128)(2,1)S(1)}, u32[]{:S(2)}, u32[]{:S(2)}) collective-permute-start(bf16[1024,256]{1,0:T(8,128)(2,1)S(1)} %copy-done.2), channel_id=1, source_target_pairs={{0,1},{1,0},{2,3},{3,2},{4,5},{5,4},{6,7},{7,6},{8,9},{9,8},{10,11... | collective-permute-start | bytes 1572872 | tf_op jit(solution)/shard_map/ppermute | solution.py:404
  35.6 9.8 %collective-permute-start.19 = (bf16[256,1024]{1,0:T(8,128)(2,1)S(1)}, bf16[256,1024]{1,0:T(8,128)(2,1)S(1)}, u32[]{:S(2)}, u32[]{:S(2)}) collective-permute-start(bf16[256,1024]{1,0:T(8,128)(2,1)S(1)} %copy-done.9), channel_id=1, source_target_pairs={{0,1},{1,0},{2,3},{3,2},{4,5},{5,4},{6,7},{7,6},{8,9},{9,8},{10,11... | collective-permute-start | bytes 1572872 | tf_op jit(solution)/shard_map/ppermute | solution.py:404
  35.6 9.8 %collective-permute-start.20 = (bf16[256,1024]{1,0:T(8,128)(2,1)S(1)}, bf16[256,1024]{1,0:T(8,128)(2,1)S(1)}, u32[]{:S(2)}, u32[]{:S(2)}) collective-permute-start(bf16[256,1024]{1,0:T(8,128)(2,1)S(1)} %copy-done.10), channel_id=1, source_target_pairs={{0,1},{1,0},{2,3},{3,2},{4,5},{5,4},{6,7},{7,6},{8,9},{9,8},{10,11... | collective-permute-start | bytes 1572872 | tf_op jit(solution)/shard_map/ppermute | solution.py:404
  37.8 7.1 %copy-start = (bf16[256,128]{1,0:T(8,128)(2,1)S(1)}, bf16[256,128]{1,0:T(8,128)(2,1)}, u32[]{:S(2)}) copy-start(bf16[256,128]{1,0:T(8,128)(2,1)} %refs_4_.1) | copy-start | bytes 196612
  39.3 9.5 %copy-start.11 = (f32[256]{0:T(256)S(1)}, f32[256]{0:T(256)}, u32[]{:S(2)}) copy-start(f32[256]{0:T(256)} %param.23) | copy-start | bytes 3076
  39.7 1.6 %collective-permute-start.13 = (bf16[512,256]{1,0:T(8,128)(2,1)S(1)}, bf16[512,256]{1,0:T(8,128)(2,1)S(1)}, u32[]{:S(2)}, u32[]{:S(2)}) collective-permute-start(bf16[512,256]{1,0:T(8,128)(2,1)S(1)} %get-tuple-element.39), channel_id=1, source_target_pairs={{0,1},{1,0},{2,3},{3,2},{4,5},{5,4},{6,7},{7,6},{8,9},{9,8},{10,11... | collective-permute-start | bytes 786440 | tf_op jit(solution)/shard_map/ppermute | solution.py:404
  39.9 2.3 %collective-permute-start.17 = (bf16[128,128]{1,0:T(8,128)(2,1)S(1)}, bf16[128,128]{1,0:T(8,128)(2,1)S(1)}, u32[]{:S(2)}, u32[]{:S(2)}) collective-permute-start(bf16[128,128]{1,0:T(8,128)(2,1)S(1)} %get-tuple-element.44), channel_id=1, source_target_pairs={{0,1},{1,0},{2,3},{3,2},{4,5},{5,4},{6,7},{7,6},{8,9},{9,8},{10,11... | collective-permute-start | bytes 98312 | tf_op jit(solution)/shard_map/ppermute | solution.py:404
  41.4 5.0 %collective-permute-start.14 = (bf16[128,256]{1,0:T(8,128)(2,1)S(1)}, bf16[128,256]{1,0:T(8,128)(2,1)S(1)}, u32[]{:S(2)}, u32[]{:S(2)}) collective-permute-start(bf16[128,256]{1,0:T(8,128)(2,1)S(1)} %get-tuple-element.41), channel_id=1, source_target_pairs={{0,2},{1,5},{2,0},{3,7},{4,6},{5,1},{6,4},{7,3},{8,10},{9,13},{10,... | collective-permute-start | bytes 196616 | tf_op jit(solution)/shard_map/ppermute | solution.py:421
  42.2 4.3 %collective-permute-start.15 = (bf16[128,256]{1,0:T(8,128)(2,1)S(1)}, bf16[128,256]{1,0:T(8,128)(2,1)S(1)}, u32[]{:S(2)}, u32[]{:S(2)}) collective-permute-start(bf16[128,256]{1,0:T(8,128)(2,1)S(1)} %get-tuple-element.42), channel_id=1, source_target_pairs={{0,4},{1,3},{2,6},{3,1},{4,0},{5,7},{6,2},{7,5},{8,12},{9,11},{10,... | collective-permute-start | bytes 196616 | tf_op jit(solution)/shard_map/ppermute | solution.py:421
  43.7 5.2 %collective-permute-start.16 = (bf16[128,256]{1,0:T(8,128)(2,1)S(1)}, bf16[128,256]{1,0:T(8,128)(2,1)S(1)}, u32[]{:S(2)}, u32[]{:S(2)}) collective-permute-start(bf16[128,256]{1,0:T(8,128)(2,1)S(1)} %get-tuple-element.43), channel_id=1, source_target_pairs={{0,6},{1,7},{2,4},{3,5},{4,2},{5,3},{6,0},{7,1},{8,14},{9,15},{10,... | collective-permute-start | bytes 196616 | tf_op jit(solution)/shard_map/ppermute | solution.py:421
  50.7 4.7 %collective-permute-start.21 = (bf16[128,256]{1,0:T(8,128)(2,1)S(1)}, bf16[128,256]{1,0:T(8,128)(2,1)S(1)}, u32[]{:S(2)}, u32[]{:S(2)}) collective-permute-start(bf16[128,256]{1,0:T(8,128)(2,1)S(1)} %shard_map.177), channel_id=1, source_target_pairs={{0,8},{2,10},{4,12},{6,14},{8,0},{10,2},{12,4},{14,6},{16,24},{18,... | collective-permute-start | bytes 196616 | tf_op jit(solution)/shard_map/ppermute | solution.py:410
  52.4 6.0 %collective-permute-start.22 = (bf16[128,256]{1,0:T(8,128)(2,1)S(1)}, bf16[128,256]{1,0:T(8,128)(2,1)S(1)}, u32[]{:S(2)}, u32[]{:S(2)}) collective-permute-start(bf16[128,256]{1,0:T(8,128)(2,1)S(1)} %shard_map.177), channel_id=1, source_target_pairs={{0,16},{2,18},{4,20},{6,22},{8,24},{10,26},{12,28},{14,30},{16,0},... | collective-permute-start | bytes 196616 | tf_op jit(solution)/shard_map/ppermute | solution.py:410
  53.8 6.1 %collective-permute-start.23 = (bf16[128,256]{1,0:T(8,128)(2,1)S(1)}, bf16[128,256]{1,0:T(8,128)(2,1)S(1)}, u32[]{:S(2)}, u32[]{:S(2)}) collective-permute-start(bf16[128,256]{1,0:T(8,128)(2,1)S(1)} %shard_map.177), channel_id=1, source_target_pairs={{0,24},{2,26},{4,28},{6,30},{8,16},{10,18},{12,20},{14,22},{16,8},... | collective-permute-start | bytes 196616 | tf_op jit(solution)/shard_map/ppermute | solution.py:410
  59.8 1.6 %collective-permute-start.24 = (bf16[512,256]{1,0:T(8,128)(2,1)S(1)}, bf16[512,256]{1,0:T(8,128)(2,1)S(1)}, u32[]{:S(2)}, u32[]{:S(2)}) collective-permute-start(bf16[512,256]{1,0:T(8,128)(2,1)S(1)} %pad_maximum_fusion.1.own_ref), channel_id=1, source_target_pairs={{0,1},{1,0},{2,3},{3,2},{4,5},{5,4},{6,7},{7,6},{8,9},{9,8},{10,11... | collective-permute-start | bytes 786440 | tf_op jit(solution)/shard_map/ppermute | solution.py:404
  61.7 6.7 %collective-permute-start.26 = (bf16[256,256]{1,0:T(8,128)(2,1)S(1)}, bf16[256,256]{1,0:T(8,128)(2,1)S(1)}, u32[]{:S(2)}, u32[]{:S(2)}) collective-permute-start(bf16[256,256]{1,0:T(8,128)(2,1)S(1)} %shard_map.180), channel_id=1, source_target_pairs={{0,4},{1,3},{2,6},{3,1},{4,0},{5,7},{6,2},{7,5},{8,12},{9,11},{10,... | collective-permute-start | bytes 393224 | tf_op jit(solution)/shard_map/ppermute | solution.py:421
  62.8 6.1 %collective-permute-start.25 = (bf16[256,256]{1,0:T(8,128)(2,1)S(1)}, bf16[256,256]{1,0:T(8,128)(2,1)S(1)}, u32[]{:S(2)}, u32[]{:S(2)}) collective-permute-start(bf16[256,256]{1,0:T(8,128)(2,1)S(1)} %get-tuple-element.46), channel_id=1, source_target_pairs={{0,2},{1,5},{2,0},{3,7},{4,6},{5,1},{6,4},{7,3},{8,10},{9,13},{10,... | collective-permute-start | bytes 393224 | tf_op jit(solution)/shard_map/ppermute | solution.py:421
  64.2 7.3 %collective-permute-start.27 = (bf16[256,256]{1,0:T(8,128)(2,1)S(1)}, bf16[256,256]{1,0:T(8,128)(2,1)S(1)}, u32[]{:S(2)}, u32[]{:S(2)}) collective-permute-start(bf16[256,256]{1,0:T(8,128)(2,1)S(1)} %get-tuple-element.47), channel_id=1, source_target_pairs={{0,6},{1,7},{2,4},{3,5},{4,2},{5,3},{6,0},{7,1},{8,14},{9,15},{10,... | collective-permute-start | bytes 393224 | tf_op jit(solution)/shard_map/ppermute | solution.py:421
  71.4 10.7 %copy-start.1 = (f32[256,128]{1,0:T(8,128)S(1)}, f32[256,128]{1,0:T(8,128)}, u32[]{:S(2)}) copy-start(f32[256,128]{1,0:T(8,128)} %refs_5_.3) | copy-start | bytes 393220
  71.4 10.7 %copy-start.6 = (f32[256,128]{1,0:T(8,128)S(1)}, f32[256,128]{1,0:T(8,128)}, u32[]{:S(2)}) copy-start(f32[256,128]{1,0:T(8,128)} %refs_6_.3) | copy-start | bytes 393220
  71.4 10.7 %copy-start.7 = (f32[256,128]{1,0:T(8,128)S(1)}, f32[256,128]{1,0:T(8,128)}, u32[]{:S(2)}) copy-start(f32[256,128]{1,0:T(8,128)} %refs_7_.3) | copy-start | bytes 393220
  73.3 1.6 %collective-permute-start.28 = (bf16[1024,128]{1,0:T(8,128)(2,1)S(1)}, bf16[1024,128]{1,0:T(8,128)(2,1)S(1)}, u32[]{:S(2)}, u32[]{:S(2)}) collective-permute-start(bf16[1024,128]{1,0:T(8,128)(2,1)S(1)} %get-tuple-element.52), channel_id=1, source_target_pairs={{0,1},{1,0},{2,3},{3,2},{4,5},{5,4},{6,7},{7,6},{8,9},{9,8},{10,11... | collective-permute-start | bytes 786440 | tf_op jit(solution)/shard_map/ppermute | solution.py:404
  75.0 4.8 %collective-permute-start.29 = (bf16[256,128]{1,0:T(8,128)(2,1)S(1)}, bf16[256,128]{1,0:T(8,128)(2,1)S(1)}, u32[]{:S(2)}, u32[]{:S(2)}) collective-permute-start(bf16[256,128]{1,0:T(8,128)(2,1)S(1)} %get-tuple-element.54), channel_id=1, source_target_pairs={{0,2},{1,5},{2,0},{3,7},{4,6},{5,1},{6,4},{7,3},{8,10},{9,13},{10,... | collective-permute-start | bytes 196616 | tf_op jit(solution)/shard_map/ppermute | solution.py:421
  75.8 4.3 %collective-permute-start.30 = (bf16[256,128]{1,0:T(8,128)(2,1)S(1)}, bf16[256,128]{1,0:T(8,128)(2,1)S(1)}, u32[]{:S(2)}, u32[]{:S(2)}) collective-permute-start(bf16[256,128]{1,0:T(8,128)(2,1)S(1)} %get-tuple-element.55), channel_id=1, source_target_pairs={{0,4},{1,3},{2,6},{3,1},{4,0},{5,7},{6,2},{7,5},{8,12},{9,11},{10,... | collective-permute-start | bytes 196616 | tf_op jit(solution)/shard_map/ppermute | solution.py:421
  77.0 5.2 %collective-permute-start.31 = (bf16[256,128]{1,0:T(8,128)(2,1)S(1)}, bf16[256,128]{1,0:T(8,128)(2,1)S(1)}, u32[]{:S(2)}, u32[]{:S(2)}) collective-permute-start(bf16[256,128]{1,0:T(8,128)(2,1)S(1)} %get-tuple-element.56), channel_id=1, source_target_pairs={{0,6},{1,7},{2,4},{3,5},{4,2},{5,3},{6,0},{7,1},{8,14},{9,15},{10,... | collective-permute-start | bytes 196616 | tf_op jit(solution)/shard_map/ppermute | solution.py:421

commit v5 on v4

--- a/solution.py
+++ b/solution.py
@@ -260,7 +260,7 @@
 def basket_body(*refs, groups):
     parts = refs[:groups]
     gain_ref, gate_a, gate_b, up_a, up_b, down_a, down_b = refs[groups : groups + 7]
-    out_ref, sum_ref, value_ref, slope_ref = refs[groups + 7 :]
+    out_ref, sum_ref, gate_ref, up_ref = refs[groups + 7 :]
     total = add_all(parts)
     sum_ref[...] = total
     normed = total * rms(total) * gain_ref[...]
@@ -274,22 +274,37 @@
             sig = sigmoid(gate_pre)
             value = gate_pre * sig
             acc = acc + dot((value * up_pre).astype(BF16), down[c : c + CHUNK, :])
-            value_ref[:, at : at + CHUNK] = value.astype(BF16)
-            slope_ref[:, at : at + CHUNK] = (up_pre * (sig + value * (1.0 - sig))).astype(BF16)
+            gate_ref[:, at : at + CHUNK] = gate_pre
+            up_ref[:, at : at + CHUNK] = up_pre
             at += CHUNK
     out_ref[...] = acc.astype(BF16)
 
 
-def message_body(mo_ref, out_ref, mine_ref, theirs_ref, all_ref, *, peers):
-    all_ref[...] = dot(mo_ref[...], out_ref[...])
+def slopes_body(gate_ref, up_ref, value_ref, slope_ref):
+    for c in range(0, gate_ref.shape[1], 256):
+        gate_pre = gate_ref[:, c : c + 256]
+        sig = sigmoid(gate_pre)
+        value = gate_pre * sig
+        value_ref[:, c : c + 256] = value.astype(BF16)
+        slope = up_ref[:, c : c + 256] * (sig + value * (1.0 - sig))
+        slope_ref[:, c : c + 256] = slope.astype(BF16)
+
+
+def message_theirs_body(mo_ref, out_ref, theirs_ref, *, peers):
+    rows = theirs_ref.shape[0] // peers
+    core = lax.axis_index("mp")
+    for l in range(peers):
+        at = pl.ds(pl.multiple_of((2 * l + 1 - core) * rows, rows), rows)
+        to = slice(crossed(l) * rows, (crossed(l) + 1) * rows)
+        theirs_ref[to, :] = dot(mo_ref[at, :], out_ref[...]).astype(BF16)
+
+
+def message_mine_body(mo_ref, out_ref, mine_ref, *, peers):
     rows = mine_ref.shape[0] // peers
     core = lax.axis_index("mp")
     for l in range(peers):
-        mine = pl.multiple_of((2 * l + core) * rows, rows)
-        theirs = pl.multiple_of((2 * l + 1 - core) * rows, rows)
-        mine_ref[l * rows : (l + 1) * rows, :] = all_ref[pl.ds(mine, rows), :]
-        to = slice(crossed(l) * rows, (crossed(l) + 1) * rows)
-        theirs_ref[to, :] = all_ref[pl.ds(theirs, rows), :].astype(BF16)
+        at = pl.ds(pl.multiple_of((2 * l + core) * rows, rows), rows)
+        mine_ref[l * rows : (l + 1) * rows, :] = dot(mo_ref[at, :], out_ref[...])
 
 
 def join_body(mine_ref, other_ref, *out_refs):
@@ -350,16 +365,21 @@
     out_ref[...] = (scale * weighted - total * (cubed * inner)).astype(BF16)
 
 
-def back_body(mo_ref, sum_ref, mine_ref, theirs_ref, all_ref, *, peers):
-    all_ref[...] = dot(mo_ref[...], sum_ref[...])
+def back_theirs_body(mo_ref, sum_ref, theirs_ref, *, peers):
+    width = theirs_ref.shape[1]
+    core = lax.axis_index("mp")
+    rows = theirs_ref.shape[0] // peers
+    wanted = sum_ref[:, pl.ds(pl.multiple_of((1 - core) * width, width), width)]
+    for l in range(peers):
+        to = slice(crossed(l) * rows, (crossed(l) + 1) * rows)
+        theirs_ref[to, :] = dot(mo_ref[l * rows : (l + 1) * rows, :], wanted).astype(BF16)
+
+
+def back_mine_body(mo_ref, sum_ref, mine_ref):
     width = mine_ref.shape[1]
     core = lax.axis_index("mp")
-    mine_ref[...] = all_ref[:, pl.ds(pl.multiple_of(core * width, width), width)]
-    rows = mine_ref.shape[0] // peers
-    theirs = pl.ds(pl.multiple_of((1 - core) * width, width), width)
-    for l in range(peers):
-        to = slice(crossed(l) * rows, (crossed(l) + 1) * rows)
-        theirs_ref[to, :] = all_ref[l * rows : (l + 1) * rows, theirs].astype(BF16)
+    wanted = sum_ref[:, pl.ds(pl.multiple_of(core * width, width), width)]
+    mine_ref[...] = dot(mo_ref[...], wanted)
 
 
 def adam_body(*refs, peers):
@@ -442,7 +462,11 @@
     )
     packs = [pack] + gather(pack)
     spread = run(
-        spread_body, sds((2 * tiles * words, tiles * BLOCK), BF16), (), (pack,), flops=1 << 29
+        spread_body,
+        sds((2 * tiles * words, tiles * BLOCK), BF16),
+        (),
+        (pack,),
+        flops=1 << 29,
     )
     cot_other = swap(cot_send)
     gate_b, up_b, down_b = gate_basket, up_basket, down_basket
@@ -491,15 +515,17 @@
         (*incs, spread),
         flops=1 << 29,
     )
-    mo = run(turn_body, sds((groups * items, per), BF16), (), (mt_plane,), flops=1 << 28)
+    mo = run(
+        turn_body, sds((groups * items, per), BF16), (), (mt_plane,), flops=1 << 28
+    )
     gate_io, up_io, down_io = swap(gate_item), swap(up_item), swap(down_item)
-    basket_out, basket_sum, value, slope = run(
+    basket_out, basket_sum, gate_pre, up_pre = run(
         functools.partial(basket_body, groups=groups),
         [
             sds((per, features), BF16),
             sds((per, features), F32),
-            sds((per, hidden), BF16),
-            sds((per, hidden), BF16),
+            sds((per, hidden), F32),
+            sds((per, hidden), F32),
         ],
         (),
         (
@@ -514,13 +540,26 @@
         ),
         flops=1 << 30,
     )
-    message_mine, message_theirs = run(
-        functools.partial(message_body, peers=groups),
-        [sds((groups * item_half, features), F32), sds((groups * item_half, features), BF16)],
+    value, slope = run(
+        slopes_body,
+        [sds((per, hidden), BF16)] * 2,
+        (),
+        (gate_pre, up_pre),
+        flops=1 << 29,
+    )
+    message_theirs = run(
+        functools.partial(message_theirs_body, peers=groups),
+        sds((groups * item_half, features), BF16),
         (),
         (mo, basket_out),
-        scratch=[pltpu.VMEM((groups * items, features), F32)],
-        flops=1 << 28,
+        flops=1 << 27,
+    )
+    message_mine = run(
+        functools.partial(message_mine_body, peers=groups),
+        sds((groups * item_half, features), F32),
+        (),
+        (mo, basket_out),
+        flops=1 << 27,
     )
     message_other = swap(message_theirs)
     item_hidden = run(
@@ -556,7 +595,11 @@
     grads = jnp.concatenate(grads, axis=0)
     grads_other = swap(grads)
     grad_acc = run(
-        grad_own_body, sds((shards * half, features), F32), (), (mt, grads), flops=1 << 28
+        grad_own_body,
+        sds((shards * half, features), F32),
+        (),
+        (mt, grads),
+        flops=1 << 28,
     )
     (lead_part,) = run(
         functools.partial(grad_sums_body, which=[lead]),
@@ -593,13 +636,19 @@
         ),
         flops=1 << 30,
     )
-    back_mine, back_theirs = run(
-        functools.partial(back_body, peers=groups),
-        [sds((groups * items, width), F32), sds((groups * items, width), BF16)],
+    back_theirs = run(
+        functools.partial(back_theirs_body, peers=groups),
+        sds((groups * items, width), BF16),
         (),
         (mo, grad_sum),
-        scratch=[pltpu.VMEM((groups * items, features), F32)],
-        flops=1 << 28,
+        flops=1 << 27,
+    )
+    back_mine = run(
+        back_mine_body,
+        sds((groups * items, width), F32),
+        (),
+        (mo, grad_sum),
+        flops=1 << 27,
     )
     back_other = swap(back_theirs)
     backs = run(

time: 83.2 us -> 87.9 us (1.056)
  waiting for transfers between devices: 37.8 us -> 40.1 us
  starting transfers between devices: 30.4 us -> 31.9 us
  Pallas kernels: 13.6 us -> 14.5 us
    ppermute x15, waiting for transfers between devices: 21.3 us -> 25.3 us  [exchange(): got.append(lax.ppermute(xs[k], ('shard', 'mp'), pairs))]
    ppermute x15, starting transfers between devices: 17.9 us -> 19.4 us  [exchange(): got.append(lax.ppermute(xs[k], ('shard', 'mp'), pairs))]
    ppermute x6, waiting for transfers between devices: 12.8 us -> 11.7 us  [gather(): got.append(lax.ppermute(x, 'shard', pairs))]
    pallas_call x19 -> x22, Pallas kernels: 13.6 us -> 14.5 us  [run(): return call(*far, *smem, *args)]
  transfers between devices with their start and end apart: 32 -> 32, of which waited for: 22 -> 20; matrix products, arithmetic and copies ran while one was open for 0% -> 0% of each run, Pallas kernels for 9% -> 10%
where the time goes in v5:
time: 87.9 us; the launch traced here: 87.8 us
  waiting for transfers between devices  40.1 us (46%)
  starting transfers between devices  31.9 us (36%)
  Pallas kernels  14.5 us (16%)
  between operations  1.06 us (1%)
    ppermute x15, waiting for transfers between devices, exchange(): got.append(lax.ppermute(xs[k], ('shard', 'mp'), pairs))  25.3 us
    ppermute x15, starting transfers between devices, exchange(): got.append(lax.ppermute(xs[k], ('shard', 'mp'), pairs))  19.4 us
    pallas_call x22, Pallas kernels, run(): return call(*far, *smem, *args)  14.5 us
    ppermute x6, waiting for transfers between devices, gather(): got.append(lax.ppermute(x, 'shard', pairs))  11.7 us
    ppermute x6, starting transfers between devices, gather(): got.append(lax.ppermute(x, 'shard', pairs))  10.2 us
    ppermute x11, waiting for transfers between devices, swap(): return lax.ppermute(x, 'mp', [(0, 1), (1, 0)])  3.12 us
    ppermute x11, starting transfers between devices, swap(): return lax.ppermute(x, 'mp', [(0, 1), (1, 0)])  2.3 us
  transfers between devices with their start and end apart: 32, of which 20 were waited for; matrix products, arithmetic and copies ran while one was open for 0% of the time, Pallas kernels for 10%

profile of v5, /device:TPU:0, one launch (start us, length us, event | category | flops | bytes accessed | tf_op | source)
XLA Modules:
  0.0 87.8 jit_solution(11496316247271217374)
XLA Ops:
  0.6 1.2 %shard_map.166 = (bf16[400,128]{1,0:T(8,128)(2,1)S(1)}, bf16[144,128]{1,0:T(8,128)(2,1)S(1)}, bf16[128,128]{1,0:T(8,128)(2,1)S(1)}) custom-call(s32[16]{0:T(128)} %dest_hbm.1, s32[16]{0:T(128)} %item_hbm.1, s32[128,128]{1,0:T(8,128)} %bitcast.6, f32[256,128]{1,0:T(8,128)} %refs_5_.3, bf16[256,128]{1,0:T(8,128)(2,1)} %refs_4_.1), custom_call_target="tpu_custom_call" | custom-call | flops 1048576 | bytes 1048576 | tf_op jit(solution)/shard_map/pallas_call | solution.py:51
  1.8 5.1 %collective-permute-start.5 = (bf16[400,128]{1,0:T(8,128)(2,1)S(1)}, bf16[400,128]{1,0:T(8,128)(2,1)S(1)}, u32[]{:S(2)}, u32[]{:S(2)}) collective-permute-start(bf16[400,128]{1,0:T(8,128)(2,1)S(1)} %get-tuple-element.29.pack_ref.refs_0_), channel_id=1, source_target_pairs={{0,24},{2,26},{4,28},{6,30},{8,16},{10,18},{12,20},{14,22},{16,8},... | collective-permute-start | bytes 307208 | tf_op jit(solution)/shard_map/ppermute | solution.py:430
  7.0 0.6 collective-permute-start.3
  7.6 3.2 %collective-permute-done.5.refs_3_ = bf16[400,128]{1,0:T(8,128)(2,1)S(1)} collective-permute-done((bf16[400,128]{1,0:T(8,128)(2,1)S(1)}, bf16[400,128]{1,0:T(8,128)(2,1)S(1)}, u32[]{:S(2)}, u32[]{:S(2)}) %collective-permute-start.5) | collective-permute-done | bytes 102432 | tf_op jit(solution)/shard_map/ppermute | solution.py:430
  10.8 4.8 %collective-permute-done.4.refs_2_ = bf16[400,128]{1,0:T(8,128)(2,1)S(1)} collective-permute-done((bf16[400,128]{1,0:T(8,128)(2,1)S(1)}, bf16[400,128]{1,0:T(8,128)(2,1)S(1)}, u32[]{:S(2)}, u32[]{:S(2)}) %collective-permute-start.4) | collective-permute-done | bytes 102432 | tf_op jit(solution)/shard_map/ppermute | solution.py:430
  17.0 1.6 %shard_map.170.mt_ref = bf16[1024,1024]{1,0:T(8,128)(2,1)S(1)} custom-call(s32[4,128]{1,0:T(4,128)S(1)} %maximum_convert_fusion.1.idx_ref, bf16[400,128]{1,0:T(8,128)(2,1)S(1)} %get-tuple-element.29.pack_ref.refs_0_, bf16[400,128]{1,0:T(8,128)(2,1)S(1)} %collective-permute-done.3.refs_1_, bf16[400,128]{1,0:T(8,128)(2,1)S(1)} %collective-permute-done.4.refs_2_, ...), custom_call_target="tpu_custom_call" | custom-call | flops 536870912 | bytes 1048576 | tf_op jit(solution)/shard_map/pallas_call | solution.py:51
  19.1 0.6 shard_map.172
  19.7 1.6 %collective-permute-start.7 = (bf16[256,256]{1,0:T(8,128)(2,1)S(1)}, bf16[256,256]{1,0:T(8,128)(2,1)S(1)}, u32[]{:S(2)}, u32[]{:S(2)}) collective-permute-start(bf16[256,256]{1,0:T(8,128)(2,1)S(1)} %get-tuple-element.32), channel_id=1, source_target_pairs={{0,2},{1,5},{2,0},{3,7},{4,6},{5,1},{6,4},{7,3},{8,10},{9,13},{10,... | collective-permute-start | bytes 393224 | tf_op jit(solution)/shard_map/ppermute | solution.py:441
  21.3 1.5 %collective-permute-start.2 = (bf16[144,128]{1,0:T(8,128)(2,1)S(1)}, bf16[144,128]{1,0:T(8,128)(2,1)S(1)}, u32[]{:S(2)}, u32[]{:S(2)}) collective-permute-start(bf16[144,128]{1,0:T(8,128)(2,1)S(1)} %get-tuple-element.28.refs_0_), channel_id=1, source_target_pairs={{0,6},{1,7},{2,4},{3,5},{4,2},{5,3},{6,0},{7,1},{8,14},{9,15},{10,... | collective-permute-start | bytes 110600 | tf_op jit(solution)/shard_map/ppermute | solution.py:441
  22.8 3.7 %collective-permute-done.2.refs_3_ = bf16[144,128]{1,0:T(8,128)(2,1)S(1)} collective-permute-done((bf16[144,128]{1,0:T(8,128)(2,1)S(1)}, bf16[144,128]{1,0:T(8,128)(2,1)S(1)}, u32[]{:S(2)}, u32[]{:S(2)}) %collective-permute-start.2) | collective-permute-done | bytes 36896 | tf_op jit(solution)/shard_map/ppermute | solution.py:441
  26.5 1.2 %collective-permute-start.1 = (bf16[144,128]{1,0:T(8,128)(2,1)S(1)}, bf16[144,128]{1,0:T(8,128)(2,1)S(1)}, u32[]{:S(2)}, u32[]{:S(2)}) collective-permute-start(bf16[144,128]{1,0:T(8,128)(2,1)S(1)} %get-tuple-element.28.refs_0_), channel_id=1, source_target_pairs={{0,4},{1,3},{2,6},{3,1},{4,0},{5,7},{6,2},{7,5},{8,12},{9,11},{10,... | collective-permute-start | bytes 110600 | tf_op jit(solution)/shard_map/ppermute | solution.py:441
  27.7 2.8 %collective-permute-done.1.refs_2_ = bf16[144,128]{1,0:T(8,128)(2,1)S(1)} collective-permute-done((bf16[144,128]{1,0:T(8,128)(2,1)S(1)}, bf16[144,128]{1,0:T(8,128)(2,1)S(1)}, u32[]{:S(2)}, u32[]{:S(2)}) %collective-permute-start.1) | collective-permute-done | bytes 36896 | tf_op jit(solution)/shard_map/ppermute | solution.py:441
  30.5 1.5 %collective-permute-start = (bf16[144,128]{1,0:T(8,128)(2,1)S(1)}, bf16[144,128]{1,0:T(8,128)(2,1)S(1)}, u32[]{:S(2)}, u32[]{:S(2)}) collective-permute-start(bf16[144,128]{1,0:T(8,128)(2,1)S(1)} %get-tuple-element.28.refs_0_), channel_id=1, source_target_pairs={{0,2},{1,5},{2,0},{3,7},{4,6},{5,1},{6,4},{7,3},{8,10},{9,13},{10,... | collective-permute-start | bytes 110600 | tf_op jit(solution)/shard_map/ppermute | solution.py:441
  32.0 2.8 %collective-permute-done.refs_1_ = bf16[144,128]{1,0:T(8,128)(2,1)S(1)} collective-permute-done((bf16[144,128]{1,0:T(8,128)(2,1)S(1)}, bf16[144,128]{1,0:T(8,128)(2,1)S(1)}, u32[]{:S(2)}, u32[]{:S(2)}) %collective-permute-start) | collective-permute-done | bytes 36896 | tf_op jit(solution)/shard_map/ppermute | solution.py:441
  34.8 1.4 %collective-permute-start.8 = (bf16[256,256]{1,0:T(8,128)(2,1)S(1)}, bf16[256,256]{1,0:T(8,128)(2,1)S(1)}, u32[]{:S(2)}, u32[]{:S(2)}) collective-permute-start(bf16[256,256]{1,0:T(8,128)(2,1)S(1)} %get-tuple-element.33), channel_id=1, source_target_pairs={{0,4},{1,3},{2,6},{3,1},{4,0},{5,7},{6,2},{7,5},{8,12},{9,11},{10,... | collective-permute-start | bytes 393224 | tf_op jit(solution)/shard_map/ppermute | solution.py:441
  36.2 1.5 %collective-permute-start.9 = (bf16[256,256]{1,0:T(8,128)(2,1)S(1)}, bf16[256,256]{1,0:T(8,128)(2,1)S(1)}, u32[]{:S(2)}, u32[]{:S(2)}) collective-permute-start(bf16[256,256]{1,0:T(8,128)(2,1)S(1)} %get-tuple-element.34), channel_id=1, source_target_pairs={{0,6},{1,7},{2,4},{3,5},{4,2},{5,3},{6,0},{7,1},{8,14},{9,15},{10,... | collective-permute-start | bytes 393224 | tf_op jit(solution)/shard_map/ppermute | solution.py:441
  37.8 2.0 %collective-permute-done.8.refs_2_ = bf16[256,256]{1,0:T(8,128)(2,1)S(1)} collective-permute-done((bf16[256,256]{1,0:T(8,128)(2,1)S(1)}, bf16[256,256]{1,0:T(8,128)(2,1)S(1)}, u32[]{:S(2)}, u32[]{:S(2)}) %collective-permute-start.8) | collective-permute-done | bytes 131104 | tf_op jit(solution)/shard_map/ppermute | solution.py:441
  39.8 2.3 %collective-permute-done.9.refs_3_ = bf16[256,256]{1,0:T(8,128)(2,1)S(1)} collective-permute-done((bf16[256,256]{1,0:T(8,128)(2,1)S(1)}, bf16[256,256]{1,0:T(8,128)(2,1)S(1)}, u32[]{:S(2)}, u32[]{:S(2)}) %collective-permute-start.9) | collective-permute-done | bytes 131104 | tf_op jit(solution)/shard_map/ppermute | solution.py:441
  42.1 0.5 collective-permute-start.20
  42.7 1.4 %shard_map.168.mt_ref = bf16[320,1024]{1,0:T(8,128)(2,1)S(1)} custom-call(s32[4,128]{1,0:T(4,128)S(1)} %maximum_convert_fusion.idx_ref, bf16[144,128]{1,0:T(8,128)(2,1)S(1)} %get-tuple-element.28.refs_0_, bf16[144,128]{1,0:T(8,128)(2,1)S(1)} %collective-permute-done.refs_1_, bf16[144,128]{1,0:T(8,128)(2,1)S(1)} %collective-permute-done.1.refs_2_, ...), custom_call_target="tpu_custom_call" | custom-call | flops 536870912 | bytes 1048576 | tf_op jit(solution)/shard_map/pallas_call | solution.py:51
  44.4 1.3 %shard_map.173 = (bf16[256,256]{1,0:T(8,128)(2,1)S(1)}, f32[256,256]{1,0:T(8,128)S(1)}, f32[256,2048]{1,0:T(8,128)S(1)}, f32[256,2048]{1,0:T(8,128)S(1)}) custom-call(f32[256,256]{1,0:T(8,128)S(1)} %get-tuple-element.31.refs_0_, bf16[256,256]{1,0:T(8,128)(2,1)S(1)} %collective-permute-done.7.refs_1_, bf16[256,256]{1,0:T(8,128)(2,1)S(1)} %collective-permute-done.8.refs_2_, ...), custom_call_target="tpu_custom_call" | custom-call | flops 1073741824 | bytes 1048576 | tf_op jit(solution)/shard_map/pallas_call | solution.py:51
  46.7 0.8 collective-permute-done.13.other_ref
  47.6 0.6 collective-permute-start.14
  48.2 1.5 %collective-permute-start.15 = (bf16[128,256]{1,0:T(8,128)(2,1)S(1)}, bf16[128,256]{1,0:T(8,128)(2,1)S(1)}, u32[]{:S(2)}, u32[]{:S(2)}) collective-permute-start(bf16[128,256]{1,0:T(8,128)(2,1)S(1)} %get-tuple-element.38), channel_id=1, source_target_pairs={{0,4},{1,3},{2,6},{3,1},{4,0},{5,7},{6,2},{7,5},{8,12},{9,11},{10,... | collective-permute-start | bytes 196616 | tf_op jit(solution)/shard_map/ppermute | solution.py:441
  49.8 1.4 %collective-permute-start.16 = (bf16[128,256]{1,0:T(8,128)(2,1)S(1)}, bf16[128,256]{1,0:T(8,128)(2,1)S(1)}, u32[]{:S(2)}, u32[]{:S(2)}) collective-permute-start(bf16[128,256]{1,0:T(8,128)(2,1)S(1)} %get-tuple-element.39), channel_id=1, source_target_pairs={{0,6},{1,7},{2,4},{3,5},{4,2},{5,3},{6,0},{7,1},{8,14},{9,15},{10,... | collective-permute-start | bytes 196616 | tf_op jit(solution)/shard_map/ppermute | solution.py:441
  51.7 0.7 collective-permute-done.14.refs_1_
  52.5 2.4 %collective-permute-done.16.refs_3_ = bf16[128,256]{1,0:T(8,128)(2,1)S(1)} collective-permute-done((bf16[128,256]{1,0:T(8,128)(2,1)S(1)}, bf16[128,256]{1,0:T(8,128)(2,1)S(1)}, u32[]{:S(2)}, u32[]{:S(2)}) %collective-permute-start.16) | collective-permute-done | bytes 65568 | tf_op jit(solution)/shard_map/ppermute | solution.py:441
  54.9 1.8 %shard_map.178 = bf16[128,256]{1,0:T(8,128)(2,1)S(1)} custom-call(f32[128,256]{1,0:T(8,128)S(1)} %get-tuple-element.36.refs_0_, bf16[128,256]{1,0:T(8,128)(2,1)S(1)} %collective-permute-done.14.refs_1_, bf16[128,256]{1,0:T(8,128)(2,1)S(1)} %collective-permute-done.15.refs_2_, bf16[128,256]{1,0:T(8,128)(2,1)S(1)} %collective-permute-done.16.refs_3_, ...), custom_call_target="tpu_custom_call" | custom-call | flops 1073741824 | bytes 1048576 | tf_op jit(solution)/shard_map/pallas_call | solution.py:51
  56.8 2.5 %collective-permute-start.23 = (bf16[128,256]{1,0:T(8,128)(2,1)S(1)}, bf16[128,256]{1,0:T(8,128)(2,1)S(1)}, u32[]{:S(2)}, u32[]{:S(2)}) collective-permute-start(bf16[128,256]{1,0:T(8,128)(2,1)S(1)} %shard_map.178), channel_id=1, source_target_pairs={{0,24},{2,26},{4,28},{6,30},{8,16},{10,18},{12,20},{14,22},{16,8},... | collective-permute-start | bytes 196616 | tf_op jit(solution)/shard_map/ppermute | solution.py:430
  59.3 1.9 %collective-permute-start.21 = (bf16[128,256]{1,0:T(8,128)(2,1)S(1)}, bf16[128,256]{1,0:T(8,128)(2,1)S(1)}, u32[]{:S(2)}, u32[]{:S(2)}) collective-permute-start(bf16[128,256]{1,0:T(8,128)(2,1)S(1)} %shard_map.178), channel_id=1, source_target_pairs={{0,8},{2,10},{4,12},{6,14},{8,0},{10,2},{12,4},{14,6},{16,24},{18,... | collective-permute-start | bytes 196616 | tf_op jit(solution)/shard_map/ppermute | solution.py:430
  61.2 2.4 %collective-permute-done.23 = bf16[128,256]{1,0:T(8,128)(2,1)S(1)} collective-permute-done((bf16[128,256]{1,0:T(8,128)(2,1)S(1)}, bf16[128,256]{1,0:T(8,128)(2,1)S(1)}, u32[]{:S(2)}, u32[]{:S(2)}) %collective-permute-start.23) | collective-permute-done | bytes 65568 | tf_op jit(solution)/shard_map/ppermute | solution.py:430
  63.6 1.3 %collective-permute-done.22 = bf16[128,256]{1,0:T(8,128)(2,1)S(1)} collective-permute-done((bf16[128,256]{1,0:T(8,128)(2,1)S(1)}, bf16[128,256]{1,0:T(8,128)(2,1)S(1)}, u32[]{:S(2)}, u32[]{:S(2)}) %collective-permute-start.22) | collective-permute-done | bytes 65568 | tf_op jit(solution)/shard_map/ppermute | solution.py:430
  65.5 1.1 %collective-permute-done.24.other_ref = bf16[512,256]{1,0:T(8,128)(2,1)S(1)} collective-permute-done((bf16[512,256]{1,0:T(8,128)(2,1)S(1)}, bf16[512,256]{1,0:T(8,128)(2,1)S(1)}, u32[]{:S(2)}, u32[]{:S(2)}) %collective-permute-start.24) | collective-permute-done | bytes 262176 | tf_op jit(solution)/shard_map/ppermute | solution.py:424
  66.9 0.6 collective-permute-start.25
  67.8 1.5 %collective-permute-start.26 = (bf16[256,256]{1,0:T(8,128)(2,1)S(1)}, bf16[256,256]{1,0:T(8,128)(2,1)S(1)}, u32[]{:S(2)}, u32[]{:S(2)}) collective-permute-start(bf16[256,256]{1,0:T(8,128)(2,1)S(1)} %shard_map.181), channel_id=1, source_target_pairs={{0,4},{1,3},{2,6},{3,1},{4,0},{5,7},{6,2},{7,5},{8,12},{9,11},{10,... | collective-permute-start | bytes 393224 | tf_op jit(solution)/shard_map/ppermute | solution.py:441
  69.3 1.5 %collective-permute-start.27 = (bf16[256,256]{1,0:T(8,128)(2,1)S(1)}, bf16[256,256]{1,0:T(8,128)(2,1)S(1)}, u32[]{:S(2)}, u32[]{:S(2)}) collective-permute-start(bf16[256,256]{1,0:T(8,128)(2,1)S(1)} %get-tuple-element.43), channel_id=1, source_target_pairs={{0,6},{1,7},{2,4},{3,5},{4,2},{5,3},{6,0},{7,1},{8,14},{9,15},{10,... | collective-permute-start | bytes 393224 | tf_op jit(solution)/shard_map/ppermute | solution.py:441
  70.8 0.8 shard_map.182
  71.6 1.8 %collective-permute-done.25.refs_1_ = bf16[256,256]{1,0:T(8,128)(2,1)S(1)} collective-permute-done((bf16[256,256]{1,0:T(8,128)(2,1)S(1)}, bf16[256,256]{1,0:T(8,128)(2,1)S(1)}, u32[]{:S(2)}, u32[]{:S(2)}) %collective-permute-start.25) | collective-permute-done | bytes 131104 | tf_op jit(solution)/shard_map/ppermute | solution.py:441
  73.4 2.8 %collective-permute-done.27.refs_3_ = bf16[256,256]{1,0:T(8,128)(2,1)S(1)} collective-permute-done((bf16[256,256]{1,0:T(8,128)(2,1)S(1)}, bf16[256,256]{1,0:T(8,128)(2,1)S(1)}, u32[]{:S(2)}, u32[]{:S(2)}) %collective-permute-start.27) | collective-permute-done | bytes 131104 | tf_op jit(solution)/shard_map/ppermute | solution.py:441
  76.2 1.5 %shard_map.183.sum_ref = bf16[256,256]{1,0:T(8,128)(2,1)S(1)} custom-call(f32[256,256]{1,0:T(8,128)S(1)} %get-tuple-element.41.refs_0_, bf16[256,256]{1,0:T(8,128)(2,1)S(1)} %collective-permute-done.25.refs_1_, bf16[256,256]{1,0:T(8,128)(2,1)S(1)} %collective-permute-done.26.refs_2_, bf16[256,256]{1,0:T(8,128)(2,1)S(1)} %collective-permute-done.27.refs_3_, ...), custom_call_target="tpu_custom_call" | custom-call | flops 1073741824 | bytes 1048576 | tf_op jit(solution)/shard_map/pallas_call | solution.py:51
  78.4 1.2 %collective-permute-done.28.other_ref = bf16[1024,128]{1,0:T(8,128)(2,1)S(1)} collective-permute-done((bf16[1024,128]{1,0:T(8,128)(2,1)S(1)}, bf16[1024,128]{1,0:T(8,128)(2,1)S(1)}, u32[]{:S(2)}, u32[]{:S(2)}) %collective-permute-start.28) | collective-permute-done | bytes 262176 | tf_op jit(solution)/shard_map/ppermute | solution.py:424
  79.6 1.3 %collective-permute-start.29 = (bf16[256,128]{1,0:T(8,128)(2,1)S(1)}, bf16[256,128]{1,0:T(8,128)(2,1)S(1)}, u32[]{:S(2)}, u32[]{:S(2)}) collective-permute-start(bf16[256,128]{1,0:T(8,128)(2,1)S(1)} %get-tuple-element.50), channel_id=1, source_target_pairs={{0,2},{1,5},{2,0},{3,7},{4,6},{5,1},{6,4},{7,3},{8,10},{9,13},{10,... | collective-permute-start | bytes 196616 | tf_op jit(solution)/shard_map/ppermute | solution.py:441
  81.0 0.8 collective-permute-start.30
  81.8 1.4 %collective-permute-start.31 = (bf16[256,128]{1,0:T(8,128)(2,1)S(1)}, bf16[256,128]{1,0:T(8,128)(2,1)S(1)}, u32[]{:S(2)}, u32[]{:S(2)}) collective-permute-start(bf16[256,128]{1,0:T(8,128)(2,1)S(1)} %get-tuple-element.52), channel_id=1, source_target_pairs={{0,6},{1,7},{2,4},{3,5},{4,2},{5,3},{6,0},{7,1},{8,14},{9,15},{10,... | collective-permute-start | bytes 196616 | tf_op jit(solution)/shard_map/ppermute | solution.py:441
  83.2 1.4 %collective-permute-done.29.refs_1_ = bf16[256,128]{1,0:T(8,128)(2,1)S(1)} collective-permute-done((bf16[256,128]{1,0:T(8,128)(2,1)S(1)}, bf16[256,128]{1,0:T(8,128)(2,1)S(1)}, u32[]{:S(2)}, u32[]{:S(2)}) %collective-permute-start.29) | collective-permute-done | bytes 65568 | tf_op jit(solution)/shard_map/ppermute | solution.py:441
  84.6 1.3 %collective-permute-done.30.refs_2_ = bf16[256,128]{1,0:T(8,128)(2,1)S(1)} collective-permute-done((bf16[256,128]{1,0:T(8,128)(2,1)S(1)}, bf16[256,128]{1,0:T(8,128)(2,1)S(1)}, u32[]{:S(2)}, u32[]{:S(2)}) %collective-permute-start.30) | collective-permute-done | bytes 65568 | tf_op jit(solution)/shard_map/ppermute | solution.py:441
  85.9 1.0 %collective-permute-done.31.refs_3_ = bf16[256,128]{1,0:T(8,128)(2,1)S(1)} collective-permute-done((bf16[256,128]{1,0:T(8,128)(2,1)S(1)}, bf16[256,128]{1,0:T(8,128)(2,1)S(1)}, u32[]{:S(2)}, u32[]{:S(2)}) %collective-permute-start.31) | collective-permute-done | bytes 65568 | tf_op jit(solution)/shard_map/ppermute | solution.py:441
  87.0 0.8 shard_map.187
  (78 shorter events, 5.7 us)
Async XLA Ops:
  1.8 9.0 %collective-permute-start.5 = (bf16[400,128]{1,0:T(8,128)(2,1)S(1)}, bf16[400,128]{1,0:T(8,128)(2,1)S(1)}, u32[]{:S(2)}, u32[]{:S(2)}) collective-permute-start(bf16[400,128]{1,0:T(8,128)(2,1)S(1)} %get-tuple-element.29.pack_ref.refs_0_), channel_id=1, source_target_pairs={{0,24},{2,26},{4,28},{6,30},{8,16},{10,18},{12,20},{14,22},{16,8},... | collective-permute-start | bytes 307208 | tf_op jit(solution)/shard_map/ppermute | solution.py:430
  7.0 8.6 %collective-permute-start.4 = (bf16[400,128]{1,0:T(8,128)(2,1)S(1)}, bf16[400,128]{1,0:T(8,128)(2,1)S(1)}, u32[]{:S(2)}, u32[]{:S(2)}) collective-permute-start(bf16[400,128]{1,0:T(8,128)(2,1)S(1)} %get-tuple-element.29.pack_ref.refs_0_), channel_id=1, source_target_pairs={{0,16},{2,18},{4,20},{6,22},{8,24},{10,26},{12,28},{14,30},{16,0},... | collective-permute-start | bytes 307208 | tf_op jit(solution)/shard_map/ppermute | solution.py:430
  7.0 8.6 %collective-permute-start.3 = (bf16[400,128]{1,0:T(8,128)(2,1)S(1)}, bf16[400,128]{1,0:T(8,128)(2,1)S(1)}, u32[]{:S(2)}, u32[]{:S(2)}) collective-permute-start(bf16[400,128]{1,0:T(8,128)(2,1)S(1)} %get-tuple-element.29.pack_ref.refs_0_), channel_id=1, source_target_pairs={{0,8},{2,10},{4,12},{6,14},{8,0},{10,2},{12,4},{14,6},{16,24},{18,... | collective-permute-start | bytes 307208 | tf_op jit(solution)/shard_map/ppermute | solution.py:430
  15.7 3.0 %collective-permute-start.6 = (bf16[1024,128]{1,0:T(8,128)(2,1)S(1)}, bf16[1024,128]{1,0:T(8,128)(2,1)S(1)}, u32[]{:S(2)}, u32[]{:S(2)}) collective-permute-start(bf16[1024,128]{1,0:T(8,128)(2,1)S(1)} %pad_maximum_fusion), channel_id=1, source_target_pairs={{0,1},{1,0},{2,3},{3,2},{4,5},{5,4},{6,7},{7,6},{8,9},{9,8},{10,11... | collective-permute-start | bytes 786440 | tf_op jit(solution)/shard_map/ppermute | solution.py:424
  15.7 26.4 %collective-permute-start.10 = (bf16[256,1024]{1,0:T(8,128)(2,1)}, bf16[256,1024]{1,0:T(8,128)(2,1)S(1)}, u32[]{:S(2)}, u32[]{:S(2)}) collective-permute-start(bf16[256,1024]{1,0:T(8,128)(2,1)} %refs_8_.3), channel_id=1, source_target_pairs={{0,1},{1,0},{2,3},{3,2},{4,5},{5,4},{6,7},{7,6},{8,9},{9,8},{10,11... | collective-permute-start | bytes 1572872 | tf_op jit(solution)/shard_map/ppermute | solution.py:424
  16.2 28.1 %collective-permute-start.11 = (bf16[256,1024]{1,0:T(8,128)(2,1)}, bf16[256,1024]{1,0:T(8,128)(2,1)S(1)}, u32[]{:S(2)}, u32[]{:S(2)}) collective-permute-start(bf16[256,1024]{1,0:T(8,128)(2,1)} %refs_10_.1), channel_id=1, source_target_pairs={{0,1},{1,0},{2,3},{3,2},{4,5},{5,4},{6,7},{7,6},{8,9},{9,8},{10,11... | collective-permute-start | bytes 1572872 | tf_op jit(solution)/shard_map/ppermute | solution.py:424
  16.3 28.0 %collective-permute-start.12 = (bf16[1024,256]{1,0:T(8,128)(2,1)}, bf16[1024,256]{1,0:T(8,128)(2,1)S(1)}, u32[]{:S(2)}, u32[]{:S(2)}) collective-permute-start(bf16[1024,256]{1,0:T(8,128)(2,1)} %refs_12_.1), channel_id=1, source_target_pairs={{0,1},{1,0},{2,3},{3,2},{4,5},{5,4},{6,7},{7,6},{8,9},{9,8},{10,11... | collective-permute-start | bytes 1572872 | tf_op jit(solution)/shard_map/ppermute | solution.py:424
  18.6 21.2 %copy-start.2 = (bf16[1024,256]{1,0:T(8,128)(2,1)S(1)}, bf16[1024,256]{1,0:T(8,128)(2,1)}, u32[]{:S(2)}) copy-start(bf16[1024,256]{1,0:T(8,128)(2,1)} %down_a.1) | copy-start | bytes 1572868
  18.6 23.5 %copy-start.9 = (bf16[256,1024]{1,0:T(8,128)(2,1)S(1)}, bf16[256,1024]{1,0:T(8,128)(2,1)}, u32[]{:S(2)}) copy-start(bf16[256,1024]{1,0:T(8,128)(2,1)} %refs_6_.2) | copy-start | bytes 1572868
  18.6 23.5 %copy-start.10 = (bf16[256,1024]{1,0:T(8,128)(2,1)S(1)}, bf16[256,1024]{1,0:T(8,128)(2,1)}, u32[]{:S(2)}) copy-start(bf16[256,1024]{1,0:T(8,128)(2,1)} %refs_8_.2) | copy-start | bytes 1572868
  19.7 24.6 %copy-start.3 = (bf16[256,1024]{1,0:T(8,128)(2,1)S(1)}, bf16[256,1024]{1,0:T(8,128)(2,1)}, u32[]{:S(2)}) copy-start(bf16[256,1024]{1,0:T(8,128)(2,1)} %refs_8_.3) | copy-start | bytes 1572868
  19.7 24.6 %copy-start.4 = (bf16[256,1024]{1,0:T(8,128)(2,1)S(1)}, bf16[256,1024]{1,0:T(8,128)(2,1)}, u32[]{:S(2)}) copy-start(bf16[256,1024]{1,0:T(8,128)(2,1)} %refs_10_.1) | copy-start | bytes 1572868
  19.7 24.6 %copy-start.5 = (bf16[1024,256]{1,0:T(8,128)(2,1)S(1)}, bf16[1024,256]{1,0:T(8,128)(2,1)}, u32[]{:S(2)}) copy-start(bf16[1024,256]{1,0:T(8,128)(2,1)} %refs_12_.1) | copy-start | bytes 1572868
  19.7 24.6 %copy-start.8 = (f32[256]{0:T(256)S(1)}, f32[256]{0:T(256)}, u32[]{:S(2)}) copy-start(f32[256]{0:T(256)} %param.22) | copy-start | bytes 3076
  19.7 16.5 %collective-permute-start.7 = (bf16[256,256]{1,0:T(8,128)(2,1)S(1)}, bf16[256,256]{1,0:T(8,128)(2,1)S(1)}, u32[]{:S(2)}, u32[]{:S(2)}) collective-permute-start(bf16[256,256]{1,0:T(8,128)(2,1)S(1)} %get-tuple-element.32), channel_id=1, source_target_pairs={{0,2},{1,5},{2,0},{3,7},{4,6},{5,1},{6,4},{7,3},{8,10},{9,13},{10,... | collective-permute-start | bytes 393224 | tf_op jit(solution)/shard_map/ppermute | solution.py:441
  21.3 5.2 %collective-permute-start.2 = (bf16[144,128]{1,0:T(8,128)(2,1)S(1)}, bf16[144,128]{1,0:T(8,128)(2,1)S(1)}, u32[]{:S(2)}, u32[]{:S(2)}) collective-permute-start(bf16[144,128]{1,0:T(8,128)(2,1)S(1)} %get-tuple-element.28.refs_0_), channel_id=1, source_target_pairs={{0,6},{1,7},{2,4},{3,5},{4,2},{5,3},{6,0},{7,1},{8,14},{9,15},{10,... | collective-permute-start | bytes 110600 | tf_op jit(solution)/shard_map/ppermute | solution.py:441
  26.5 4.0 %collective-permute-start.1 = (bf16[144,128]{1,0:T(8,128)(2,1)S(1)}, bf16[144,128]{1,0:T(8,128)(2,1)S(1)}, u32[]{:S(2)}, u32[]{:S(2)}) collective-permute-start(bf16[144,128]{1,0:T(8,128)(2,1)S(1)} %get-tuple-element.28.refs_0_), channel_id=1, source_target_pairs={{0,4},{1,3},{2,6},{3,1},{4,0},{5,7},{6,2},{7,5},{8,12},{9,11},{10,... | collective-permute-start | bytes 110600 | tf_op jit(solution)/shard_map/ppermute | solution.py:441
  30.5 4.3 %collective-permute-start = (bf16[144,128]{1,0:T(8,128)(2,1)S(1)}, bf16[144,128]{1,0:T(8,128)(2,1)S(1)}, u32[]{:S(2)}, u32[]{:S(2)}) collective-permute-start(bf16[144,128]{1,0:T(8,128)(2,1)S(1)} %get-tuple-element.28.refs_0_), channel_id=1, source_target_pairs={{0,2},{1,5},{2,0},{3,7},{4,6},{5,1},{6,4},{7,3},{8,10},{9,13},{10,... | collective-permute-start | bytes 110600 | tf_op jit(solution)/shard_map/ppermute | solution.py:441
  34.8 5.0 %collective-permute-start.8 = (bf16[256,256]{1,0:T(8,128)(2,1)S(1)}, bf16[256,256]{1,0:T(8,128)(2,1)S(1)}, u32[]{:S(2)}, u32[]{:S(2)}) collective-permute-start(bf16[256,256]{1,0:T(8,128)(2,1)S(1)} %get-tuple-element.33), channel_id=1, source_target_pairs={{0,4},{1,3},{2,6},{3,1},{4,0},{5,7},{6,2},{7,5},{8,12},{9,11},{10,... | collective-permute-start | bytes 393224 | tf_op jit(solution)/shard_map/ppermute | solution.py:441
  36.2 5.9 %collective-permute-start.9 = (bf16[256,256]{1,0:T(8,128)(2,1)S(1)}, bf16[256,256]{1,0:T(8,128)(2,1)S(1)}, u32[]{:S(2)}, u32[]{:S(2)}) collective-permute-start(bf16[256,256]{1,0:T(8,128)(2,1)S(1)} %get-tuple-element.34), channel_id=1, source_target_pairs={{0,6},{1,7},{2,4},{3,5},{4,2},{5,3},{6,0},{7,1},{8,14},{9,15},{10,... | collective-permute-start | bytes 393224 | tf_op jit(solution)/shard_map/ppermute | solution.py:441
  39.8 10.0 %collective-permute-start.18 = (bf16[1024,256]{1,0:T(8,128)(2,1)S(1)}, bf16[1024,256]{1,0:T(8,128)(2,1)S(1)}, u32[]{:S(2)}, u32[]{:S(2)}) collective-permute-start(bf16[1024,256]{1,0:T(8,128)(2,1)S(1)} %copy-done.2), channel_id=1, source_target_pairs={{0,1},{1,0},{2,3},{3,2},{4,5},{5,4},{6,7},{7,6},{8,9},{9,8},{10,11... | collective-permute-start | bytes 1572872 | tf_op jit(solution)/shard_map/ppermute | solution.py:424
  42.1 9.5 %collective-permute-start.19 = (bf16[256,1024]{1,0:T(8,128)(2,1)S(1)}, bf16[256,1024]{1,0:T(8,128)(2,1)S(1)}, u32[]{:S(2)}, u32[]{:S(2)}) collective-permute-start(bf16[256,1024]{1,0:T(8,128)(2,1)S(1)} %copy-done.9), channel_id=1, source_target_pairs={{0,1},{1,0},{2,3},{3,2},{4,5},{5,4},{6,7},{7,6},{8,9},{9,8},{10,11... | collective-permute-start | bytes 1572872 | tf_op jit(solution)/shard_map/ppermute | solution.py:424
  42.1 9.5 %collective-permute-start.20 = (bf16[256,1024]{1,0:T(8,128)(2,1)S(1)}, bf16[256,1024]{1,0:T(8,128)(2,1)S(1)}, u32[]{:S(2)}, u32[]{:S(2)}) collective-permute-start(bf16[256,1024]{1,0:T(8,128)(2,1)S(1)} %copy-done.10), channel_id=1, source_target_pairs={{0,1},{1,0},{2,3},{3,2},{4,5},{5,4},{6,7},{7,6},{8,9},{9,8},{10,11... | collective-permute-start | bytes 1572872 | tf_op jit(solution)/shard_map/ppermute | solution.py:424
  45.7 5.5 %copy-start = (bf16[256,128]{1,0:T(8,128)(2,1)S(1)}, bf16[256,128]{1,0:T(8,128)(2,1)}, u32[]{:S(2)}) copy-start(bf16[256,128]{1,0:T(8,128)(2,1)} %refs_4_.1) | copy-start | bytes 196612
  45.9 9.0 %copy-start.11 = (f32[256]{0:T(256)S(1)}, f32[256]{0:T(256)}, u32[]{:S(2)}) copy-start(f32[256]{0:T(256)} %param.23) | copy-start | bytes 3076
  45.9 1.6 %collective-permute-start.13 = (bf16[512,256]{1,0:T(8,128)(2,1)S(1)}, bf16[512,256]{1,0:T(8,128)(2,1)S(1)}, u32[]{:S(2)}, u32[]{:S(2)}) collective-permute-start(bf16[512,256]{1,0:T(8,128)(2,1)S(1)} %shard_map.175), channel_id=1, source_target_pairs={{0,1},{1,0},{2,3},{3,2},{4,5},{5,4},{6,7},{7,6},{8,9},{9,8},{10,11... | collective-permute-start | bytes 786440 | tf_op jit(solution)/shard_map/ppermute | solution.py:424
  46.1 2.2 %collective-permute-start.17 = (bf16[128,128]{1,0:T(8,128)(2,1)S(1)}, bf16[128,128]{1,0:T(8,128)(2,1)S(1)}, u32[]{:S(2)}, u32[]{:S(2)}) collective-permute-start(bf16[128,128]{1,0:T(8,128)(2,1)S(1)} %get-tuple-element.40), channel_id=1, source_target_pairs={{0,1},{1,0},{2,3},{3,2},{4,5},{5,4},{6,7},{7,6},{8,9},{9,8},{10,11... | collective-permute-start | bytes 98312 | tf_op jit(solution)/shard_map/ppermute | solution.py:424
  47.6 4.8 %collective-permute-start.14 = (bf16[128,256]{1,0:T(8,128)(2,1)S(1)}, bf16[128,256]{1,0:T(8,128)(2,1)S(1)}, u32[]{:S(2)}, u32[]{:S(2)}) collective-permute-start(bf16[128,256]{1,0:T(8,128)(2,1)S(1)} %get-tuple-element.37), channel_id=1, source_target_pairs={{0,2},{1,5},{2,0},{3,7},{4,6},{5,1},{6,4},{7,3},{8,10},{9,13},{10,... | collective-permute-start | bytes 196616 | tf_op jit(solution)/shard_map/ppermute | solution.py:441
  48.2 4.3 %collective-permute-start.15 = (bf16[128,256]{1,0:T(8,128)(2,1)S(1)}, bf16[128,256]{1,0:T(8,128)(2,1)S(1)}, u32[]{:S(2)}, u32[]{:S(2)}) collective-permute-start(bf16[128,256]{1,0:T(8,128)(2,1)S(1)} %get-tuple-element.38), channel_id=1, source_target_pairs={{0,4},{1,3},{2,6},{3,1},{4,0},{5,7},{6,2},{7,5},{8,12},{9,11},{10,... | collective-permute-start | bytes 196616 | tf_op jit(solution)/shard_map/ppermute | solution.py:441
  49.8 5.2 %collective-permute-start.16 = (bf16[128,256]{1,0:T(8,128)(2,1)S(1)}, bf16[128,256]{1,0:T(8,128)(2,1)S(1)}, u32[]{:S(2)}, u32[]{:S(2)}) collective-permute-start(bf16[128,256]{1,0:T(8,128)(2,1)S(1)} %get-tuple-element.39), channel_id=1, source_target_pairs={{0,6},{1,7},{2,4},{3,5},{4,2},{5,3},{6,0},{7,1},{8,14},{9,15},{10,... | collective-permute-start | bytes 196616 | tf_op jit(solution)/shard_map/ppermute | solution.py:441
  56.8 6.9 %collective-permute-start.23 = (bf16[128,256]{1,0:T(8,128)(2,1)S(1)}, bf16[128,256]{1,0:T(8,128)(2,1)S(1)}, u32[]{:S(2)}, u32[]{:S(2)}) collective-permute-start(bf16[128,256]{1,0:T(8,128)(2,1)S(1)} %shard_map.178), channel_id=1, source_target_pairs={{0,24},{2,26},{4,28},{6,30},{8,16},{10,18},{12,20},{14,22},{16,8},... | collective-permute-start | bytes 196616 | tf_op jit(solution)/shard_map/ppermute | solution.py:430
  59.3 5.6 %collective-permute-start.22 = (bf16[128,256]{1,0:T(8,128)(2,1)S(1)}, bf16[128,256]{1,0:T(8,128)(2,1)S(1)}, u32[]{:S(2)}, u32[]{:S(2)}) collective-permute-start(bf16[128,256]{1,0:T(8,128)(2,1)S(1)} %shard_map.178), channel_id=1, source_target_pairs={{0,16},{2,18},{4,20},{6,22},{8,24},{10,26},{12,28},{14,30},{16,0},... | collective-permute-start | bytes 196616 | tf_op jit(solution)/shard_map/ppermute | solution.py:430
  59.3 5.6 %collective-permute-start.21 = (bf16[128,256]{1,0:T(8,128)(2,1)S(1)}, bf16[128,256]{1,0:T(8,128)(2,1)S(1)}, u32[]{:S(2)}, u32[]{:S(2)}) collective-permute-start(bf16[128,256]{1,0:T(8,128)(2,1)S(1)} %shard_map.178), channel_id=1, source_target_pairs={{0,8},{2,10},{4,12},{6,14},{8,0},{10,2},{12,4},{14,6},{16,24},{18,... | collective-permute-start | bytes 196616 | tf_op jit(solution)/shard_map/ppermute | solution.py:430
  65.0 1.6 %collective-permute-start.24 = (bf16[512,256]{1,0:T(8,128)(2,1)S(1)}, bf16[512,256]{1,0:T(8,128)(2,1)S(1)}, u32[]{:S(2)}, u32[]{:S(2)}) collective-permute-start(bf16[512,256]{1,0:T(8,128)(2,1)S(1)} %pad_maximum_fusion.1.own_ref), channel_id=1, source_target_pairs={{0,1},{1,0},{2,3},{3,2},{4,5},{5,4},{6,7},{7,6},{8,9},{9,8},{10,11... | collective-permute-start | bytes 786440 | tf_op jit(solution)/shard_map/ppermute | solution.py:424
  66.9 6.4 %collective-permute-start.25 = (bf16[256,256]{1,0:T(8,128)(2,1)S(1)}, bf16[256,256]{1,0:T(8,128)(2,1)S(1)}, u32[]{:S(2)}, u32[]{:S(2)}) collective-permute-start(bf16[256,256]{1,0:T(8,128)(2,1)S(1)} %get-tuple-element.42), channel_id=1, source_target_pairs={{0,2},{1,5},{2,0},{3,7},{4,6},{5,1},{6,4},{7,3},{8,10},{9,13},{10,... | collective-permute-start | bytes 393224 | tf_op jit(solution)/shard_map/ppermute | solution.py:441
  67.8 5.6 %collective-permute-start.26 = (bf16[256,256]{1,0:T(8,128)(2,1)S(1)}, bf16[256,256]{1,0:T(8,128)(2,1)S(1)}, u32[]{:S(2)}, u32[]{:S(2)}) collective-permute-start(bf16[256,256]{1,0:T(8,128)(2,1)S(1)} %shard_map.181), channel_id=1, source_target_pairs={{0,4},{1,3},{2,6},{3,1},{4,0},{5,7},{6,2},{7,5},{8,12},{9,11},{10,... | collective-permute-start | bytes 393224 | tf_op jit(solution)/shard_map/ppermute | solution.py:441
  69.3 6.9 %collective-permute-start.27 = (bf16[256,256]{1,0:T(8,128)(2,1)S(1)}, bf16[256,256]{1,0:T(8,128)(2,1)S(1)}, u32[]{:S(2)}, u32[]{:S(2)}) collective-permute-start(bf16[256,256]{1,0:T(8,128)(2,1)S(1)} %get-tuple-element.43), channel_id=1, source_target_pairs={{0,6},{1,7},{2,4},{3,5},{4,2},{5,3},{6,0},{7,1},{8,14},{9,15},{10,... | collective-permute-start | bytes 393224 | tf_op jit(solution)/shard_map/ppermute | solution.py:441
  77.7 9.3 %copy-start.1 = (f32[256,128]{1,0:T(8,128)S(1)}, f32[256,128]{1,0:T(8,128)}, u32[]{:S(2)}) copy-start(f32[256,128]{1,0:T(8,128)} %refs_5_.3) | copy-start | bytes 393220
  77.7 9.3 %copy-start.6 = (f32[256,128]{1,0:T(8,128)S(1)}, f32[256,128]{1,0:T(8,128)}, u32[]{:S(2)}) copy-start(f32[256,128]{1,0:T(8,128)} %refs_6_.3) | copy-start | bytes 393220
  77.7 9.3 %copy-start.7 = (f32[256,128]{1,0:T(8,128)S(1)}, f32[256,128]{1,0:T(8,128)}, u32[]{:S(2)}) copy-start(f32[256,128]{1,0:T(8,128)} %refs_7_.3) | copy-start | bytes 393220
  78.0 1.6 %collective-permute-start.28 = (bf16[1024,128]{1,0:T(8,128)(2,1)S(1)}, bf16[1024,128]{1,0:T(8,128)(2,1)S(1)}, u32[]{:S(2)}, u32[]{:S(2)}) collective-permute-start(bf16[1024,128]{1,0:T(8,128)(2,1)S(1)} %shard_map.185), channel_id=1, source_target_pairs={{0,1},{1,0},{2,3},{3,2},{4,5},{5,4},{6,7},{7,6},{8,9},{9,8},{10,11... | collective-permute-start | bytes 786440 | tf_op jit(solution)/shard_map/ppermute | solution.py:424
  79.6 4.9 %collective-permute-start.29 = (bf16[256,128]{1,0:T(8,128)(2,1)S(1)}, bf16[256,128]{1,0:T(8,128)(2,1)S(1)}, u32[]{:S(2)}, u32[]{:S(2)}) collective-permute-start(bf16[256,128]{1,0:T(8,128)(2,1)S(1)} %get-tuple-element.50), channel_id=1, source_target_pairs={{0,2},{1,5},{2,0},{3,7},{4,6},{5,1},{6,4},{7,3},{8,10},{9,13},{10,... | collective-permute-start | bytes 196616 | tf_op jit(solution)/shard_map/ppermute | solution.py:441
  81.0 5.0 %collective-permute-start.30 = (bf16[256,128]{1,0:T(8,128)(2,1)S(1)}, bf16[256,128]{1,0:T(8,128)(2,1)S(1)}, u32[]{:S(2)}, u32[]{:S(2)}) collective-permute-start(bf16[256,128]{1,0:T(8,128)(2,1)S(1)} %get-tuple-element.51), channel_id=1, source_target_pairs={{0,4},{1,3},{2,6},{3,1},{4,0},{5,7},{6,2},{7,5},{8,12},{9,11},{10,... | collective-permute-start | bytes 196616 | tf_op jit(solution)/shard_map/ppermute | solution.py:441
  81.8 5.2 %collective-permute-start.31 = (bf16[256,128]{1,0:T(8,128)(2,1)S(1)}, bf16[256,128]{1,0:T(8,128)(2,1)S(1)}, u32[]{:S(2)}, u32[]{:S(2)}) collective-permute-start(bf16[256,128]{1,0:T(8,128)(2,1)S(1)} %get-tuple-element.52), channel_id=1, source_target_pairs={{0,6},{1,7},{2,4},{3,5},{4,2},{5,3},{6,0},{7,1},{8,14},{9,15},{10,... | collective-permute-start | bytes 196616 | tf_op jit(solution)/shard_map/ppermute | solution.py:441
